TPU v7x, 256 devices: a whole 4x4x8 slice. The times are simulated.
256 devices in a mesh: gx: 16 (over y, x), gy: 16 (over z, core).
Axes of the slice: x: 4, y: 4, z: 8, core: 2. Of those that a mesh axis runs over, the one named last changes fastest.
Arguments:
- source_heat: float32 [160, 256, 2048], P(None, 'gx', 'gy'), may hold values from -8 to 8
- horiz_coef: float32 [160], replicated, may hold values from 0.5 to 4
- face_coef: float32 [161], replicated, may hold values from 0.25 to 4
- column_inverse: float32 [160, 160], replicated, as said below
Outputs:
- pressure: float32 [160, 256, 2048], P(None, 'gx', 'gy')
- true_residual: float32 [160, 256, 2048], P(None, 'gx', 'gy')
Inputs may be any that keep to these rules, and one draw needn't show every extreme that they name: `column_inverse`: the inverse of the tridiagonal matrix with diagonal 4 horiz_coef[k] + face_coef[k] + face_coef[k+1] and off-diagonal entries -face_coef[k] between levels k-1 and k.
All inputs are finite; a program needn't handle non-finite values.
Results may differ from a plain program's by a relative error of at most 0.0003.
Values sent between devices are 32-bit elements; how exact they have to be, the bound alone decides.
No kernel may reach another device: no remote copies, remote signals or barrier semaphores. Data moves between devices by JAX's collectives and lax.ppermute only.
A program may use at most 64 MiB of HBM per device.

v0:
```python
import jax
import jax.numpy as jnp
from jax import lax
from jax.sharding import Mesh
from jax.sharding import PartitionSpec as P

ITERS = 3
GX = ("gx_0", "gx_1")
GY = ("gy_0", "gy_1")


def with_halo(shard, sides, width):
    edges = {}
    for axis, dim in sides:
        size, length = (lax.axis_size(axis), shard.shape[dim])
        up = [(i, (i + 1) % size) for i in range(size)]
        last = lax.slice_in_dim(shard, length - width, length, axis=dim)
        leading = lax.slice_in_dim(shard, 0, width, axis=dim)
        edges[dim] = (
            lax.ppermute(last, axis, up),
            lax.ppermute(leading, axis, [(b, a) for a, b in up]),
        )
    done = []
    for _, dim in sides:
        low, high = edges[dim]
        around = [(width, width) if d in done else (0, 0) for d in range(shard.ndim)]
        shard = jnp.concatenate([jnp.pad(low, around), shard, jnp.pad(high, around)], axis=dim)
        done.append(dim)
    return shard


def copy_for_each(shard, axis):
    copies = jnp.broadcast_to(shard, (lax.axis_size(axis), *shard.shape))
    return lax.all_to_all(copies, axis, split_axis=0, concat_axis=0, tiled=True)


def taken_together(shard, axis):
    everything = copy_for_each(shard, axis)
    return jnp.sum(everything, axis=0)


def by_axis(shard, axes):
    far, near = axes
    nearer = taken_together(shard, near)
    return taken_together(nearer, far)


def together(arrays, axis):
    flat, at, outs = (jnp.concatenate([a.reshape(-1) for a in arrays]), 0, [])
    total = by_axis(flat, axis)
    for a in arrays:
        outs.append(total[at : at + a.size].reshape(a.shape))
        at += a.size
    return tuple(outs)


def operate(values_in, horizontal, face_coef):
    padded = with_halo(values_in, ((GX, 1), (GY, 2)), 1)
    beside = padded[:, 2:, 1:-1] + padded[:, :-2, 1:-1] + padded[:, 1:-1, 2:] + padded[:, 1:-1, :-2]
    zero_layer = jnp.zeros_like(values_in[:1])
    upward = jnp.concatenate([values_in[1:], zero_layer], 0)
    downward = jnp.concatenate([zero_layer, values_in[:-1]], 0)
    lower_face = face_coef[:-1][:, None, None]
    upper_face = face_coef[1:][:, None, None]
    return (
        horizontal[:, None, None] * (4.0 * values_in - beside)
        + upper_face * (values_in - upward)
        + lower_face * (values_in - downward)
    )


def precondition(values_in, column_inverse):
    layout = values_in.shape
    columns = values_in.reshape(layout[0], -1)
    return jnp.dot(column_inverse, columns, precision=lax.Precision.HIGHEST).reshape(layout)


def paired(residual, precond, image):
    return together(
        (jnp.sum(residual * precond), jnp.sum(precond * image)), ("gx_0", ("gx_1", "gy_0", "gy_1"))
    )


def on_device(source_heat, horiz_coef, face_coef, column_inverse):
    pressure = jnp.zeros_like(source_heat)
    residual = source_heat
    precond = precondition(residual, column_inverse)
    image = operate(precond, horiz_coef, face_coef)
    inner, product = paired(residual, precond, image)
    step_len = inner / product
    direction, along = (precond, image)
    for iteration in range(ITERS):
        pressure = pressure + step_len * direction
        residual = residual - step_len * along
        if iteration + 1 < ITERS:
            precond = precondition(residual, column_inverse)
            image = operate(precond, horiz_coef, face_coef)
            inner_next, product = paired(residual, precond, image)
            ratio = inner_next / inner
            step_len = inner_next / (product - ratio * inner_next / step_len)
            direction = precond + ratio * direction
            along = image + ratio * along
            inner = inner_next
    true_residual = source_heat - operate(pressure, horiz_coef, face_coef)
    return (pressure, true_residual)


def solution(mesh):
    split = Mesh(mesh.devices.reshape(4, 4, 8, 2), ("gx_0", "gx_1", "gy_0", "gy_1"))
    return jax.shard_map(
        on_device,
        mesh=split,
        in_specs=(P(None, GX, GY), P(), P(), P()),
        out_specs=(P(None, GX, GY), P(None, GX, GY)),
        check_vma=False,
    )
```

profile of v0, /device:TPU:1, one launch (start us, length us, event | category | flops | bytes accessed | tf_op | source)
XLA Modules:
  0.0 211.3 jit_solution(1802082521977575198)
XLA Ops:
  0.6 0.9 copy-done
  1.6 2.9 %fusion = f32[160,2048]{1,0:T(8,128)S(1)} fusion(f32[160,160]{1,0:T(8,128)S(1)} %copy-done, f32[20,8,16,128]{3,2,1,0:T(8,128)} %bitcast.116), kind=kOutput, calls=%fused_computation | convolution fusion | flops 629145600 | bytes 2723840 | tf_op jit(solution)/shard_map/dot_general | solution.py:75
  4.6 5.8 %collective-permute-start = (f32[160,1,128]{2,0,1:T(8,128)S(1)}, f32[160,1,128]{2,0,1:T(8,128)S(1)}, u32[]{:S(2)}, u32[]{:S(2)}) collective-permute-start(f32[160,1,128]{2,0,1:T(8,128)S(1)} %get-tuple-element.37), channel_id=1, source_target_pairs={{16,0},{32,16},{48,32},{64,48},{80,64},{96,80},{112,96},{128,112},... | collective-permute-start | bytes 245768 | tf_op jit(solution)/shard_map/ppermute | solution.py:21
  10.7 1.9 fusion.54
  12.6 1.9 copy.261
  14.6 2.5 %collective-permute-start.3 = (f32[160,16,1]{0,1,2:T(8,128)S(1)}, f32[160,16,1]{0,1,2:T(8,128)S(1)}, u32[]{:S(2)}, u32[]{:S(2)}) collective-permute-start(f32[160,16,1]{0,1,2:T(8,128)S(1)} %copy.261), channel_id=1, source_target_pairs={{0,1},{1,2},{2,3},{3,4},{4,5},{5,6},{6,7},{7,8},{8,9},{9,10},{10,1... | collective-permute-start | bytes 30728 | tf_op jit(solution)/shard_map/ppermute | solution.py:20
  17.1 1.9 copy.260
  19.8 0.6 copy-done.5
  20.4 0.9 multiply_reduce_fusion.4
  22.4 1.5 copy.197
  23.9 1.6 copy.272
  25.4 1.6 copy.273
  27.2 1.1 copy-done.11
  28.7 4.4 %multiply_reduce_fusion.3 = (f32[]{:T(128)}, f32[160,16,128]{2,0,1:T(8,128)}) fusion(f32[160,16,128]{2,0,1:T(8,128)S(1)} %copy-done.11, f32[159,16,128]{2,0,1:T(8,128)S(1)} %copy.199, f32[160]{0:T(256)S(1)} %get-tuple-element.42, f32[159,16,128]{2,0,1:T(8,128)S(1)} %copy-done.16, f32[160]{0:T(256)S(1)} %get-tuple-element.41, ...), kind=kLoop, calls=%fused_computation.79 | loop fusion | flops 7864319 | bytes 8198020 | tf_op jit(solution)/shard_map/reduce_sum | solution.py:80
  33.1 1.3 pad_maximum_fusion.18
  34.4 19.7 %all_to_all.36 = f32[64,1,2]{2,1,0:T(1,128)S(1)} all-to-all(f32[64,1,2]{2,1,0:T(1,128)S(1)} %broadcast_in_dim.12), channel_id=1, replica_groups=mesh['gx_0'=4,'gx_1'=4,'gy_0'=8,'gy_1'=2] {'gx_1','gy_0','gy_1'}, dimensions={0} | all-to-all | bytes 1024 | tf_op jit(solution)/shard_map/all_to_all | solution.py:34
  54.2 9.2 %all_to_all.37 = f32[4,1,2]{2,1,0:T(1,128)S(1)} all-to-all(f32[4,1,2]{2,1,0:T(1,128)S(1)} %broadcast_in_dim.13), channel_id=1, replica_groups=mesh['gx_0'=4,'gx_1'=4,'gy_0'=8,'gy_1'=2] {'gx_0'}, dimensions={0} | all-to-all | bytes 64 | tf_op jit(solution)/shard_map/all_to_all | solution.py:34
  63.4 0.6 fusion.60
  65.2 3.4 %fusion.6 = f32[2048,160]{0,1:T(8,128)S(1)} fusion(f32[160,160]{1,0:T(8,128)S(1)} %copy-done, f32[160,16,128]{2,0,1:T(8,128)} %get-tuple-element.14, f32[]{:T(128)S(6)} %div.21, f32[160,16,128]{2,1,0:T(8,128)} %param.4), kind=kOutput, calls=%fused_computation.6 | convolution fusion | flops 629800960 | bytes 4034564 | tf_op jit(solution)/shard_map/dot_general | solution.py:75
  68.7 1.7 collective-permute-start.4
  70.7 1.9 fusion.51
  72.6 1.9 copy.264
  74.6 2.0 copy.265
  76.5 2.9 %collective-permute-start.7 = (f32[160,16,1]{0,1,2:T(8,128)S(1)}, f32[160,16,1]{0,1,2:T(8,128)S(1)}, u32[]{:S(2)}, u32[]{:S(2)}) collective-permute-start(f32[160,16,1]{0,1,2:T(8,128)S(1)} %copy.265), channel_id=1, source_target_pairs={{0,1},{1,2},{2,3},{3,4},{4,5},{5,6},{6,7},{7,8},{8,9},{9,10},{10,1... | collective-permute-start | bytes 30728 | tf_op jit(solution)/shard_map/ppermute | solution.py:20
  80.4 1.5 copy.220
  81.8 1.5 copy.218
  83.3 1.6 copy.274
  84.9 1.5 copy.275
  86.7 1.1 copy-done.6
  88.2 6.1 %multiply_reduce_fusion.2 = (f32[]{:T(128)}, f32[]{:T(128)}, f32[160,16,128]{2,0,1:T(8,128)}) fusion(f32[160,16,128]{2,0,1:T(8,128)S(1)} %copy-done.8, f32[]{:T(128)S(6)} %div.21, f32[160,16,128]{2,1,0:T(8,128)S(1)} %copy-done.6, f32[160,16,128]{2,0,1:T(8,128)} %copy-done.12, f32[159,16,128]{2,0,1:T(8,128)} %copy.220, f32[160]{0:T(256)S(1)} %get-tuple-element.42, ...), kind=kLoop, calls=%fused_computation.77 | loop fusion | flops 9175038 | bytes 10819468 | tf_op jit(solution)/shard_map/reduce_sum | solution.py:80
  94.3 1.4 pad_maximum_fusion.19
  95.7 17.1 %all_to_all.38 = f32[64,1,2]{2,1,0:T(1,128)S(1)} all-to-all(f32[64,1,2]{2,1,0:T(1,128)S(1)} %broadcast_in_dim.14), channel_id=1, replica_groups=mesh['gx_0'=4,'gx_1'=4,'gy_0'=8,'gy_1'=2] {'gx_1','gy_0','gy_1'}, dimensions={0} | all-to-all | bytes 1024 | tf_op jit(solution)/shard_map/all_to_all | solution.py:34
  112.9 7.3 %all_to_all.39 = f32[4,1,2]{2,1,0:T(1,128)S(1)} all-to-all(f32[4,1,2]{2,1,0:T(1,128)S(1)} %broadcast_in_dim.15), channel_id=1, replica_groups=mesh['gx_0'=4,'gx_1'=4,'gy_0'=8,'gy_1'=2] {'gx_0'}, dimensions={0} | all-to-all | bytes 64 | tf_op jit(solution)/shard_map/all_to_all | solution.py:34
  120.2 0.6 fusion.59
  125.3 2.7 %multiply_subtract_fusion = f32[160,16,128]{2,0,1:T(8,128)S(1)} fusion(f32[160,16,128]{2,0,1:T(8,128)} %get-tuple-element.12, f32[160,16,128]{2,0,1:T(8,128)} %get-tuple-element.14, f32[]{:T(128)S(6)} %div.22, f32[]{:T(128)S(6)} %div.24, f32[]{:T(128)S(6)} %div.21, f32[160,16,128]{2,1,0:T(8,128)} %param.4), kind=kLoop, calls=%fused_computation.75 | loop fusion | flops 1966080 | bytes 5242892 | tf_op jit(solution)/shard_map/sub | solution.py:94
  128.0 1.3 fusion.3
  129.5 1.5 collective-permute-start.8
  131.3 1.9 fusion.49
  133.2 1.9 copy.268
  135.2 2.0 copy.269
  137.1 2.9 %collective-permute-start.11 = (f32[160,16,1]{0,1,2:T(8,128)S(1)}, f32[160,16,1]{0,1,2:T(8,128)S(1)}, u32[]{:S(2)}, u32[]{:S(2)}) collective-permute-start(f32[160,16,1]{0,1,2:T(8,128)S(1)} %copy.269), channel_id=1, source_target_pairs={{0,1},{1,2},{2,3},{3,4},{4,5},{5,6},{6,7},{7,8},{8,9},{9,10},{10,1... | collective-permute-start | bytes 30728 | tf_op jit(solution)/shard_map/ppermute | solution.py:20
  140.0 1.9 fusion.48
  142.6 1.5 copy.241
  144.1 1.5 copy.239
  145.6 1.6 copy.276
  147.1 1.6 copy.277
  148.7 2.8 %multiply_reduce_fusion = (f32[]{:T(128)}, f32[160,18,128]{2,0,1:T(8,128)S(1)}) fusion(f32[160,16,128]{2,0,1:T(8,128)} %copy-done.9, f32[160,18,128]{2,0,1:T(8,128)S(1)} %constant_dynamic-update-slice_fusion.8, f32[2048,160]{0,1:T(8,128)} %copy-done.4), kind=kLoop, calls=%fused_computation.74 | loop fusion | flops 655359 | bytes 3932164 | tf_op jit(solution)/shard_map/reduce_sum | solution.py:80
  151.6 3.6 %fusion.25 = f32[]{:T(128)} fusion(f32[160,16,128]{2,0,1:T(8,128)S(1)} %copy-done.14, f32[160,18,128]{2,0,1:T(8,128)S(1)} %constant_dynamic-update-slice_fusion.6, f32[160,16,1]{2,0,1:T(8,128)} %copy.277, f32[160,16,1]{2,0,1:T(8,128)} %copy.276, f32[160,1,128]{2,0,1:T(8,128)S(1)} %collective-permute-done.9, f32[160,1,128]{2,0,1:T(8,128)S(1)} %collective-permute-done.8, ...), kind=kLoop, calls=%fused_computation.37 | loop fusion | flops 7864319 | bytes 5576580 | tf_op jit(solution)/shard_map/reduce_sum | solution.py:80
  155.3 1.3 pad_maximum_fusion.20
  156.6 17.1 %all_to_all.40 = f32[64,1,2]{2,1,0:T(1,128)S(1)} all-to-all(f32[64,1,2]{2,1,0:T(1,128)S(1)} %broadcast_in_dim.16), channel_id=1, replica_groups=mesh['gx_0'=4,'gx_1'=4,'gy_0'=8,'gy_1'=2] {'gx_1','gy_0','gy_1'}, dimensions={0} | all-to-all | bytes 1024 | tf_op jit(solution)/shard_map/all_to_all | solution.py:34
  173.7 7.3 %all_to_all.41 = f32[4,1,2]{2,1,0:T(1,128)S(1)} all-to-all(f32[4,1,2]{2,1,0:T(1,128)S(1)} %broadcast_in_dim.17), channel_id=1, replica_groups=mesh['gx_0'=4,'gx_1'=4,'gy_0'=8,'gy_1'=2] {'gx_0'}, dimensions={0} | all-to-all | bytes 64 | tf_op jit(solution)/shard_map/all_to_all | solution.py:34
  181.1 0.6 fusion.58
  185.7 1.7 multiply_add_fusion
  187.4 1.5 fusion.46
  189.3 4.4 %collective-permute-start.12 = (f32[160,1,128]{2,0,1:T(8,128)S(1)}, f32[160,1,128]{2,0,1:T(8,128)S(1)}, u32[]{:S(2)}, u32[]{:S(2)}) collective-permute-start(f32[160,1,128]{2,0,1:T(8,128)S(1)} %get-tuple-element.20), channel_id=1, source_target_pairs={{16,0},{32,16},{48,32},{64,48},{80,64},{96,80},{112,96},{128,112},... | collective-permute-start | bytes 245768 | tf_op jit(solution)/shard_map/ppermute | solution.py:21
  193.7 2.0 copy.247
  195.7 0.6 copy.249
  196.3 2.9 %collective-permute-start.15 = (f32[160,16,1]{0,1,2:T(8,128)S(1)}, f32[160,16,1]{0,1,2:T(8,128)S(1)}, u32[]{:S(2)}, u32[]{:S(2)}) collective-permute-start(f32[160,16,1]{0,1,2:T(8,128)S(1)} %copy.249), channel_id=1, source_target_pairs={{0,1},{1,2},{2,3},{3,4},{4,5},{5,6},{6,7},{7,8},{8,9},{9,10},{10,1... | collective-permute-start | bytes 30728 | tf_op jit(solution)/shard_map/ppermute | solution.py:20
  199.3 1.7 fusion.45
  200.9 1.8 copy.252
  202.8 1.6 copy.248
  204.3 1.5 copy.250
  205.9 3.5 %fusion.15 = f32[160,16,128]{2,0,1:T(8,128)S(1)} fusion(f32[160,16,1]{2,0,1:T(8,128)} %copy.250, f32[160,1,128]{2,0,1:T(8,128)S(1)} %collective-permute-done.12, f32[160,16,128]{2,0,1:T(8,128)S(1)} %copy-done.3, f32[160,1,128]{2,0,1:T(8,128)S(1)} %collective-permute-done.13, f32[160,16,1]{2,0,1:T(8,128)} %copy.248, f32[159,16,128]{2,0,1:T(8,128)} %get-tuple-element.16, ...), kind=kLoop, calls=%fused_computation.19 | loop fusion | flops 8847360 | bytes 6723456 | tf_op jit(solution)/shard_map/sub | solution.py:104
  209.5 1.8 copy.253
  (106 shorter events, 6.7 us)
Async XLA Ops:
  0.6 0.9 copy-start
  4.6 6.1 %copy-start.10 = (f32[160,16,128]{2,0,1:T(8,128)}, f32[160,16,128]{2,0,1:T(8,128)S(1)}, u32[]{:S(2)}) copy-start(f32[160,16,128]{2,0,1:T(8,128)S(1)} %copy_bitcast_fusion.2) | copy-start | bytes 3932164
  4.6 22.6 %collective-permute-start = (f32[160,1,128]{2,0,1:T(8,128)S(1)}, f32[160,1,128]{2,0,1:T(8,128)S(1)}, u32[]{:S(2)}, u32[]{:S(2)}) collective-permute-start(f32[160,1,128]{2,0,1:T(8,128)S(1)} %get-tuple-element.37), channel_id=1, source_target_pairs={{16,0},{32,16},{48,32},{64,48},{80,64},{96,80},{112,96},{128,112},... | collective-permute-start | bytes 245768 | tf_op jit(solution)/shard_map/ppermute | solution.py:21
  10.4 16.6 %collective-permute-start.1 = (f32[160,1,128]{2,0,1:T(8,128)S(1)}, f32[160,1,128]{2,0,1:T(8,128)S(1)}, u32[]{:S(2)}, u32[]{:S(2)}) collective-permute-start(f32[160,1,128]{2,0,1:T(8,128)S(1)} %get-tuple-element.38), channel_id=1, source_target_pairs={{0,16},{16,32},{32,48},{48,64},{64,80},{80,96},{96,112},{112,128},... | collective-permute-start | bytes 245768 | tf_op jit(solution)/shard_map/ppermute | solution.py:20
  14.6 10.8 %collective-permute-start.3 = (f32[160,16,1]{0,1,2:T(8,128)S(1)}, f32[160,16,1]{0,1,2:T(8,128)S(1)}, u32[]{:S(2)}, u32[]{:S(2)}) collective-permute-start(f32[160,16,1]{0,1,2:T(8,128)S(1)} %copy.261), channel_id=1, source_target_pairs={{0,1},{1,2},{2,3},{3,4},{4,5},{5,6},{6,7},{7,8},{8,9},{9,10},{10,1... | collective-permute-start | bytes 30728 | tf_op jit(solution)/shard_map/ppermute | solution.py:20
  19.0 0.7 copy-start.19
  19.0 1.3 copy-start.5
  19.0 4.8 %collective-permute-start.2 = (f32[160,16,1]{0,1,2:T(8,128)S(1)}, f32[160,16,1]{0,1,2:T(8,128)S(1)}, u32[]{:S(2)}, u32[]{:S(2)}) collective-permute-start(f32[160,16,1]{0,1,2:T(8,128)S(1)} %copy.260), channel_id=1, source_target_pairs={{1,0},{2,1},{3,2},{4,3},{5,4},{6,5},{7,6},{8,7},{9,8},{10,9},{11,1... | collective-permute-start | bytes 30728 | tf_op jit(solution)/shard_map/ppermute | solution.py:21
  27.0 1.3 copy-start.11
  27.0 1.7 copy-start.16
  27.0 1.7 copy-start.18
  68.7 2.0 copy-start.12
  68.7 17.9 %collective-permute-start.4 = (f32[160,1,128]{2,0,1:T(8,128)S(1)}, f32[160,1,128]{2,0,1:T(8,128)S(1)}, u32[]{:S(2)}, u32[]{:S(2)}) collective-permute-start(f32[160,1,128]{2,0,1:T(8,128)S(1)} %get-tuple-element.31), channel_id=1, source_target_pairs={{16,0},{32,16},{48,32},{64,48},{80,64},{96,80},{112,96},{128,112},... | collective-permute-start | bytes 245768 | tf_op jit(solution)/shard_map/ppermute | solution.py:21
  70.4 16.1 %collective-permute-start.5 = (f32[160,1,128]{2,0,1:T(8,128)S(1)}, f32[160,1,128]{2,0,1:T(8,128)S(1)}, u32[]{:S(2)}, u32[]{:S(2)}) collective-permute-start(f32[160,1,128]{2,0,1:T(8,128)S(1)} %get-tuple-element.32), channel_id=1, source_target_pairs={{0,16},{16,32},{32,48},{48,64},{64,80},{80,96},{96,112},{112,128},... | collective-permute-start | bytes 245768 | tf_op jit(solution)/shard_map/ppermute | solution.py:20
  76.5 8.4 %collective-permute-start.7 = (f32[160,16,1]{0,1,2:T(8,128)S(1)}, f32[160,16,1]{0,1,2:T(8,128)S(1)}, u32[]{:S(2)}, u32[]{:S(2)}) collective-permute-start(f32[160,16,1]{0,1,2:T(8,128)S(1)} %copy.265), channel_id=1, source_target_pairs={{0,1},{1,2},{2,3},{3,4},{4,5},{5,6},{6,7},{7,8},{8,9},{9,10},{10,1... | collective-permute-start | bytes 30728 | tf_op jit(solution)/shard_map/ppermute | solution.py:20
  79.4 3.9 %collective-permute-start.6 = (f32[160,16,1]{0,1,2:T(8,128)S(1)}, f32[160,16,1]{0,1,2:T(8,128)S(1)}, u32[]{:S(2)}, u32[]{:S(2)}) collective-permute-start(f32[160,16,1]{0,1,2:T(8,128)S(1)} %copy.264), channel_id=1, source_target_pairs={{1,0},{2,1},{3,2},{4,3},{5,4},{6,5},{7,6},{8,7},{9,8},{10,9},{11,1... | collective-permute-start | bytes 30728 | tf_op jit(solution)/shard_map/ppermute | solution.py:21
  86.5 1.3 copy-start.6
  86.5 1.7 copy-start.8
  128.0 1.3 copy-start.9
  129.3 1.7 copy-start.4
  129.5 1.8 copy-start.13
  129.5 22.0 %collective-permute-start.8 = (f32[160,1,128]{2,0,1:T(8,128)S(1)}, f32[160,1,128]{2,0,1:T(8,128)S(1)}, u32[]{:S(2)}, u32[]{:S(2)}) collective-permute-start(f32[160,1,128]{2,0,1:T(8,128)S(1)} %get-tuple-element.27), channel_id=1, source_target_pairs={{16,0},{32,16},{48,32},{64,48},{80,64},{96,80},{112,96},{128,112},... | collective-permute-start | bytes 245768 | tf_op jit(solution)/shard_map/ppermute | solution.py:21
  131.0 17.7 %collective-permute-start.9 = (f32[160,1,128]{2,0,1:T(8,128)S(1)}, f32[160,1,128]{2,0,1:T(8,128)S(1)}, u32[]{:S(2)}, u32[]{:S(2)}) collective-permute-start(f32[160,1,128]{2,0,1:T(8,128)S(1)} %get-tuple-element.28), channel_id=1, source_target_pairs={{0,16},{16,32},{32,48},{48,64},{64,80},{80,96},{96,112},{112,128},... | collective-permute-start | bytes 245768 | tf_op jit(solution)/shard_map/ppermute | solution.py:20
  137.1 10.0 %collective-permute-start.11 = (f32[160,16,1]{0,1,2:T(8,128)S(1)}, f32[160,16,1]{0,1,2:T(8,128)S(1)}, u32[]{:S(2)}, u32[]{:S(2)}) collective-permute-start(f32[160,16,1]{0,1,2:T(8,128)S(1)} %copy.269), channel_id=1, source_target_pairs={{0,1},{1,2},{2,3},{3,4},{4,5},{5,6},{6,7},{7,8},{8,9},{9,10},{10,1... | collective-permute-start | bytes 30728 | tf_op jit(solution)/shard_map/ppermute | solution.py:20
  140.0 5.6 %collective-permute-start.10 = (f32[160,16,1]{0,1,2:T(8,128)S(1)}, f32[160,16,1]{0,1,2:T(8,128)S(1)}, u32[]{:S(2)}, u32[]{:S(2)}) collective-permute-start(f32[160,16,1]{0,1,2:T(8,128)S(1)} %copy.268), channel_id=1, source_target_pairs={{1,0},{2,1},{3,2},{4,3},{5,4},{6,5},{7,6},{8,7},{9,8},{10,9},{11,1... | collective-permute-start | bytes 30728 | tf_op jit(solution)/shard_map/ppermute | solution.py:21
  148.7 2.9 %copy-start.14 = (f32[160,16,128]{2,0,1:T(8,128)S(1)}, f32[160,16,128]{2,0,1:T(8,128)}, u32[]{:S(2)}) copy-start(f32[160,16,128]{2,0,1:T(8,128)} %copy-done.13) | copy-start | bytes 3932164
  148.7 2.9 %copy-start.15 = (f32[159,16,128]{2,0,1:T(8,128)S(1)}, f32[159,16,128]{2,0,1:T(8,128)}, u32[]{:S(2)}) copy-start(f32[159,16,128]{2,0,1:T(8,128)} %copy.241) | copy-start | bytes 3907588
  148.7 2.9 %copy-start.17 = (f32[159,16,128]{2,0,1:T(8,128)S(1)}, f32[159,16,128]{2,0,1:T(8,128)}, u32[]{:S(2)}) copy-start(f32[159,16,128]{2,0,1:T(8,128)} %copy.239) | copy-start | bytes 3907588
  187.4 1.5 copy-start.2
  188.9 17.0 %collective-permute-start.13 = (f32[160,1,128]{2,0,1:T(8,128)S(1)}, f32[160,1,128]{2,0,1:T(8,128)S(1)}, u32[]{:S(2)}, u32[]{:S(2)}) collective-permute-start(f32[160,1,128]{2,0,1:T(8,128)S(1)} %get-tuple-element.19), channel_id=1, source_target_pairs={{0,16},{16,32},{32,48},{48,64},{64,80},{80,96},{96,112},{112,128},... | collective-permute-start | bytes 245768 | tf_op jit(solution)/shard_map/ppermute | solution.py:20
  189.3 16.6 %collective-permute-start.12 = (f32[160,1,128]{2,0,1:T(8,128)S(1)}, f32[160,1,128]{2,0,1:T(8,128)S(1)}, u32[]{:S(2)}, u32[]{:S(2)}) collective-permute-start(f32[160,1,128]{2,0,1:T(8,128)S(1)} %get-tuple-element.20), channel_id=1, source_target_pairs={{16,0},{32,16},{48,32},{64,48},{80,64},{96,80},{112,96},{128,112},... | collective-permute-start | bytes 245768 | tf_op jit(solution)/shard_map/ppermute | solution.py:21
  193.7 5.6 %copy-start.3 = (f32[160,16,128]{2,0,1:T(8,128)S(1)}, f32[160,16,128]{2,0,1:T(8,128)}, u32[]{:S(2)}) copy-start(f32[160,16,128]{2,0,1:T(8,128)} %copy-done.2) | copy-start | bytes 3932164
  196.3 8.0 %collective-permute-start.15 = (f32[160,16,1]{0,1,2:T(8,128)S(1)}, f32[160,16,1]{0,1,2:T(8,128)S(1)}, u32[]{:S(2)}, u32[]{:S(2)}) collective-permute-start(f32[160,16,1]{0,1,2:T(8,128)S(1)} %copy.249), channel_id=1, source_target_pairs={{0,1},{1,2},{2,3},{3,4},{4,5},{5,6},{6,7},{7,8},{8,9},{9,10},{10,1... | collective-permute-start | bytes 30728 | tf_op jit(solution)/shard_map/ppermute | solution.py:20
  199.3 3.5 %collective-permute-start.14 = (f32[160,16,1]{0,1,2:T(8,128)S(1)}, f32[160,16,1]{0,1,2:T(8,128)S(1)}, u32[]{:S(2)}, u32[]{:S(2)}) collective-permute-start(f32[160,16,1]{0,1,2:T(8,128)S(1)} %copy.247), channel_id=1, source_target_pairs={{1,0},{2,1},{3,2},{4,3},{5,4},{6,5},{7,6},{8,7},{9,8},{10,9},{11,1... | collective-permute-start | bytes 30728 | tf_op jit(solution)/shard_map/ppermute | solution.py:21
  202.8 3.1 %copy-start.7 = (f32[160,16,128]{2,1,0:T(8,128)S(1)}, f32[160,16,128]{2,1,0:T(8,128)}, u32[]{:S(2)}) copy-start(f32[160,16,128]{2,1,0:T(8,128)} %param.4) | copy-start | bytes 3932164
  205.9 5.4 %copy-start.1 = (f32[160,160]{1,0:T(8,128)S(1)}, f32[160,160]{1,0:T(8,128)}, u32[]{:S(2)}) copy-start(f32[160,160]{1,0:T(8,128)} %param.7) | copy-start | bytes 307204
where the time goes:
time: 212 us; the launch traced here: 211 us
  blocking collectives  77.6 us (37%)
  local copies, waits for them, and re-layouts  59.9 us (28%)
  other arithmetic  30 us (14%)
  starting transfers between devices  25.1 us (12%)
  between operations  10.9 us (5%)
  matrix products  7.6 us (4%)
    all_to_all x6, blocking collectives, copy_for_each(): return lax.all_to_all(copies, axis, split_axis=0, concat_axis=0, tiled=True)  77.6 us
    unnamed x68, local copies, waits for them, and re-layouts  32.2 us
    ppermute x8, starting transfers between devices, with_halo(): lax.ppermute(leading, axis, [(b, a) for a, b in up])  13.4 us
    ppermute x8, starting transfers between devices, with_halo(): lax.ppermute(last, axis, up)  11.7 us
    reduce_sum x3, other arithmetic, paired(): jnp.sum(residual * precond)  9.86 us
    slice x8, local copies, waits for them, and re-layouts, with_halo(): leading = lax.slice_in_dim(shard, 0, width, axis=dim)  9.31 us
    slice x10, local copies, waits for them, and re-layouts, operate(): upward = jnp.concatenate([values_in[1:], zero_layer], 0)  8.8 us
    reduce_sum x2, other arithmetic, paired(): jnp.sum(precond * image)  7.99 us
  transfers between devices with their start and end apart: 16, of which 0 were waited for; matrix products, arithmetic and copies ran while one was open for 25% of the time, Pallas kernels for 0%

commit v1 on v0

v1 whole, which is shorter than its diff:
```python
import jax
import jax.numpy as jnp
from jax import lax
from jax.experimental import pallas as pl
from jax.experimental.pallas import tpu as pltpu
from jax.sharding import Mesh
from jax.sharding import PartitionSpec as P

F32 = jnp.float32
LANES = 128
EDGE = 6
STEPS = 3


def vmem(rows, cols=LANES):
    return pltpu.VMEM((rows, cols), F32)


def spec():
    return pl.BlockSpec(memory_space=pltpu.VMEM)


def params(mib):
    return pltpu.CompilerParams(vmem_limit_bytes=mib * 1024 * 1024)


def cost(flops, size):
    return pl.CostEstimate(flops=flops, bytes_accessed=size, transcendentals=0)


def lane_ids(rows):
    return lax.broadcasted_iota(jnp.int32, (rows, LANES), 1)


def product(matrix, columns):
    return jnp.dot(matrix, columns, precision=lax.Precision.HIGHEST, preferred_element_type=F32)


def apply_inverse(matrix, src, dst, nz, tiles, width):
    def some(first, count):
        parts = [src[pl.ds(pl.multiple_of((first + t) * nz, 8), nz), :] for t in range(count)]
        out = product(matrix, jnp.concatenate(parts, axis=1) if count > 1 else parts[0])
        for t in range(count):
            dst[pl.ds(pl.multiple_of((first + t) * nz, 8), nz), :] = out[:, t * LANES : (t + 1) * LANES]

    whole = tiles // width

    def body(i, carry):
        some(i * width, width)
        return carry

    lax.fori_loop(0, whole, body, 0)
    if tiles % width:
        some(whole * width, tiles % width)


def load_kernel(nz, nx, b_hbm, nat, low, high, sem):
    copy = pltpu.make_async_copy(b_hbm, nat, sem)
    copy.start()
    copy.wait()
    for i in range(STEPS):
        low[i * nz : (i + 1) * nz, :] = nat[pl.ds(i, nz, stride=nx), :]
        high[i * nz : (i + 1) * nz, :] = nat[pl.ds(nx - STEPS + i, nz, stride=nx), :]


def own_kernel(nz, nx, nat, h_row, inv, b_t, u0, h_wide, edge):
    eye = lax.broadcasted_iota(jnp.int32, (nz, nz), 0) == lax.broadcasted_iota(jnp.int32, (nz, nz), 1)
    column = jnp.sum(jnp.where(eye, jnp.broadcast_to(h_row[...], (nz, nz)), 0.0), axis=1, keepdims=True)
    h_wide[...] = jnp.broadcast_to(column, (nz, LANES))
    lane = lane_ids(nz)
    packed = jnp.zeros((nz, LANES), F32)
    for x in range(nx):
        row = nat[pl.ds(x, nz, stride=nx), :]
        b_t[x * nz : (x + 1) * nz, :] = row
        at = EDGE * (x + 2)
        packed = jnp.where((lane >= at) & (lane < at + EDGE), pltpu.roll(row, at + 3, 1), packed)
    edge[...] = packed
    apply_inverse(inv[...], b_t, u0, nz, nx, 4)


def pack_kernel(nz, nx, edge, below, above, packed):
    lane = lane_ids(nz)
    out = edge[...]
    for x, ref, i in ((-2, below, 1), (-1, below, 2), (nx, above, 0), (nx + 1, above, 1)):
        at = EDGE * (x + 2)
        row = ref[i * nz : (i + 1) * nz, :]
        out = jnp.where((lane >= at) & (lane < at + EDGE), pltpu.roll(row, (at + 3) % LANES, 1), out)
    packed[...] = out


def outer_kernel(nz, nx, u0, below, above, inv, u0e):
    u0e[STEPS * nz : (STEPS + nx) * nz, :] = u0[...]
    for ref, first in ((below, 0), (above, STEPS + nx)):
        out = product(inv[...], jnp.concatenate([ref[i * nz : (i + 1) * nz, :] for i in range(STEPS)], axis=1))
        for i in range(STEPS):
            u0e[(first + i) * nz : (first + i + 1) * nz, :] = out[:, i * LANES : (i + 1) * LANES]


def stencil_row(v, top, here, nz, x, side, lane):
    row = lambda r: v[pl.ds(pl.multiple_of(r * nz, 8), nz), :]
    mid = row(here)
    turned = pltpu.roll(side, lax.rem(2 * LANES - (EDGE * (x + 2) + 3), LANES), 1)
    left = jnp.where(lane == 0, turned, pltpu.roll(mid, 1, 1))
    right = jnp.where(lane == LANES - 1, turned, pltpu.roll(mid, LANES - 1, 1))
    return row(here - 1) + row(here + 1) + left + right, mid


def pack_row(packed, mid, x, lane):
    at = EDGE * (x + 2)
    turned = pltpu.roll(mid, lax.rem(at + 3, LANES), 1)
    return jnp.where((lane == at + 2) | (lane == at + 3), turned, packed)


def stencil(v, base, g, side_ref, h_ref, nz, first, count, pack_first, pack_count, side_out):
    lane = lane_ids(nz)

    def body(i, packed):
        x = first + i
        around, mid = stencil_row(v, None, x - base, nz, x, side_ref[...], lane)
        g[pl.ds(pl.multiple_of(i * nz, 8), nz), :] = h_ref[...] * around
        return pack_row(packed, mid, x, lane)

    packed = lax.fori_loop(0, count, body, jnp.zeros((nz, LANES), F32))
    if side_out is not None:
        side = side_ref[...]
        pos = lax.rem(lane, EDGE)
        after = jnp.where(pos == 2, packed, pltpu.roll(side, LANES - 1, 1))
        before = jnp.where(pos == 3, packed, pltpu.roll(side, 1, 1))
        rows = pltpu.roll(side, EDGE, 1) + pltpu.roll(side, LANES - EDGE, 1)
        side_out[...] = h_ref[...] * (after + before + rows)


def fold(v):
    out = v[0:8]
    for i in range(1, v.shape[0] // 8):
        out = out + v[8 * i : 8 * i + 8]
    return out


def krylov_kernel(nz, nx, members, b_t, u0e, from_left, from_right, inv, h_wide, u1e, u2e, g1e, g2e, g3, send, side):
    lane = lane_ids(nz)
    pos = lax.rem(lane, EDGE)
    near = jnp.where(pos < 3, from_left[...], from_right[...])
    turned = jnp.zeros_like(near)
    for p in range(EDGE):
        turned = jnp.where(pos == p, pltpu.roll(near, (LANES - (5 - 2 * p)) % LANES, 1), turned)
    side[...] = product(inv[...], turned)
    n1 = nx + 4
    stencil(u0e, -3, g1e, side, h_wide, nz, -2, n1, -1, nx + 2, g1e.at[pl.ds(n1 * nz, nz), :])
    apply_inverse(inv[...], g1e, u1e, nz, n1 + 1, 4)
    n2 = nx + 2
    side[...] = u1e[n1 * nz : (n1 + 1) * nz, :]
    stencil(u1e, -2, g2e, side, h_wide, nz, -1, n2, 0, nx, g2e.at[pl.ds(n2 * nz, nz), :])
    apply_inverse(inv[...], g2e, u2e, nz, n2 + 1, 4)
    side[...] = u2e[n2 * nz : (n2 + 1) * nz, :]

    def body(x, sums):
        at = lambda ref, r: ref[pl.ds(pl.multiple_of(r * nz, 8), nz), :]
        around, w2 = stencil_row(u2e, None, x + 1, nz, x, side[...], lane)
        next_g = h_wide[...] * around
        g3[pl.ds(pl.multiple_of(x * nz, 8), nz), :] = next_g
        b, f1, f2 = at(b_t, x), at(g1e, x + 2), at(g2e, x + 1)
        v0, v1 = at(u0e, x + 3), at(u1e, x + 2)
        a0, a1, a2 = b - f1, f1 - f2, f2 - next_g
        terms = (v0 * a0, v1 * a0, v1 * a1, w2 * a0, w2 * a1, w2 * a2, v0 * b, v1 * b, w2 * b)
        return tuple(s + fold(t) for s, t in zip(sums, terms))

    zero = jnp.zeros((8, LANES), F32)
    sums = lax.fori_loop(0, nx, body, (zero,) * 9)
    line = lax.broadcasted_iota(jnp.int32, (8, LANES), 1)
    out = zero
    for i, s in enumerate(sums):
        total = jnp.sum(jnp.sum(s, axis=0, keepdims=True), axis=1, keepdims=True)
        out = jnp.where(line == i, jnp.broadcast_to(total, (8, LANES)), out)
    for i in range(members // 8):
        send[8 * i : 8 * i + 8, :] = out


def solve_small(t):
    g00, g10, g11, g20, g21, g22, m0, m1, m2 = t
    l1, l2 = g10 / g00, g20 / g00
    d1 = g11 - l1 * g10
    e = g21 - l2 * g10
    l3 = e / d1
    d2 = g22 - l2 * g20 - l3 * e
    y1 = m1 - l1 * m0
    y2 = m2 - l2 * m0 - l3 * y1
    c2 = y2 / d2
    c1 = y1 / d1 - l3 * c2
    return m0 / g00 - l1 * c1 - l2 * c2, c1, c2


def combine_kernel(nz, nx, kz, got, b_t, u0e, u1e, u2e, g1e, g2e, g3, pressure, true_residual, coef):
    step = pl.program_id(0)

    @pl.when(step == 0)
    def _():
        total = jnp.sum(fold(got[...]), axis=0, keepdims=True)
        line = lax.broadcasted_iota(jnp.int32, (1, LANES), 1)
        pick = lambda i: jnp.sum(jnp.where(line == i, total, 0.0), axis=1, keepdims=True)
        for i, c in enumerate(solve_small([pick(i) for i in range(9)])):
            coef[i * 8 : i * 8 + 8, :] = jnp.broadcast_to(c, (8, LANES))

    c0, c1, c2 = (jnp.concatenate([coef[i * 8 : i * 8 + 8, :]] * (kz // 8), axis=0) for i in range(3))

    def body(x, carry):
        at = lambda ref, r: ref[pl.ds(pl.multiple_of(r * nz + step * kz, 8), kz), :]
        v0, v1, v2 = at(u0e, x + 3), at(u1e, x + 2), at(u2e, x + 1)
        b, f1, f2, f3 = at(b_t, x), at(g1e, x + 2), at(g2e, x + 1), at(g3, x)
        pressure[pl.ds(x, kz, stride=nx), :] = c0 * v0 + c1 * v1 + c2 * v2
        true_residual[pl.ds(x, kz, stride=nx), :] = b - (c0 * (b - f1) + c1 * (f1 - f2) + c2 * (f2 - f3))
        return carry

    lax.fori_loop(0, nx, body, 0)


def neighbours(array, axes, up):
    size = lax.axis_size(axes)
    pairs = [(i, (i + 1) % size) for i in range(size)]
    return lax.ppermute(array, axes, pairs if up else [(b, a) for a, b in pairs])


def on_device(source_heat, horiz_coef, face_coef, column_inverse):
    nz, nx, ny = source_heat.shape
    gx, gy = "gx", "gy"
    members = lax.axis_size(gx) * lax.axis_size(gy)
    part = lambda f, *a: (lambda *refs: f(*a, *refs))
    nat, low, high = pl.pallas_call(
        part(load_kernel, nz, nx),
        in_specs=[pl.BlockSpec(memory_space=pltpu.HBM)],
        out_specs=[spec()] * 3,
        out_shape=[vmem(nz * nx), vmem(STEPS * nz), vmem(STEPS * nz)],
        scratch_shapes=[pltpu.SemaphoreType.DMA],
        compiler_params=params(4),
    )(source_heat.reshape(nz * nx, ny))
    below = neighbours(high, gx, True)
    above = neighbours(low, gx, False)
    b_t, u0, h_wide, edge = pl.pallas_call(
        part(own_kernel, nz, nx),
        in_specs=[spec()] * 3,
        out_specs=[spec()] * 4,
        out_shape=[vmem(nz * nx), vmem(nz * nx), vmem(nz), vmem(nz)],
        compiler_params=params(8),
        cost_estimate=cost(12 * nz * nz * nx * ny, 1 << 20),
    )(nat, horiz_coef.reshape(1, nz), column_inverse)
    packed = pl.pallas_call(
        part(pack_kernel, nz, nx),
        in_specs=[spec()] * 3,
        out_specs=spec(),
        out_shape=vmem(nz),
        compiler_params=params(4),
    )(edge, below, above)
    from_left = neighbours(packed, gy, True)
    from_right = neighbours(packed, gy, False)
    u0e = pl.pallas_call(
        part(outer_kernel, nz, nx),
        in_specs=[spec()] * 4,
        out_specs=spec(),
        out_shape=vmem((nx + 6) * nz),
        compiler_params=params(8),
        cost_estimate=cost(12 * nz * nz * 6 * ny, 1 << 20),
    )(u0, below, above, column_inverse)
    u1e, u2e, g1e, g2e, g3, send = pl.pallas_call(
        part(krylov_kernel, nz, nx, members),
        in_specs=[spec()] * 6,
        out_specs=[spec()] * 6,
        out_shape=[
            vmem((nx + 5) * nz),
            vmem((nx + 3) * nz),
            vmem((nx + 5) * nz),
            vmem((nx + 3) * nz),
            vmem(nx * nz),
            vmem(members),
        ],
        scratch_shapes=[pltpu.VMEM((nz, LANES), F32)],
        compiler_params=params(8),
        cost_estimate=cost(36 * nz * nz * nx * ny, 1 << 20),
    )(b_t, u0e, from_left, from_right, column_inverse, h_wide)
    got = lax.all_to_all(send.reshape(members, 1, LANES), (gx, gy), split_axis=0, concat_axis=0, tiled=True)
    kz = 32
    pressure, true_residual = pl.pallas_call(
        part(combine_kernel, nz, nx, kz),
        grid=(nz // kz,),
        in_specs=[spec()] * 8,
        out_specs=[pl.BlockSpec((kz * nx, ny), lambda i: (i, 0))] * 2,
        out_shape=[jax.ShapeDtypeStruct((nz * nx, ny), F32)] * 2,
        scratch_shapes=[pltpu.VMEM((24, LANES), F32)],
        compiler_params=params(8),
    )(got.reshape(members, LANES), b_t, u0e, u1e, u2e, g1e, g2e, g3)
    return pressure.reshape(nz, nx, ny), true_residual.reshape(nz, nx, ny)


def solution(mesh):
    field = P(None, "gx", "gy")
    return jax.shard_map(
        on_device,
        mesh=mesh,
        in_specs=(field, P(), P(), P()),
        out_specs=(field, field),
        check_vma=False,
    )
```

time: 212 us -> 63.8 us (0.30)
  local copies, waits for them, and re-layouts: 59.9 us -> 1.32 us
  blocking collectives: 77.6 us -> 26.1 us
  other arithmetic: 30 us -> 0 us
  Pallas kernels: 0 us -> 20.7 us
  starting transfers between devices: 25.1 us -> 10.8 us
  between operations: 10.9 us -> 0.69 us
  matrix products: 7.6 us -> 0 us
  waiting for transfers between devices: 0.04 us -> 4.06 us
    all_to_all x6 -> x1, blocking collectives: 77.6 us -> 26.1 us  [on_device(): lax.all_to_all(send.reshape(members, 1, LANES), (gx, gy), split_axis=0, c...]
    unnamed x68 -> x6, local copies, waits for them, and re-layouts: 32.2 us -> 1.32 us
    slice x30 -> x0, local copies, waits for them, and re-layouts: 24.2 us -> none  [the longest x8 9.31 us: with_halo(): leading = lax.slice_in_dim(shard, 0, width, axis=dim)]
    pallas_call x0 -> x6, Pallas kernels: none -> 20.7 us  [the longest x1 13.6 us: on_device(): pl.pallas_call(part(krylov_kernel, nz, nx, members), in_specs=[spec()] *...]
    reduce_sum x11 -> x0, other arithmetic: 18.2 us -> none  [the longest x3 9.86 us: paired(): jnp.sum(residual * precond)]
    ppermute x16 -> x4, starting transfers between devices: 25.1 us -> 10.8 us  [neighbours(): lax.ppermute(array, axes, pairs if up else [(b, a) for a, b in pairs])]
    dot_general x3 -> x0, matrix products: 7.6 us -> none  [precondition(): jnp.dot(column_inverse, columns, precision=lax.Precision.HIGHEST)]
    sub x2 -> x0, other arithmetic: 6.2 us -> none  [the longest x1 3.54 us: on_device(): true_residual = source_heat - operate(pressure, horiz_coef, face_coef)]
  transfers between devices with their start and end apart: 16 -> 4, of which waited for: 0 -> 3; matrix products, arithmetic and copies ran while one was open for 25% -> 0% of each run, Pallas kernels for 0% -> 5%
where the time goes in v1:
time: 63.8 us; the launch traced here: 63.7 us
  blocking collectives  26.1 us (41%)
  Pallas kernels  20.7 us (32%)
  starting transfers between devices  10.8 us (17%)
  waiting for transfers between devices  4.06 us (6%)
  local copies, waits for them, and re-layouts  1.32 us (2%)
  between operations  0.69 us (1%)
    all_to_all x1, blocking collectives, on_device(): lax.all_to_all(send.reshape(members, 1, LANES), (gx, gy), split_axis=0, c...  26.1 us
    pallas_call x1, Pallas kernels, on_device(): pl.pallas_call(part(krylov_kernel, nz, nx, members), in_specs=[spec()] *...  13.6 us
    ppermute x4, starting transfers between devices, neighbours(): lax.ppermute(array, axes, pairs if up else [(b, a) for a, b in pairs])  10.8 us
    ppermute x4, waiting for transfers between devices, neighbours(): lax.ppermute(array, axes, pairs if up else [(b, a) for a, b in pairs])  4.06 us
    pallas_call x1, Pallas kernels, on_device(): pl.pallas_call(part(combine_kernel, nz, nx, kz), grid=(nz // kz,), in_spe...  3.48 us
    pallas_call x1, Pallas kernels, on_device(): pl.pallas_call(part(own_kernel, nz, nx), in_specs=[spec()] * 3, out_specs...  2.36 us
    unnamed x6, local copies, waits for them, and re-layouts  1.32 us
  transfers between devices with their start and end apart: 4, of which 3 were waited for; matrix products, arithmetic and copies ran while one was open for 0% of the time, Pallas kernels for 5%

profile of v1, /device:TPU:1, one launch (start us, length us, event | category | flops | bytes accessed | tf_op | source)
XLA Modules:
  0.0 63.7 jit_solution(17707689625632068685)
XLA Ops:
  0.6 0.0 copy-start.2
  0.6 0.0 copy-start
  0.6 1.3 %copy-done = f32[160,16,128]{2,1,0:T(8,128)S(1)} copy-done((f32[160,16,128]{2,1,0:T(8,128)S(1)}, f32[160,16,128]{2,1,0:T(8,128)}, u32[]{:S(2)}) %copy-start) | copy-done | bytes 1310744
  2.0 0.0 copy-start.1
  2.0 0.3 shard_map.50
  2.3 2.1 %collective-permute-start = (f32[480,128]{1,0:T(8,128)S(1)}, f32[480,128]{1,0:T(8,128)S(1)}, u32[]{:S(2)}, u32[]{:S(2)}) collective-permute-start(f32[480,128]{1,0:T(8,128)S(1)} %get-tuple-element.20), channel_id=1, source_target_pairs={{0,16},{16,32},{32,48},{48,64},{64,80},{80,96},{96,112},{112,128},... | collective-permute-start | bytes 737288 | tf_op jit(solution)/shard_map/ppermute | solution.py:220
  4.4 3.8 %collective-permute-start.1 = (f32[480,128]{1,0:T(8,128)S(1)}, f32[480,128]{1,0:T(8,128)S(1)}, u32[]{:S(2)}, u32[]{:S(2)}) collective-permute-start(f32[480,128]{1,0:T(8,128)S(1)} %get-tuple-element.21), channel_id=1, source_target_pairs={{16,0},{32,16},{48,32},{64,48},{80,64},{96,80},{112,96},{128,112},... | collective-permute-start | bytes 737288 | tf_op jit(solution)/shard_map/ppermute | solution.py:220
  8.2 0.0 copy-done.2
  8.2 0.0 copy-done.1
  8.2 2.4 %shard_map.51 = (f32[2560,128]{1,0:T(8,128)S(1)}, f32[2560,128]{1,0:T(8,128)S(1)}, f32[160,128]{1,0:T(8,128)S(1)}, f32[160,128]{1,0:T(8,128)S(1)}) custom-call(f32[2560,128]{1,0:T(8,128)S(1)} %get-tuple-element.17.refs_0_, f32[1,160]{1,0:T(1,128)S(1)} %bitcast.11, f32[160,160]{1,0:T(8,128)S(1)} %copy-done.1), custom_call_target="tpu_custom_call" | custom-call | flops 629145600 | bytes 1048576 | tf_op jit(solution)/shard_map/pallas_call | solution.py:238
  10.5 1.1 %collective-permute-done.refs_1_ = f32[480,128]{1,0:T(8,128)S(1)} collective-permute-done((f32[480,128]{1,0:T(8,128)S(1)}, f32[480,128]{1,0:T(8,128)S(1)}, u32[]{:S(2)}, u32[]{:S(2)}) %collective-permute-start) | collective-permute-done | bytes 245792 | tf_op jit(solution)/shard_map/ppermute | solution.py:220
  11.7 0.0 collective-permute-done.1.refs_2_
  11.7 0.1 shard_map.53
  11.8 3.4 %collective-permute-start.3 = (f32[160,128]{1,0:T(8,128)S(1)}, f32[160,128]{1,0:T(8,128)S(1)}, u32[]{:S(2)}, u32[]{:S(2)}) collective-permute-start(f32[160,128]{1,0:T(8,128)S(1)} %shard_map.53), channel_id=1, source_target_pairs={{1,0},{2,1},{3,2},{4,3},{5,4},{6,5},{7,6},{8,7},{9,8},{10,9},{11,1... | collective-permute-start | bytes 245768 | tf_op jit(solution)/shard_map/ppermute | solution.py:220
  15.2 1.5 %collective-permute-start.2 = (f32[160,128]{1,0:T(8,128)S(1)}, f32[160,128]{1,0:T(8,128)S(1)}, u32[]{:S(2)}, u32[]{:S(2)}) collective-permute-start(f32[160,128]{1,0:T(8,128)S(1)} %shard_map.53), channel_id=1, source_target_pairs={{0,1},{1,2},{2,3},{3,4},{4,5},{5,6},{6,7},{7,8},{8,9},{9,10},{10,1... | collective-permute-start | bytes 245768 | tf_op jit(solution)/shard_map/ppermute | solution.py:220
  16.7 0.9 %shard_map.52.refs_1_.refs_2_ = f32[3520,128]{1,0:T(8,128)S(1)} custom-call(f32[2560,128]{1,0:T(8,128)S(1)} %get-tuple-element.19.refs_0_, f32[480,128]{1,0:T(8,128)S(1)} %collective-permute-done.refs_1_, f32[480,128]{1,0:T(8,128)S(1)} %collective-permute-done.1.refs_2_, f32[160,160]{1,0:T(8,128)S(1)} %copy-done.1), custom_call_target="tpu_custom_call" | custom-call | flops 235929600 | bytes 1048576 | tf_op jit(solution)/shard_map/pallas_call | solution.py:255
  17.6 1.2 %collective-permute-done.3.refs_3_ = f32[160,128]{1,0:T(8,128)S(1)} collective-permute-done((f32[160,128]{1,0:T(8,128)S(1)}, f32[160,128]{1,0:T(8,128)S(1)}, u32[]{:S(2)}, u32[]{:S(2)}) %collective-permute-start.3) | collective-permute-done | bytes 81952 | tf_op jit(solution)/shard_map/ppermute | solution.py:220
  18.8 1.7 %collective-permute-done.2.refs_2_ = f32[160,128]{1,0:T(8,128)S(1)} collective-permute-done((f32[160,128]{1,0:T(8,128)S(1)}, f32[160,128]{1,0:T(8,128)S(1)}, u32[]{:S(2)}, u32[]{:S(2)}) %collective-permute-start.2) | collective-permute-done | bytes 81952 | tf_op jit(solution)/shard_map/ppermute | solution.py:220
  20.5 13.6 %shard_map.54 = (f32[3360,128]{1,0:T(8,128)S(1)}, f32[3040,128]{1,0:T(8,128)S(1)}, f32[3360,128]{1,0:T(8,128)S(1)}, f32[3040,128]{1,0:T(8,128)S(1)}, f32[2560,128]{1,0:T(8,128)S(1)}, /*index=5*/f32[256,128]{1,0:T(8,128)S(1)}) custom-call(f32[2560,128]{1,0:T(8,128)S(1)} %get-tuple-element.18.refs_0_.refs_1_, f32[3520,128]{1,0:T(8,128)S(1)} %shard_map.52.refs_1_.refs_2_, ...), custom_call_target="tpu_custom_call" | custom-call | flops 1887436800 | bytes 1048576 | tf_op jit(solution)/shard_map/pallas_call | solution.py:263
  34.1 26.1 %all_to_all.5 = f32[256,1,128]{2,1,0:T(1,128)S(1)} all-to-all(f32[256,1,128]{2,1,0:T(1,128)S(1)} %bitcast.10), channel_id=1, replica_groups=mesh['gx'=16,'gy'=16] {'gx','gy'}, dimensions={0} | all-to-all | bytes 262144 | tf_op jit(solution)/shard_map/all_to_all | solution.py:279
  60.2 3.5 %shard_map.55 = (f32[2560,128]{1,0:T(8,128)}, f32[2560,128]{1,0:T(8,128)}) custom-call(f32[256,128]{1,0:T(8,128)S(1)} %bitcast.9, f32[2560,128]{1,0:T(8,128)S(1)} %get-tuple-element.18.refs_0_.refs_1_, f32[3520,128]{1,0:T(8,128)S(1)} %shard_map.52.refs_1_.refs_2_, f32[3360,128]{1,0:T(8,128)S(1)} %get-tuple-element.25.refs_3_, ...), custom_call_target="tpu_custom_call" | custom-call | tf_op jit(solution)/shard_map/pallas_call | solution.py:281
Async XLA Ops:
  0.6 7.5 %copy-start.2 = (f32[160]{0:T(256)S(1)}, f32[160]{0:T(256)}, u32[]{:S(2)}) copy-start(f32[160]{0:T(256)} %param.5) | copy-start | bytes 1924
  0.6 1.3 %copy-start = (f32[160,16,128]{2,1,0:T(8,128)S(1)}, f32[160,16,128]{2,1,0:T(8,128)}, u32[]{:S(2)}) copy-start(f32[160,16,128]{2,1,0:T(8,128)} %param.4) | copy-start | bytes 3932164
  2.0 6.2 %copy-start.1 = (f32[160,160]{1,0:T(8,128)S(1)}, f32[160,160]{1,0:T(8,128)}, u32[]{:S(2)}) copy-start(f32[160,160]{1,0:T(8,128)} %refs_4_.1) | copy-start | bytes 307204
  2.3 9.4 %collective-permute-start = (f32[480,128]{1,0:T(8,128)S(1)}, f32[480,128]{1,0:T(8,128)S(1)}, u32[]{:S(2)}, u32[]{:S(2)}) collective-permute-start(f32[480,128]{1,0:T(8,128)S(1)} %get-tuple-element.20), channel_id=1, source_target_pairs={{0,16},{16,32},{32,48},{48,64},{64,80},{80,96},{96,112},{112,128},... | collective-permute-start | bytes 737288 | tf_op jit(solution)/shard_map/ppermute | solution.py:220
  4.4 7.3 %collective-permute-start.1 = (f32[480,128]{1,0:T(8,128)S(1)}, f32[480,128]{1,0:T(8,128)S(1)}, u32[]{:S(2)}, u32[]{:S(2)}) collective-permute-start(f32[480,128]{1,0:T(8,128)S(1)} %get-tuple-element.21), channel_id=1, source_target_pairs={{16,0},{32,16},{48,32},{64,48},{80,64},{96,80},{112,96},{128,112},... | collective-permute-start | bytes 737288 | tf_op jit(solution)/shard_map/ppermute | solution.py:220
  11.8 7.0 %collective-permute-start.3 = (f32[160,128]{1,0:T(8,128)S(1)}, f32[160,128]{1,0:T(8,128)S(1)}, u32[]{:S(2)}, u32[]{:S(2)}) collective-permute-start(f32[160,128]{1,0:T(8,128)S(1)} %shard_map.53), channel_id=1, source_target_pairs={{1,0},{2,1},{3,2},{4,3},{5,4},{6,5},{7,6},{8,7},{9,8},{10,9},{11,1... | collective-permute-start | bytes 245768 | tf_op jit(solution)/shard_map/ppermute | solution.py:220
  15.2 5.3 %collective-permute-start.2 = (f32[160,128]{1,0:T(8,128)S(1)}, f32[160,128]{1,0:T(8,128)S(1)}, u32[]{:S(2)}, u32[]{:S(2)}) collective-permute-start(f32[160,128]{1,0:T(8,128)S(1)} %shard_map.53), channel_id=1, source_target_pairs={{0,1},{1,2},{2,3},{3,4},{4,5},{5,6},{6,7},{7,8},{8,9},{9,10},{10,1... | collective-permute-start | bytes 245768 | tf_op jit(solution)/shard_map/ppermute | solution.py:220

commit v2 on v1

v2 whole, which is shorter than its diff:
```python
import jax
import jax.numpy as jnp
from jax import lax
from jax.experimental import pallas as pl
from jax.experimental.pallas import tpu as pltpu
from jax.sharding import Mesh
from jax.sharding import PartitionSpec as P

F32 = jnp.float32
LANES = 128
GROUP = 9
STEPS = 3


def vmem(rows, cols=LANES):
    return pltpu.VMEM((rows, cols), F32)


def spec():
    return pl.BlockSpec(memory_space=pltpu.VMEM)


def params(mib):
    return pltpu.CompilerParams(vmem_limit_bytes=mib * 1024 * 1024)


def cost(flops, size):
    return pl.CostEstimate(flops=flops, bytes_accessed=size, transcendentals=0)


def lane_ids(rows):
    return lax.broadcasted_iota(jnp.int32, (rows, LANES), 1)


def product(matrix, columns):
    return jnp.dot(matrix, columns, precision=lax.Precision.HIGHEST, preferred_element_type=F32)


def apply_inverse(matrix, src, dst, nz, tiles, width):
    def some(first, count):
        parts = [src[pl.ds(pl.multiple_of((first + t) * nz, 8), nz), :] for t in range(count)]
        out = product(matrix, jnp.concatenate(parts, axis=1) if count > 1 else parts[0])
        for t in range(count):
            dst[pl.ds(pl.multiple_of((first + t) * nz, 8), nz), :] = out[:, t * LANES : (t + 1) * LANES]

    whole = tiles // width

    def body(i, carry):
        some(i * width, width)
        return carry

    lax.fori_loop(0, whole, body, 0)
    if tiles % width:
        some(whole * width, tiles % width)


def load_kernel(nz, nx, nat, low, high):
    for i in range(STEPS):
        low[i * nz : (i + 1) * nz, :] = nat[pl.ds(i, nz, stride=nx), :]
        high[i * nz : (i + 1) * nz, :] = nat[pl.ds(nx - STEPS + i, nz, stride=nx), :]


def strip_places(nx):
    half = nx // 2
    count = half + 2 * STEPS
    return [(t, t * half - STEPS + r, r) for t in range(2) for r in range(count)]


def add_edges(row, group, lane, inner, outer):
    first = GROUP * group
    turned = pltpu.roll(row, (first + STEPS) % LANES, 1)
    shifted = lax.rem(lane + (LANES - first), LANES)
    inner = jnp.where(shifted < GROUP, turned, inner)
    outer = jnp.where(lax.rem(shifted + STEPS, LANES) < GROUP, turned, outer)
    return inner, outer


def pack_edges(rows, first_x, nx, nz, inner, outer, tile, fresh):
    lane = lane_ids(tile)
    wanted, have = rows

    def body(i, carry):
        k = i * tile
        for t in range(2):
            at = pl.ds(pl.multiple_of(t * nz + k, 8), tile)
            if fresh:
                packed = (jnp.zeros((tile, LANES), F32),) * 2
            else:
                packed = (inner[at, :], outer[at, :])
            for u, x, group in strip_places(nx):
                if u == t and x in wanted:
                    packed = add_edges(have(x, k), group, lane, *packed)
            inner[at, :], outer[at, :] = packed
        return carry

    lax.fori_loop(0, nz // tile, body, 0, unroll=2)


def own_kernel(nz, nx, nat, h_row, inv, b_t, u0, h_wide, inner, outer):
    eye = lax.broadcasted_iota(jnp.int32, (nz, nz), 0) == lax.broadcasted_iota(jnp.int32, (nz, nz), 1)
    column = jnp.sum(jnp.where(eye, jnp.broadcast_to(h_row[...], (nz, nz)), 0.0), axis=1, keepdims=True)
    h_wide[...] = jnp.broadcast_to(column, (nz, LANES))
    for x in range(nx):
        b_t[x * nz : (x + 1) * nz, :] = nat[pl.ds(x, nz, stride=nx), :]
    have = lambda x, k: b_t[pl.ds(pl.multiple_of(x * nz + k, 8), 8), :]
    pack_edges((range(nx), have), 0, nx, nz, inner, outer, 8, True)
    apply_inverse(inv[...], b_t, u0, nz, nx, nx)


def pack_kernel(nz, nx, inner_own, outer_own, below, above, inner, outer):
    inner[...] = inner_own[...]
    outer[...] = outer_own[...]

    def have(x, k):
        ref, r = (below, x + STEPS) if x < 0 else (above, x - nx)
        return ref[pl.ds(pl.multiple_of(r * nz + k, 8), 8), :]

    wanted = [*range(-STEPS, 0), *range(nx, nx + STEPS)]
    pack_edges((wanted, have), -STEPS, nx, nz, inner, outer, 8, False)


def rows_at(ref, k, tile, nz):
    return lambda r: ref[pl.ds(pl.multiple_of(r * nz + k, 8), tile), :]


def sideways(mid, step=1):
    return pltpu.roll(mid, step, 1) + pltpu.roll(mid, LANES - step, 1)


def stencil(v, g, h_ref, nz, count, tile=8, unroll=4):
    def body(i, carry):
        k = i * tile
        load = rows_at(v, k, tile, nz)
        h = h_ref[pl.ds(pl.multiple_of(k, 8), tile), :]
        for j in range(count):
            g[pl.ds(pl.multiple_of(j * nz + k, 8), tile), :] = h * ((load(j) + load(j + 2)) + sideways(load(j + 1)))
        return carry

    lax.fori_loop(0, nz // tile, body, 0, unroll=unroll)


def inner_terms(b, f1, f2, f3, v0, v1, v2):
    a0, a1, a2 = b - f1, f1 - f2, f2 - f3
    return v0 * a0, v1 * a0, v1 * a1, v2 * a0, v2 * a1, v2 * a2, v0 * b, v1 * b, v2 * b


def add_all(a, b):
    return tuple(p + q for p, q in zip(a, b))


def main_kernel(nz, nx, b_t, u0, below, above, inv, h_wide, u0e, u1e, u2e, g1e, g2e, g3, sums_out):
    u0e[STEPS * nz : (STEPS + nx) * nz, :] = u0[...]
    for ref, first in ((below, 0), (above, STEPS + nx)):
        out = product(inv[...], jnp.concatenate([ref[i * nz : (i + 1) * nz, :] for i in range(STEPS)], axis=1))
        for i in range(STEPS):
            u0e[(first + i) * nz : (first + i + 1) * nz, :] = out[:, i * LANES : (i + 1) * LANES]
    stencil(u0e, g1e, h_wide, nz, nx + 4)
    apply_inverse(inv[...], g1e, u1e, nz, nx + 4, nx + 4)
    stencil(u1e, g2e, h_wide, nz, nx + 2)
    apply_inverse(inv[...], g2e, u2e, nz, nx + 2, nx + 2)
    tile = 8

    def body(i, sums):
        k = i * tile
        at_b, at_0, at_1, at_2, at_f1, at_f2 = (rows_at(ref, k, tile, nz) for ref in (b_t, u0e, u1e, u2e, g1e, g2e))
        h = h_wide[pl.ds(pl.multiple_of(k, 8), tile), :]
        part = None
        for x in range(nx):
            v2 = at_2(x + 1)
            f3 = h * ((at_2(x) + at_2(x + 2)) + sideways(v2))
            g3[pl.ds(pl.multiple_of(x * nz + k, 8), tile), :] = f3
            terms = inner_terms(at_b(x), at_f1(x + 2), at_f2(x + 1), f3, at_0(x + 3), at_1(x + 2), v2)
            part = terms if part is None else add_all(part, terms)
        return add_all(sums, part)

    sums = lax.fori_loop(0, nz // tile, body, (jnp.zeros((tile, LANES), F32),) * 9)
    lane = lane_ids(tile)
    for i, s in enumerate(sums):
        sums_out[8 * i : 8 * i + 8, :] = jnp.where((lane >= STEPS) & (lane < LANES - STEPS), s, 0.0)


def strip_kernel(nz, nx, members, inner, outer, left, right, inv, h_wide, sums_in, bs, u0s, u1s, u2s, g1s, g2s, g3s, send):
    tile = 8
    lane = lane_ids(nz)
    pos = lax.rem(lane, GROUP)
    used = lane < GROUP * (nx // 2 + 2 * STEPS)
    for t in range(2):
        at = slice(t * nz, (t + 1) * nz)
        bs[t * nz : (t + 1) * nz, :] = jnp.where((pos < STEPS) & used, left[at, :], inner[at, :])
        bs[(t + 2) * nz : (t + 3) * nz, :] = jnp.where((pos >= STEPS) & (pos < 2 * STEPS) & used, right[at, :], outer[at, :])

    def spread(v, g):
        def body(i, carry):
            k = i * tile
            load = rows_at(v, k, tile, nz)
            h = h_wide[pl.ds(pl.multiple_of(k, 8), tile), :]
            for j in range(4):
                mid = load(j)
                g[pl.ds(pl.multiple_of(j * nz + k, 8), tile), :] = h * (sideways(mid) + sideways(mid, GROUP))
            return carry

        lax.fori_loop(0, nz // tile, body, 0, unroll=4)

    apply_inverse(inv[...], bs, u0s, nz, 4, 4)
    spread(u0s, g1s)
    apply_inverse(inv[...], g1s, u1s, nz, 4, 4)
    spread(u1s, g2s)
    apply_inverse(inv[...], g2s, u2s, nz, 4, 4)
    lane8 = lane_ids(tile)
    pos8 = lax.rem(lane8, GROUP)
    rows = (lane8 >= GROUP * STEPS) & (lane8 < GROUP * (STEPS + nx // 2))

    def body(i, sums):
        k = i * tile
        at_b, at_0, at_1, at_2, at_f1, at_f2 = (rows_at(ref, k, tile, nz) for ref in (bs, u0s, u1s, u2s, g1s, g2s))
        h = h_wide[pl.ds(pl.multiple_of(k, 8), tile), :]
        part = [None, None]
        for j in range(4):
            v2 = at_2(j)
            f3 = h * (sideways(v2) + sideways(v2, GROUP))
            g3s[pl.ds(pl.multiple_of(j * nz + k, 8), tile), :] = f3
            terms = inner_terms(at_b(j), at_f1(j), at_f2(j), f3, at_0(j), at_1(j), v2)
            part[j // 2] = terms if part[j // 2] is None else add_all(part[j // 2], terms)
        mine = tuple(
            jnp.where(rows & (pos8 >= STEPS) & (pos8 < 2 * STEPS), p, jnp.where(rows & (pos8 < STEPS), q, 0.0))
            for p, q in zip(*part)
        )
        return add_all(sums, mine)

    sums = tuple(sums_in[8 * i : 8 * i + 8, :] for i in range(9))
    sums = lax.fori_loop(0, nz // tile, body, sums)
    out = jnp.zeros((8, LANES), F32)
    for i, s in enumerate(sums):
        total = jnp.sum(jnp.sum(s, axis=0, keepdims=True), axis=1, keepdims=True)
        out = jnp.where(lane8 == i, jnp.broadcast_to(total, (8, LANES)), out)
    for i in range(members // 8):
        send[8 * i : 8 * i + 8, :] = out


def fold(v):
    out = v[0:8]
    for i in range(1, v.shape[0] // 8):
        out = out + v[8 * i : 8 * i + 8]
    return out


def solve_small(t):
    g00, g10, g11, g20, g21, g22, m0, m1, m2 = t
    l1, l2 = g10 / g00, g20 / g00
    d1 = g11 - l1 * g10
    e = g21 - l2 * g10
    l3 = e / d1
    d2 = g22 - l2 * g20 - l3 * e
    y1 = m1 - l1 * m0
    y2 = m2 - l2 * m0 - l3 * y1
    c2 = y2 / d2
    c1 = y1 / d1 - l3 * c2
    return m0 / g00 - l1 * c1 - l2 * c2, c1, c2


def combine_kernel(nz, nx, kz, *refs):
    got, fields, strips, outs, coef = refs[0], refs[1:8], refs[8:15], refs[15:17], refs[17]
    step = pl.program_id(0)

    @pl.when(step == 0)
    def _():
        total = jnp.sum(fold(got[...]), axis=0, keepdims=True)
        line = lax.broadcasted_iota(jnp.int32, (1, LANES), 1)
        pick = lambda i: jnp.sum(jnp.where(line == i, total, 0.0), axis=1, keepdims=True)
        for i, c in enumerate(solve_small([pick(i) for i in range(9)])):
            coef[i * 8 : i * 8 + 8, :] = jnp.broadcast_to(c, (8, LANES))

    c0, c1, c2 = (jnp.concatenate([coef[i * 8 : i * 8 + 8, :]] * (kz // 8), axis=0) for i in range(3))
    lane = lane_ids(kz)
    inside = (lane >= STEPS) & (lane < LANES - STEPS)
    pos = lax.rem(lane, GROUP)

    def combined(b, v0, v1, v2, f1, f2, f3):
        return c0 * v0 + c1 * v1 + c2 * v2, b - (c0 * (b - f1) + c1 * (f1 - f2) + c2 * (f2 - f3))

    def at(ref, r):
        return ref[pl.ds(pl.multiple_of(r * nz + step * kz, 8), kz), :]

    edges = []
    for t in range(2):
        near, far = combined(*(at(ref, t) for ref in strips)), combined(*(at(ref, t + 2) for ref in strips))
        edges.append([jnp.where(pos >= STEPS, p, q) for p, q in zip(near, far)])
    for t, x, group in strip_places(nx):
        if not t * (nx // 2) <= x < (t + 1) * (nx // 2):
            continue
        values = combined(*(at(ref, x + skip) for ref, skip in zip(fields, (0, 3, 2, 1, 2, 1, 0))))
        for out, value, edge in zip(outs, values, edges[t]):
            turned = pltpu.roll(edge, (-(GROUP * group + STEPS)) % LANES, 1)
            out[pl.ds(x, kz, stride=nx), :] = jnp.where(inside, value, turned)


def neighbours(array, axes, up):
    size = lax.axis_size(axes)
    pairs = [(i, (i + 1) % size) for i in range(size)]
    return lax.ppermute(array, axes, pairs if up else [(b, a) for a, b in pairs])


def on_device(source_heat, horiz_coef, face_coef, column_inverse):
    nz, nx, ny = source_heat.shape
    gx, gy = "gx", "gy"
    members = lax.axis_size(gx) * lax.axis_size(gy)
    part = lambda f, *a: (lambda *refs: f(*a, *refs))
    nat = source_heat.reshape(nz * nx, ny)
    low, high = pl.pallas_call(
        part(load_kernel, nz, nx),
        in_specs=[spec()],
        out_specs=[spec()] * 2,
        out_shape=[vmem(STEPS * nz)] * 2,
        compiler_params=params(4),
    )(nat)
    below = neighbours(high, gx, True)
    above = neighbours(low, gx, False)
    b_t, u0, h_wide, inner_own, outer_own = pl.pallas_call(
        part(own_kernel, nz, nx),
        in_specs=[spec()] * 3,
        out_specs=[spec()] * 5,
        out_shape=[vmem(nz * nx), vmem(nz * nx), vmem(nz), vmem(2 * nz), vmem(2 * nz)],
        compiler_params=params(8),
        cost_estimate=cost(12 * nz * nz * nx * ny, 1 << 20),
    )(nat, horiz_coef.reshape(1, nz), column_inverse)
    inner, outer = pl.pallas_call(
        part(pack_kernel, nz, nx),
        in_specs=[spec()] * 4,
        out_specs=[spec()] * 2,
        out_shape=[vmem(2 * nz)] * 2,
        compiler_params=params(4),
    )(inner_own, outer_own, below, above)
    from_left = neighbours(inner, gy, True)
    from_right = neighbours(inner, gy, False)
    u0e, u1e, u2e, g1e, g2e, g3, sums = pl.pallas_call(
        part(main_kernel, nz, nx),
        in_specs=[spec()] * 6,
        out_specs=[spec()] * 7,
        out_shape=[vmem(r * nz) for r in (nx + 6, nx + 4, nx + 2, nx + 4, nx + 2, nx)] + [vmem(72)],
        compiler_params=params(12),
        cost_estimate=cost(36 * nz * nz * nx * ny, 1 << 20),
    )(b_t, u0, below, above, column_inverse, h_wide)
    *strips, send = pl.pallas_call(
        part(strip_kernel, nz, nx, members),
        in_specs=[spec()] * 7,
        out_specs=[spec()] * 8,
        out_shape=[vmem(4 * nz)] * 7 + [vmem(members)],
        compiler_params=params(8),
    )(inner, outer, from_left, from_right, column_inverse, h_wide, sums)
    got = lax.all_to_all(send.reshape(members, 1, LANES), (gx, gy), split_axis=0, concat_axis=0, tiled=True)
    kz = 32
    pressure, true_residual = pl.pallas_call(
        part(combine_kernel, nz, nx, kz),
        grid=(nz // kz,),
        in_specs=[spec()] * 15,
        out_specs=[pl.BlockSpec((kz * nx, ny), lambda i: (i, 0))] * 2,
        out_shape=[jax.ShapeDtypeStruct((nz * nx, ny), F32)] * 2,
        scratch_shapes=[pltpu.VMEM((24, LANES), F32)],
        compiler_params=params(8),
    )(got.reshape(members, LANES), b_t, u0e, u1e, u2e, g1e, g2e, g3, *strips)
    return pressure.reshape(nz, nx, ny), true_residual.reshape(nz, nx, ny)


def solution(mesh):
    field = P(None, "gx", "gy")
    return jax.shard_map(
        on_device,
        mesh=mesh,
        in_specs=(field, P(), P(), P()),
        out_specs=(field, field),
        check_vma=False,
    )
```

time: 63.8 us -> 59.7 us (0.936)
  waiting for transfers between devices: 4.06 us -> 0.01 us
  local copies, waits for them, and re-layouts: 1.32 us -> 2.24 us
    ppermute x4, waiting for transfers between devices: 4.06 us -> 0.01 us  [neighbours(): lax.ppermute(array, axes, pairs if up else [(b, a) for a, b in pairs])]
    unnamed x6 -> x10, local copies, waits for them, and re-layouts: 1.32 us -> 2.24 us
    pallas_call x4, Pallas kernels: 14.9 us -> 14.2 us  [the longest x1 8.48 us: on_device(): pl.pallas_call(part(main_kernel, nz, nx), in_specs=[spec()] * 6, out_spec...]
  transfers between devices with their start and end apart: 4 -> 4, of which waited for: 3 -> 0; matrix products, arithmetic and copies ran while one was open for 0% -> 0% of each run, Pallas kernels for 5% -> 19%
where the time goes in v2:
time: 59.7 us; the launch traced here: 59.6 us
  blocking collectives  25.6 us (43%)
  Pallas kernels  20.6 us (35%)
  starting transfers between devices  10.5 us (18%)
  local copies, waits for them, and re-layouts  2.24 us (4%)
  between operations  0.71 us (1%)
    all_to_all x1, blocking collectives, on_device(): lax.all_to_all(send.reshape(members, 1, LANES), (gx, gy), split_axis=0, c...  25.6 us
    ppermute x4, starting transfers between devices, neighbours(): lax.ppermute(array, axes, pairs if up else [(b, a) for a, b in pairs])  10.5 us
    pallas_call x1, Pallas kernels, on_device(): pl.pallas_call(part(main_kernel, nz, nx), in_specs=[spec()] * 6, out_spec...  8.48 us
    pallas_call x1, Pallas kernels, on_device(): pl.pallas_call(part(strip_kernel, nz, nx, members), in_specs=[spec()] * 7...  4.67 us
    pallas_call x1, Pallas kernels, on_device(): pl.pallas_call(part(combine_kernel, nz, nx, kz), grid=(nz // kz,), in_spe...  3.58 us
    pallas_call x1, Pallas kernels, on_device(): pl.pallas_call(part(own_kernel, nz, nx), in_specs=[spec()] * 3, out_specs...  2.86 us
    unnamed x10, local copies, waits for them, and re-layouts  2.24 us
  transfers between devices with their start and end apart: 4, of which 0 were waited for; matrix products, arithmetic and copies ran while one was open for 0% of the time, Pallas kernels for 19%

profile of v2, /device:TPU:1, one launch (start us, length us, event | category | flops | bytes accessed | tf_op | source)
XLA Modules:
  0.0 59.6 jit_solution(17356879407166011534)
XLA Ops:
  0.6 0.0 copy-start.4
  0.6 0.0 copy-start
  0.6 1.3 %copy-done = f32[160,16,128]{2,1,0:T(8,128)S(1)} copy-done((f32[160,16,128]{2,1,0:T(8,128)S(1)}, f32[160,16,128]{2,1,0:T(8,128)}, u32[]{:S(2)}) %copy-start) | copy-done | bytes 1310744
  2.0 0.0 copy-start.1
  2.0 0.2 shard_map.51
  2.2 2.1 %collective-permute-start = (f32[480,128]{1,0:T(8,128)S(1)}, f32[480,128]{1,0:T(8,128)S(1)}, u32[]{:S(2)}, u32[]{:S(2)}) collective-permute-start(f32[480,128]{1,0:T(8,128)S(1)} %get-tuple-element.30), channel_id=1, source_target_pairs={{0,16},{16,32},{32,48},{48,64},{64,80},{80,96},{96,112},{112,128},... | collective-permute-start | bytes 737288 | tf_op jit(solution)/shard_map/ppermute | solution.py:300
  4.3 3.8 %collective-permute-start.1 = (f32[480,128]{1,0:T(8,128)S(1)}, f32[480,128]{1,0:T(8,128)S(1)}, u32[]{:S(2)}, u32[]{:S(2)}) collective-permute-start(f32[480,128]{1,0:T(8,128)S(1)} %get-tuple-element.31), channel_id=1, source_target_pairs={{16,0},{32,16},{48,32},{64,48},{80,64},{96,80},{112,96},{128,112},... | collective-permute-start | bytes 737288 | tf_op jit(solution)/shard_map/ppermute | solution.py:300
  8.1 0.0 copy-done.4
  8.1 0.0 copy-done.1
  8.1 0.0 copy-start.2
  8.1 0.9 %copy-done.2 = f32[160,160]{1,0:T(8,128)S(1)} copy-done((f32[160,160]{1,0:T(8,128)S(1)}, f32[160,160]{1,0:T(8,128)}, u32[]{:S(2)}) %copy-start.2) | copy-done | bytes 102424
  9.0 0.0 copy-start.3
  9.0 2.9 %shard_map.50 = (f32[2560,128]{1,0:T(8,128)S(1)}, f32[2560,128]{1,0:T(8,128)S(1)}, f32[160,128]{1,0:T(8,128)S(1)}, f32[320,128]{1,0:T(8,128)S(1)}, f32[320,128]{1,0:T(8,128)S(1)}) custom-call(f32[2560,128]{1,0:T(8,128)S(1)} %bitcast.9, f32[1,160]{1,0:T(1,128)S(1)} %bitcast.12, f32[160,160]{1,0:T(8,128)S(1)} %copy-done.2), custom_call_target="tpu_custom_call" | custom-call | flops 629145600 | bytes 1048576 | tf_op jit(solution)/shard_map/pallas_call | solution.py:318
  11.9 0.0 collective-permute-done.refs_2_
  11.9 0.0 collective-permute-done.1.refs_3_
  11.9 0.8 %shard_map.52 = (f32[320,128]{1,0:T(8,128)S(1)}, f32[320,128]{1,0:T(8,128)S(1)}) custom-call(f32[320,128]{1,0:T(8,128)S(1)} %get-tuple-element.28.refs_0_, f32[320,128]{1,0:T(8,128)S(1)} %get-tuple-element.29.refs_1_, f32[480,128]{1,0:T(8,128)S(1)} %collective-permute-done.refs_2_, f32[480,128]{1,0:T(8,128)S(1)} %collective-permute-done.1.refs_3_), custom_call_target="tpu_custom_call" | custom-call | tf_op jit(solution)/shard_map/pallas_call | solution.py:326
  12.7 3.1 %collective-permute-start.3 = (f32[320,128]{1,0:T(8,128)S(1)}, f32[320,128]{1,0:T(8,128)S(1)}, u32[]{:S(2)}, u32[]{:S(2)}) collective-permute-start(f32[320,128]{1,0:T(8,128)S(1)} %get-tuple-element.32.refs_0_), channel_id=1, source_target_pairs={{1,0},{2,1},{3,2},{4,3},{5,4},{6,5},{7,6},{8,7},{9,8},{10,9},{11,1... | collective-permute-start | bytes 491528 | tf_op jit(solution)/shard_map/ppermute | solution.py:300
  15.8 1.5 %collective-permute-start.2 = (f32[320,128]{1,0:T(8,128)S(1)}, f32[320,128]{1,0:T(8,128)S(1)}, u32[]{:S(2)}, u32[]{:S(2)}) collective-permute-start(f32[320,128]{1,0:T(8,128)S(1)} %get-tuple-element.32.refs_0_), channel_id=1, source_target_pairs={{0,1},{1,2},{2,3},{3,4},{4,5},{5,6},{6,7},{7,8},{8,9},{9,10},{10,1... | collective-permute-start | bytes 491528 | tf_op jit(solution)/shard_map/ppermute | solution.py:300
  17.3 0.0 copy-done.3
  17.3 8.5 %shard_map.53 = (f32[3520,128]{1,0:T(8,128)S(1)}, f32[3200,128]{1,0:T(8,128)S(1)}, f32[2880,128]{1,0:T(8,128)S(1)}, f32[3200,128]{1,0:T(8,128)S(1)}, f32[2880,12...) custom-call(f32[2560,128]{1,0:T(8,128)S(1)} %get-tuple-element.35.refs_0_.refs_1_, ...), custom_call_target="tpu_custom_call" | custom-call | flops 1887436800 | bytes 1048576 | tf_op jit(solution)/shard_map/pallas_call | solution.py:335
  25.8 0.0 collective-permute-done.3.refs_3_
  25.8 0.0 collective-permute-done.2.refs_2_
  25.8 4.7 %shard_map.54 = (f32[640,128]{1,0:T(8,128)S(1)}, f32[640,128]{1,0:T(8,128)S(1)}, f32[640,128]{1,0:T(8,128)S(1)}, f32[640,128]{1,0:T(8,128)S(1)}, f32[640,128]{1,...) custom-call(f32[320,128]{1,0:T(8,128)S(1)} %get-tuple-element.32.refs_0_, ...), custom_call_target="tpu_custom_call" | custom-call | tf_op jit(solution)/shard_map/pallas_call | solution.py:343
  30.5 25.6 %all_to_all.5 = f32[256,1,128]{2,1,0:T(1,128)S(1)} all-to-all(f32[256,1,128]{2,1,0:T(1,128)S(1)} %bitcast.11), channel_id=1, replica_groups=mesh['gx'=16,'gy'=16] {'gx','gy'}, dimensions={0} | all-to-all | bytes 262144 | tf_op jit(solution)/shard_map/all_to_all | solution.py:350
  56.0 3.6 %shard_map.55 = (f32[2560,128]{1,0:T(8,128)}, f32[2560,128]{1,0:T(8,128)}) custom-call(f32[256,128]{1,0:T(8,128)S(1)} %bitcast.10, f32[2560,128]{1,0:T(8,128)S(1)} %get-tuple-element.35.refs_0_.refs_1_, f32[3520,128]{1,0:T(8,128)S(1)} %get-tuple-element.39.refs_2_, f32[3200,128]{1,0:T(8,128)S(1)} %get-tuple-element.40.refs_3_, ...), custom_call_target="tpu_custom_call" | custom-call | tf_op jit(solution)/shard_map/pallas_call | solution.py:352
Async XLA Ops:
  0.6 7.4 %copy-start.4 = (f32[160]{0:T(256)S(1)}, f32[160]{0:T(256)}, u32[]{:S(2)}) copy-start(f32[160]{0:T(256)} %param.5) | copy-start | bytes 1924
  0.6 1.3 %copy-start = (f32[160,16,128]{2,1,0:T(8,128)S(1)}, f32[160,16,128]{2,1,0:T(8,128)}, u32[]{:S(2)}) copy-start(f32[160,16,128]{2,1,0:T(8,128)} %param.4) | copy-start | bytes 3932164
  2.0 6.1 %copy-start.1 = (f32[160,16,128]{2,1,0:T(8,128)S(1)}, f32[160,16,128]{2,1,0:T(8,128)}, u32[]{:S(2)}) copy-start(f32[160,16,128]{2,1,0:T(8,128)} %param.4) | copy-start | bytes 3932164
  2.2 9.7 %collective-permute-start = (f32[480,128]{1,0:T(8,128)S(1)}, f32[480,128]{1,0:T(8,128)S(1)}, u32[]{:S(2)}, u32[]{:S(2)}) collective-permute-start(f32[480,128]{1,0:T(8,128)S(1)} %get-tuple-element.30), channel_id=1, source_target_pairs={{0,16},{16,32},{32,48},{48,64},{64,80},{80,96},{96,112},{112,128},... | collective-permute-start | bytes 737288 | tf_op jit(solution)/shard_map/ppermute | solution.py:300
  4.3 7.6 %collective-permute-start.1 = (f32[480,128]{1,0:T(8,128)S(1)}, f32[480,128]{1,0:T(8,128)S(1)}, u32[]{:S(2)}, u32[]{:S(2)}) collective-permute-start(f32[480,128]{1,0:T(8,128)S(1)} %get-tuple-element.31), channel_id=1, source_target_pairs={{16,0},{32,16},{48,32},{64,48},{80,64},{96,80},{112,96},{128,112},... | collective-permute-start | bytes 737288 | tf_op jit(solution)/shard_map/ppermute | solution.py:300
  8.1 0.9 %copy-start.2 = (f32[160,160]{1,0:T(8,128)S(1)}, f32[160,160]{1,0:T(8,128)}, u32[]{:S(2)}) copy-start(f32[160,160]{1,0:T(8,128)} %refs_4_.3) | copy-start | bytes 307204
  9.0 8.3 %copy-start.3 = (f32[160,160]{1,0:T(8,128)S(1)}, f32[160,160]{1,0:T(8,128)}, u32[]{:S(2)}) copy-start(f32[160,160]{1,0:T(8,128)} %refs_4_.3) | copy-start | bytes 307204
  12.7 13.0 %collective-permute-start.3 = (f32[320,128]{1,0:T(8,128)S(1)}, f32[320,128]{1,0:T(8,128)S(1)}, u32[]{:S(2)}, u32[]{:S(2)}) collective-permute-start(f32[320,128]{1,0:T(8,128)S(1)} %get-tuple-element.32.refs_0_), channel_id=1, source_target_pairs={{1,0},{2,1},{3,2},{4,3},{5,4},{6,5},{7,6},{8,7},{9,8},{10,9},{11,1... | collective-permute-start | bytes 491528 | tf_op jit(solution)/shard_map/ppermute | solution.py:300
  15.8 10.0 %collective-permute-start.2 = (f32[320,128]{1,0:T(8,128)S(1)}, f32[320,128]{1,0:T(8,128)S(1)}, u32[]{:S(2)}, u32[]{:S(2)}) collective-permute-start(f32[320,128]{1,0:T(8,128)S(1)} %get-tuple-element.32.refs_0_), channel_id=1, source_target_pairs={{0,1},{1,2},{2,3},{3,4},{4,5},{5,6},{6,7},{7,8},{8,9},{9,10},{10,1... | collective-permute-start | bytes 491528 | tf_op jit(solution)/shard_map/ppermute | solution.py:300

commit v3 on v2

v3 whole, which is shorter than its diff:
```python
import jax
import jax.numpy as jnp
from jax import lax
from jax.experimental import pallas as pl
from jax.experimental.pallas import tpu as pltpu
from jax.sharding import Mesh
from jax.sharding import PartitionSpec as P

F32 = jnp.float32
BF16 = jnp.bfloat16
LANES = 128
GROUP = 9
STEPS = 3
WIDTH = 4


def vmem(rows, cols=LANES):
    return pltpu.VMEM((rows, cols), F32)


def spec():
    return pl.BlockSpec(memory_space=pltpu.VMEM)


def params(mib):
    return pltpu.CompilerParams(vmem_limit_bytes=mib * 1024 * 1024)


def cost(flops, size):
    return pl.CostEstimate(flops=flops, bytes_accessed=size, transcendentals=0)


def lane_ids(rows):
    return lax.broadcasted_iota(jnp.int32, (rows, LANES), 1)


def pieces(v):
    high = v.astype(BF16)
    rest = v - high.astype(F32)
    middle = rest.astype(BF16)
    return high, middle, (rest - middle.astype(F32)).astype(BF16)


def product(factors, columns):
    nz = columns.shape[0]
    stacked = jnp.concatenate(pieces(columns), axis=0)
    dot = lambda f, count: jnp.dot(f[...], stacked[: count * nz], preferred_element_type=F32)
    return dot(factors[0], 3) + dot(factors[1], 2) + dot(factors[2], 1)


def apply_inverse(factors, src, dst, nz, tiles, width):
    for first in range(0, tiles, width):
        count = min(width, tiles - first)
        parts = [src[(first + t) * nz : (first + t + 1) * nz, :] for t in range(count)]
        out = product(factors, jnp.concatenate(parts, axis=1) if count > 1 else parts[0])
        for t in range(count):
            dst[(first + t) * nz : (first + t + 1) * nz, :] = out[:, t * LANES : (t + 1) * LANES]


def load_kernel(nz, nx, nat, inv, low, high, inv_out):
    inv_out[...] = inv[...]
    for i in range(STEPS):
        low[i * nz : (i + 1) * nz, :] = nat[pl.ds(i, nz, stride=nx), :]
        high[i * nz : (i + 1) * nz, :] = nat[pl.ds(nx - STEPS + i, nz, stride=nx), :]


def place(lane):
    return lane - GROUP * lax.shift_right_logical(lane * 57, 9)


def strip_places(nx):
    half = nx // 2
    count = half + 2 * STEPS
    return [(t, t * half - STEPS + r, r) for t in range(2) for r in range(count)]


def add_edges(row, group, lane, inner, outer):
    first = GROUP * group
    turned = pltpu.roll(row, (first + STEPS) % LANES, 1)
    inner = jnp.where((lane >= first) & (lane < first + GROUP), turned, inner)
    if first:
        mine = (lane >= first - STEPS) & (lane < first + 2 * STEPS)
    else:
        mine = (lane >= LANES - STEPS) | (lane < 2 * STEPS)
    outer = jnp.where(mine, turned, outer)
    return inner, outer


def pack_edges(rows, first_x, nx, nz, inner, outer, tile, fresh):
    lane = lane_ids(tile)
    wanted, have = rows

    def body(i, carry):
        k = i * tile
        for t in range(2):
            at = pl.ds(pl.multiple_of(t * nz + k, 8), tile)
            if fresh:
                packed = (jnp.zeros((tile, LANES), F32),) * 2
            else:
                packed = (inner[at, :], outer[at, :])
            for u, x, group in strip_places(nx):
                if u == t and x in wanted:
                    packed = add_edges(have(x, k), group, lane, *packed)
            inner[at, :], outer[at, :] = packed
        return carry

    lax.fori_loop(0, nz // tile, body, 0, unroll=4 if fresh else True)


def own_kernel(nz, nx, nat, h_row, inv, b_t, u0, h_wide, inner, outer, *factors):
    for ref, piece, count in zip(factors, pieces(inv[...]), (3, 2, 1)):
        wide = piece.astype(F32)
        ref[...] = jnp.concatenate([wide] * count, axis=1).astype(BF16) if count > 1 else piece
    eye = lax.broadcasted_iota(jnp.int32, (nz, nz), 0) == lax.broadcasted_iota(jnp.int32, (nz, nz), 1)
    column = jnp.sum(jnp.where(eye, jnp.broadcast_to(h_row[...], (nz, nz)), 0.0), axis=1, keepdims=True)
    h_wide[...] = jnp.broadcast_to(column, (nz, LANES))
    for x in range(nx):
        b_t[x * nz : (x + 1) * nz, :] = nat[pl.ds(x, nz, stride=nx), :]
    have = lambda x, k: b_t[pl.ds(pl.multiple_of(x * nz + k, 8), 8), :]
    pack_edges((range(nx), have), 0, nx, nz, inner, outer, 8, True)
    apply_inverse(factors, b_t, u0, nz, nx, nx)


def pack_kernel(nz, nx, inner_own, outer_own, below, above, inner, outer):
    inner[...] = inner_own[...]
    outer[...] = outer_own[...]

    def have(x, k):
        ref, r = (below, x + STEPS) if x < 0 else (above, x - nx)
        return ref[pl.ds(pl.multiple_of(r * nz + k, 8), 8), :]

    wanted = [*range(-STEPS, 0), *range(nx, nx + STEPS)]
    pack_edges((wanted, have), -STEPS, nx, nz, inner, outer, 8, False)


def sideways(mid, step=1):
    return pltpu.roll(mid, step, 1) + pltpu.roll(mid, LANES - step, 1)


class Sums:
    def __init__(self):
        self.total = {}

    def add(self, terms):
        for name in terms[0]:
            row = terms[0][name]
            for more in terms[1:]:
                row = row + more[name]
            self.total[name] = row if name not in self.total else self.total[name] + row


NAMES = ("00", "10", "11", "20", "21", "22", "0b", "1b", "2b")


def stage_terms(level, b, gs, v):
    chain = (b, *gs)
    out = {f"{level}{j}": v * (chain[j] - chain[j + 1]) for j in range(level + 1)}
    out[f"{level}b"] = v * b
    return out


def advance(factors, neighbours_of, g, u, h_ref, nz, count, width, visit, tile=8):
    for first in range(0, count, width):
        rows = []
        for j in range(first, min(first + width, count)):
            parts, terms = [], []
            for k in range(0, nz, tile):
                parts.append(h_ref[k : k + tile, :] * neighbours_of(j, k))
                found = visit(j, k, parts[-1])
                if found:
                    terms.append(found)
            visit.finish(j, terms)
            rows.append(jnp.concatenate(parts, axis=0))
            g[j * nz : (j + 1) * nz, :] = rows[-1]
        if u is None:
            continue
        out = product(factors, jnp.concatenate(rows, axis=1) if len(rows) > 1 else rows[0])
        for t in range(len(rows)):
            u[(first + t) * nz : (first + t + 1) * nz, :] = out[:, t * LANES : (t + 1) * LANES]


class Visit:
    def __init__(self, level, nz, fields, rows, sums_of):
        self.level, self.nz, self.fields, self.rows, self.sums_of = level, nz, fields, rows, sums_of

    def __call__(self, j, k, g):
        x = self.rows(j)
        if x is None:
            return None
        b, *gs, v = (ref[(x + skip) * self.nz + k : (x + skip) * self.nz + k + 8, :] for ref, skip in self.fields)
        return stage_terms(self.level, b, (*gs, g), v)

    def finish(self, j, terms):
        if terms:
            self.sums_of(j).add(terms)


def main_kernel(nz, nx, b_t, u0, below, above, h_wide, f0, f1, f2, u0e, u1e, u2e, g1e, g2e, g3, sums_out):
    u0e[STEPS * nz : (STEPS + nx) * nz, :] = u0[...]
    factors = (f0, f1, f2)
    for ref, first in ((below, 0), (above, STEPS + nx)):
        apply_inverse(factors, ref, u0e.at[pl.ds(first * nz, STEPS * nz), :], nz, STEPS, STEPS)
    sums = Sums()

    def around(v):
        def of(j, k):
            at = lambda r: v[r * nz + k : r * nz + k + 8, :]
            return (at(j) + at(j + 2)) + sideways(at(j + 1))

        return of

    inside = lambda extra: (lambda j: j - extra if 0 <= j - extra < nx else None)
    b_f, f1_f, f2_f = (b_t, 0), (g1e, 2), (g2e, 1)
    one = Visit(0, nz, (b_f, (u0e, 3)), inside(2), lambda j: sums)
    advance(factors, around(u0e), g1e, u1e, h_wide, nz, nx + 4, WIDTH, one)
    two = Visit(1, nz, (b_f, f1_f, (u1e, 2)), inside(1), lambda j: sums)
    advance(factors, around(u1e), g2e, u2e, h_wide, nz, nx + 2, WIDTH, two)
    three = Visit(2, nz, (b_f, f1_f, f2_f, (u2e, 1)), inside(0), lambda j: sums)
    advance(factors, around(u2e), g3, None, h_wide, nz, nx, WIDTH, three)
    lane = lane_ids(8)
    for i, name in enumerate(NAMES):
        sums_out[8 * i : 8 * i + 8, :] = jnp.where((lane >= STEPS) & (lane < LANES - STEPS), sums.total[name], 0.0)


def strip_kernel(nz, nx, members, inner, outer, left, right, h_wide, sums_in, f0, f1, f2, bs, u0s, u1s, u2s, g1s, g2s, g3s, send):
    factors = (f0, f1, f2)
    lane = lane_ids(nz)
    pos = place(lane)
    used = lane < GROUP * (nx // 2 + 2 * STEPS)
    for t in range(2):
        at = slice(t * nz, (t + 1) * nz)
        bs[t * nz : (t + 1) * nz, :] = jnp.where((pos < STEPS) & used, left[at, :], inner[at, :])
        bs[(t + 2) * nz : (t + 3) * nz, :] = jnp.where((pos >= STEPS) & (pos < 2 * STEPS) & used, right[at, :], outer[at, :])
    near, far = Sums(), Sums()
    sums_of = lambda j: near if j < 2 else far

    def around(v):
        def of(j, k):
            mid = v[j * nz + k : j * nz + k + 8, :]
            return sideways(mid) + sideways(mid, GROUP)

        return of

    every = lambda j: j
    apply_inverse(factors, bs, u0s, nz, 4, 4)
    advance(factors, around(u0s), g1s, u1s, h_wide, nz, 4, 4, Visit(0, nz, ((bs, 0), (u0s, 0)), every, sums_of))
    advance(factors, around(u1s), g2s, u2s, h_wide, nz, 4, 4, Visit(1, nz, ((bs, 0), (g1s, 0), (u1s, 0)), every, sums_of))
    last = Visit(2, nz, ((bs, 0), (g1s, 0), (g2s, 0), (u2s, 0)), every, sums_of)
    advance(factors, around(u2s), g3s, None, h_wide, nz, 4, 4, last)
    lane = lane_ids(8)
    pos = place(lane)
    rows = (lane >= GROUP * STEPS) & (lane < GROUP * (STEPS + nx // 2))
    out = jnp.zeros((8, LANES), F32)
    for i, name in enumerate(NAMES):
        p = jnp.where(rows & (pos >= STEPS) & (pos < 2 * STEPS), near.total[name], 0.0)
        q = jnp.where(rows & (pos < STEPS), far.total[name], 0.0)
        s = sums_in[8 * i : 8 * i + 8, :] + (p + q)
        total = jnp.sum(jnp.sum(s, axis=0, keepdims=True), axis=1, keepdims=True)
        out = jnp.where(lane == i, jnp.broadcast_to(total, (8, LANES)), out)
    for i in range(members // 8):
        send[8 * i : 8 * i + 8, :] = out


def fold(v):
    out = v[0:8]
    for i in range(1, v.shape[0] // 8):
        out = out + v[8 * i : 8 * i + 8]
    return out


def solve_small(t):
    g00, g10, g11, g20, g21, g22, m0, m1, m2 = t
    l1, l2 = g10 / g00, g20 / g00
    d1 = g11 - l1 * g10
    e = g21 - l2 * g10
    l3 = e / d1
    d2 = g22 - l2 * g20 - l3 * e
    y1 = m1 - l1 * m0
    y2 = m2 - l2 * m0 - l3 * y1
    c2 = y2 / d2
    c1 = y1 / d1 - l3 * c2
    return m0 / g00 - l1 * c1 - l2 * c2, c1, c2


def combine_kernel(nz, nx, kz, *refs):
    got, fields, strips, outs, coef = refs[0], refs[1:8], refs[8:15], refs[15:17], refs[17]
    step = pl.program_id(0)

    @pl.when(step == 0)
    def _():
        total = jnp.sum(fold(got[...]), axis=0, keepdims=True)
        line = lax.broadcasted_iota(jnp.int32, (1, LANES), 1)
        pick = lambda i: jnp.sum(jnp.where(line == i, total, 0.0), axis=1, keepdims=True)
        for i, c in enumerate(solve_small([pick(i) for i in range(9)])):
            coef[i * 8 : i * 8 + 8, :] = jnp.broadcast_to(c, (8, LANES))

    c0, c1, c2 = (jnp.concatenate([coef[i * 8 : i * 8 + 8, :]] * (kz // 8), axis=0) for i in range(3))
    lane = lane_ids(kz)
    inside = (lane >= STEPS) & (lane < LANES - STEPS)
    pos = place(lane)

    def combined(b, v0, v1, v2, f1, f2, f3):
        return c0 * v0 + c1 * v1 + c2 * v2, b - (c0 * (b - f1) + c1 * (f1 - f2) + c2 * (f2 - f3))

    def at(ref, r):
        return ref[pl.ds(pl.multiple_of(r * nz + step * kz, 8), kz), :]

    edges = []
    for t in range(2):
        near, far = combined(*(at(ref, t) for ref in strips)), combined(*(at(ref, t + 2) for ref in strips))
        edges.append([jnp.where(pos >= STEPS, p, q) for p, q in zip(near, far)])
    for t, x, group in strip_places(nx):
        if not t * (nx // 2) <= x < (t + 1) * (nx // 2):
            continue
        values = combined(*(at(ref, x + skip) for ref, skip in zip(fields, (0, 3, 2, 1, 2, 1, 0))))
        for out, value, edge in zip(outs, values, edges[t]):
            turned = pltpu.roll(edge, (-(GROUP * group + STEPS)) % LANES, 1)
            out[pl.ds(x, kz, stride=nx), :] = jnp.where(inside, value, turned)


def neighbours(array, axes, up):
    size = lax.axis_size(axes)
    pairs = [(i, (i + 1) % size) for i in range(size)]
    return lax.ppermute(array, axes, pairs if up else [(b, a) for a, b in pairs])


def on_device(source_heat, horiz_coef, face_coef, column_inverse):
    nz, nx, ny = source_heat.shape
    gx, gy = "gx", "gy"
    members = lax.axis_size(gx) * lax.axis_size(gy)
    part = lambda f, *a: (lambda *refs: f(*a, *refs))
    nat = source_heat.reshape(nz * nx, ny)
    low, high, inv = pl.pallas_call(
        part(load_kernel, nz, nx),
        in_specs=[spec()] * 2,
        out_specs=[spec()] * 3,
        out_shape=[vmem(STEPS * nz)] * 2 + [vmem(nz, nz)],
        compiler_params=params(4),
    )(nat, column_inverse)
    below = neighbours(high, gx, True)
    above = neighbours(low, gx, False)
    b_t, u0, h_wide, inner_own, outer_own, *factors = pl.pallas_call(
        part(own_kernel, nz, nx),
        in_specs=[spec()] * 3,
        out_specs=[spec()] * 8,
        out_shape=[vmem(nz * nx), vmem(nz * nx), vmem(nz), vmem(2 * nz), vmem(2 * nz)]
        + [pltpu.VMEM((nz, count * nz), BF16) for count in (3, 2, 1)],
        compiler_params=params(8),
        cost_estimate=cost(12 * nz * nz * nx * ny, 1 << 20),
    )(nat, horiz_coef.reshape(1, nz), inv)
    inner, outer = pl.pallas_call(
        part(pack_kernel, nz, nx),
        in_specs=[spec()] * 4,
        out_specs=[spec()] * 2,
        out_shape=[vmem(2 * nz)] * 2,
        compiler_params=params(4),
    )(inner_own, outer_own, below, above)
    from_left = neighbours(inner, gy, True)
    from_right = neighbours(inner, gy, False)
    u0e, u1e, u2e, g1e, g2e, g3, sums = pl.pallas_call(
        part(main_kernel, nz, nx),
        in_specs=[spec()] * 8,
        out_specs=[spec()] * 7,
        out_shape=[vmem(r * nz) for r in (nx + 6, nx + 4, nx + 2, nx + 4, nx + 2, nx)] + [vmem(72)],
        compiler_params=params(12),
        cost_estimate=cost(36 * nz * nz * nx * ny, 1 << 20),
    )(b_t, u0, below, above, h_wide, *factors)
    *strips, send = pl.pallas_call(
        part(strip_kernel, nz, nx, members),
        in_specs=[spec()] * 9,
        out_specs=[spec()] * 8,
        out_shape=[vmem(4 * nz)] * 7 + [vmem(members)],
        compiler_params=params(8),
    )(inner, outer, from_left, from_right, h_wide, sums, *factors)
    got = lax.all_to_all(send.reshape(members, 1, LANES), (gx, gy), split_axis=0, concat_axis=0, tiled=True)
    kz = 80
    pressure, true_residual = pl.pallas_call(
        part(combine_kernel, nz, nx, kz),
        grid=(nz // kz,),
        in_specs=[spec()] * 15,
        out_specs=[pl.BlockSpec((kz * nx, ny), lambda i: (i, 0))] * 2,
        out_shape=[jax.ShapeDtypeStruct((nz * nx, ny), F32)] * 2,
        scratch_shapes=[pltpu.VMEM((24, LANES), F32)],
        compiler_params=params(8),
    )(got.reshape(members, LANES), b_t, u0e, u1e, u2e, g1e, g2e, g3, *strips)
    return pressure.reshape(nz, nx, ny), true_residual.reshape(nz, nx, ny)


def solution(mesh):
    field = P(None, "gx", "gy")
    return jax.shard_map(
        on_device,
        mesh=mesh,
        in_specs=(field, P(), P(), P()),
        out_specs=(field, field),
        check_vma=False,
    )
```

time: 59.7 us -> 54 us (0.905)
  Pallas kernels: 20.6 us -> 13.2 us
  waiting for transfers between devices: 0.01 us -> 1.05 us
    pallas_call x3, Pallas kernels: 13.3 us -> 7.47 us  [the longest x1 4.86 us: on_device(): pl.pallas_call(part(main_kernel, nz, nx), in_specs=[spec()] * 8, out_spec...]
    ppermute x4, waiting for transfers between devices: 0.01 us -> 1.05 us  [neighbours(): lax.ppermute(array, axes, pairs if up else [(b, a) for a, b in pairs])]
    pallas_call x1, Pallas kernels: 0.83 us -> 0.19 us  [on_device(): pl.pallas_call(part(pack_kernel, nz, nx), in_specs=[spec()] * 4, out_spec...]
    unnamed x10 -> x8, local copies, waits for them, and re-layouts: 2.24 us -> 2.24 us
  transfers between devices with their start and end apart: 4 -> 4, of which waited for: 0 -> 1; matrix products, arithmetic and copies ran while one was open for 0% -> 0% of each run, Pallas kernels for 19% -> 14%
where the time goes in v3:
time: 54 us; the launch traced here: 53.9 us
  blocking collectives  25.9 us (48%)
  Pallas kernels  13.2 us (24%)
  starting transfers between devices  10.8 us (20%)
  local copies, waits for them, and re-layouts  2.24 us (4%)
  waiting for transfers between devices  1.05 us (2%)
  between operations  0.7 us (1%)
    all_to_all x1, blocking collectives, on_device(): lax.all_to_all(send.reshape(members, 1, LANES), (gx, gy), split_axis=0, c...  25.9 us
    ppermute x4, starting transfers between devices, neighbours(): lax.ppermute(array, axes, pairs if up else [(b, a) for a, b in pairs])  10.8 us
    pallas_call x1, Pallas kernels, on_device(): pl.pallas_call(part(main_kernel, nz, nx), in_specs=[spec()] * 8, out_spec...  4.86 us
    pallas_call x1, Pallas kernels, on_device(): pl.pallas_call(part(combine_kernel, nz, nx, kz), grid=(nz // kz,), in_spe...  3.11 us
    pallas_call x1, Pallas kernels, on_device(): pl.pallas_call(part(own_kernel, nz, nx), in_specs=[spec()] * 3, out_specs...  2.44 us
    pallas_call x1, Pallas kernels, on_device(): pl.pallas_call(part(strip_kernel, nz, nx, members), in_specs=[spec()] * 9...  2.41 us
    unnamed x8, local copies, waits for them, and re-layouts  2.24 us
  transfers between devices with their start and end apart: 4, of which 1 were waited for; matrix products, arithmetic and copies ran while one was open for 0% of the time, Pallas kernels for 14%

profile of v3, /device:TPU:1, one launch (start us, length us, event | category | flops | bytes accessed | tf_op | source)
XLA Modules:
  0.0 53.9 jit_solution(4017409806765141888)
XLA Ops:
  0.6 0.0 copy-start.3
  0.6 0.0 copy-start
  0.6 1.3 %copy-done = f32[160,16,128]{2,1,0:T(8,128)S(1)} copy-done((f32[160,16,128]{2,1,0:T(8,128)S(1)}, f32[160,16,128]{2,1,0:T(8,128)}, u32[]{:S(2)}) %copy-start) | copy-done | bytes 1310744
  2.0 0.0 copy-start.2
  2.0 0.9 %copy-done.2 = f32[160,160]{1,0:T(8,128)S(1)} copy-done((f32[160,160]{1,0:T(8,128)S(1)}, f32[160,160]{1,0:T(8,128)}, u32[]{:S(2)}) %copy-start.2) | copy-done | bytes 102424
  2.9 0.0 copy-start.1
  2.9 0.2 shard_map.50
  3.1 2.1 %collective-permute-start = (f32[480,128]{1,0:T(8,128)S(1)}, f32[480,128]{1,0:T(8,128)S(1)}, u32[]{:S(2)}, u32[]{:S(2)}) collective-permute-start(f32[480,128]{1,0:T(8,128)S(1)} %get-tuple-element.35), channel_id=1, source_target_pairs={{0,16},{16,32},{32,48},{48,64},{64,80},{80,96},{96,112},{112,128},... | collective-permute-start | bytes 737288 | tf_op jit(solution)/shard_map/ppermute | solution.py:324
  5.2 3.8 %collective-permute-start.1 = (f32[480,128]{1,0:T(8,128)S(1)}, f32[480,128]{1,0:T(8,128)S(1)}, u32[]{:S(2)}, u32[]{:S(2)}) collective-permute-start(f32[480,128]{1,0:T(8,128)S(1)} %get-tuple-element.36), channel_id=1, source_target_pairs={{16,0},{32,16},{48,32},{64,48},{80,64},{96,80},{112,96},{128,112},... | collective-permute-start | bytes 737288 | tf_op jit(solution)/shard_map/ppermute | solution.py:324
  9.0 0.0 copy-done.3
  9.0 0.0 copy-done.1
  9.0 2.4 %shard_map.51 = (f32[2560,128]{1,0:T(8,128)S(1)}, f32[2560,128]{1,0:T(8,128)S(1)}, f32[160,128]{1,0:T(8,128)S(1)}, f32[320,128]{1,0:T(8,128)S(1)}, f32[320,128]{...) custom-call(f32[2560,128]{1,0:T(8,128)S(1)} %bitcast.9, ...), custom_call_target="tpu_custom_call" | custom-call | flops 629145600 | bytes 1048576 | tf_op jit(solution)/shard_map/pallas_call | solution.py:342
  11.5 1.0 %collective-permute-done.refs_2_ = f32[480,128]{1,0:T(8,128)S(1)} collective-permute-done((f32[480,128]{1,0:T(8,128)S(1)}, f32[480,128]{1,0:T(8,128)S(1)}, u32[]{:S(2)}, u32[]{:S(2)}) %collective-permute-start) | collective-permute-done | bytes 245792 | tf_op jit(solution)/shard_map/ppermute | solution.py:324
  12.5 0.0 collective-permute-done.1.refs_3_
  12.5 0.2 shard_map.52
  12.7 3.4 %collective-permute-start.3 = (f32[320,128]{1,0:T(8,128)S(1)}, f32[320,128]{1,0:T(8,128)S(1)}, u32[]{:S(2)}, u32[]{:S(2)}) collective-permute-start(f32[320,128]{1,0:T(8,128)S(1)} %get-tuple-element.37.refs_0_), channel_id=1, source_target_pairs={{1,0},{2,1},{3,2},{4,3},{5,4},{6,5},{7,6},{8,7},{9,8},{10,9},{11,1... | collective-permute-start | bytes 491528 | tf_op jit(solution)/shard_map/ppermute | solution.py:324
  16.1 1.5 %collective-permute-start.2 = (f32[320,128]{1,0:T(8,128)S(1)}, f32[320,128]{1,0:T(8,128)S(1)}, u32[]{:S(2)}, u32[]{:S(2)}) collective-permute-start(f32[320,128]{1,0:T(8,128)S(1)} %get-tuple-element.37.refs_0_), channel_id=1, source_target_pairs={{0,1},{1,2},{2,3},{3,4},{4,5},{5,6},{6,7},{7,8},{8,9},{9,10},{10,1... | collective-permute-start | bytes 491528 | tf_op jit(solution)/shard_map/ppermute | solution.py:324
  17.6 4.9 %shard_map.53 = (f32[3520,128]{1,0:T(8,128)S(1)}, f32[3200,128]{1,0:T(8,128)S(1)}, f32[2880,128]{1,0:T(8,128)S(1)}, f32[3200,128]{1,0:T(8,128)S(1)}, f32[2880,12...) custom-call(f32[2560,128]{1,0:T(8,128)S(1)} %get-tuple-element.40.refs_0_.refs_1_, ...), custom_call_target="tpu_custom_call" | custom-call | flops 1887436800 | bytes 1048576 | tf_op jit(solution)/shard_map/pallas_call | solution.py:360
  22.4 0.0 collective-permute-done.3.refs_3_
  22.5 0.0 collective-permute-done.2.refs_2_
  22.5 2.4 %shard_map.54 = (f32[640,128]{1,0:T(8,128)S(1)}, f32[640,128]{1,0:T(8,128)S(1)}, f32[640,128]{1,0:T(8,128)S(1)}, f32[640,128]{1,0:T(8,128)S(1)}, f32[640,128]{1,...) custom-call(f32[320,128]{1,0:T(8,128)S(1)} %get-tuple-element.37.refs_0_, ...), custom_call_target="tpu_custom_call" | custom-call | tf_op jit(solution)/shard_map/pallas_call | solution.py:368
  24.9 25.9 %all_to_all.5 = f32[256,1,128]{2,1,0:T(1,128)S(1)} all-to-all(f32[256,1,128]{2,1,0:T(1,128)S(1)} %bitcast.11), channel_id=1, replica_groups=mesh['gx'=16,'gy'=16] {'gx','gy'}, dimensions={0} | all-to-all | bytes 262144 | tf_op jit(solution)/shard_map/all_to_all | solution.py:375
  50.8 3.1 %shard_map.55 = (f32[2560,128]{1,0:T(8,128)}, f32[2560,128]{1,0:T(8,128)}) custom-call(f32[256,128]{1,0:T(8,128)S(1)} %bitcast.10, f32[2560,128]{1,0:T(8,128)S(1)} %get-tuple-element.40.refs_0_.refs_1_, f32[3520,128]{1,0:T(8,128)S(1)} %get-tuple-element.47.refs_2_, f32[3200,128]{1,0:T(8,128)S(1)} %get-tuple-element.48.refs_3_, ...), custom_call_target="tpu_custom_call" | custom-call | tf_op jit(solution)/shard_map/pallas_call | solution.py:377
Async XLA Ops:
  0.6 8.4 %copy-start.3 = (f32[160]{0:T(256)S(1)}, f32[160]{0:T(256)}, u32[]{:S(2)}) copy-start(f32[160]{0:T(256)} %param.5) | copy-start | bytes 1924
  0.6 1.3 %copy-start = (f32[160,16,128]{2,1,0:T(8,128)S(1)}, f32[160,16,128]{2,1,0:T(8,128)}, u32[]{:S(2)}) copy-start(f32[160,16,128]{2,1,0:T(8,128)} %param.4) | copy-start | bytes 3932164
  2.0 0.9 %copy-start.2 = (f32[160,160]{1,0:T(8,128)S(1)}, f32[160,160]{1,0:T(8,128)}, u32[]{:S(2)}) copy-start(f32[160,160]{1,0:T(8,128)} %refs_1_.1) | copy-start | bytes 307204
  2.9 6.1 %copy-start.1 = (f32[160,16,128]{2,1,0:T(8,128)S(1)}, f32[160,16,128]{2,1,0:T(8,128)}, u32[]{:S(2)}) copy-start(f32[160,16,128]{2,1,0:T(8,128)} %param.4) | copy-start | bytes 3932164
  3.1 9.4 %collective-permute-start = (f32[480,128]{1,0:T(8,128)S(1)}, f32[480,128]{1,0:T(8,128)S(1)}, u32[]{:S(2)}, u32[]{:S(2)}) collective-permute-start(f32[480,128]{1,0:T(8,128)S(1)} %get-tuple-element.35), channel_id=1, source_target_pairs={{0,16},{16,32},{32,48},{48,64},{64,80},{80,96},{96,112},{112,128},... | collective-permute-start | bytes 737288 | tf_op jit(solution)/shard_map/ppermute | solution.py:324
  5.2 7.3 %collective-permute-start.1 = (f32[480,128]{1,0:T(8,128)S(1)}, f32[480,128]{1,0:T(8,128)S(1)}, u32[]{:S(2)}, u32[]{:S(2)}) collective-permute-start(f32[480,128]{1,0:T(8,128)S(1)} %get-tuple-element.36), channel_id=1, source_target_pairs={{16,0},{32,16},{48,32},{64,48},{80,64},{96,80},{112,96},{128,112},... | collective-permute-start | bytes 737288 | tf_op jit(solution)/shard_map/ppermute | solution.py:324
  12.7 9.8 %collective-permute-start.3 = (f32[320,128]{1,0:T(8,128)S(1)}, f32[320,128]{1,0:T(8,128)S(1)}, u32[]{:S(2)}, u32[]{:S(2)}) collective-permute-start(f32[320,128]{1,0:T(8,128)S(1)} %get-tuple-element.37.refs_0_), channel_id=1, source_target_pairs={{1,0},{2,1},{3,2},{4,3},{5,4},{6,5},{7,6},{8,7},{9,8},{10,9},{11,1... | collective-permute-start | bytes 491528 | tf_op jit(solution)/shard_map/ppermute | solution.py:324
  16.1 6.4 %collective-permute-start.2 = (f32[320,128]{1,0:T(8,128)S(1)}, f32[320,128]{1,0:T(8,128)S(1)}, u32[]{:S(2)}, u32[]{:S(2)}) collective-permute-start(f32[320,128]{1,0:T(8,128)S(1)} %get-tuple-element.37.refs_0_), channel_id=1, source_target_pairs={{0,1},{1,2},{2,3},{3,4},{4,5},{5,6},{6,7},{7,8},{8,9},{9,10},{10,1... | collective-permute-start | bytes 491528 | tf_op jit(solution)/shard_map/ppermute | solution.py:324

commit v4 on v3

--- a/solution.py
+++ b/solution.py
@@ -12,6 +12,8 @@
 GROUP = 9
 STEPS = 3
 WIDTH = 4
+WIDE = 3
+BLOCK = 32
 
 
 def vmem(rows, cols=LANES):
@@ -57,8 +59,7 @@
             dst[(first + t) * nz : (first + t + 1) * nz, :] = out[:, t * LANES : (t + 1) * LANES]
 
 
-def load_kernel(nz, nx, nat, inv, low, high, inv_out):
-    inv_out[...] = inv[...]
+def load_kernel(nz, nx, nat, low, high):
     for i in range(STEPS):
         low[i * nz : (i + 1) * nz, :] = nat[pl.ds(i, nz, stride=nx), :]
         high[i * nz : (i + 1) * nz, :] = nat[pl.ds(nx - STEPS + i, nz, stride=nx), :]
@@ -159,19 +160,30 @@
     return out
 
 
-def advance(factors, neighbours_of, g, u, h_ref, nz, count, width, visit, tile=8):
-    for first in range(0, count, width):
+class Field:
+    def __init__(self, nz, *places):
+        self.nz = nz
+        self.where = {x: (ref, i) for ref, xs in places for i, x in enumerate(xs)}
+
+    def at(self, x, k, size=8):
+        ref, i = self.where[x]
+        return ref[i * self.nz + k : i * self.nz + k + size, :]
+
+
+def advance(factors, xs, u_last, around, g, u, h_ref, width, visit, tile=8):
+    nz = u_last.nz
+    for first in range(0, len(xs), width):
         rows = []
-        for j in range(first, min(first + width, count)):
+        for i, x in enumerate(xs[first : first + width], first):
             parts, terms = [], []
             for k in range(0, nz, tile):
-                parts.append(h_ref[k : k + tile, :] * neighbours_of(j, k))
-                found = visit(j, k, parts[-1])
+                parts.append(h_ref[k : k + tile, :] * around(u_last, x, k))
+                found = visit(x, k, parts[-1])
                 if found:
                     terms.append(found)
-            visit.finish(j, terms)
+            visit.finish(x, terms)
             rows.append(jnp.concatenate(parts, axis=0))
-            g[j * nz : (j + 1) * nz, :] = rows[-1]
+            g[i * nz : (i + 1) * nz, :] = rows[-1]
         if u is None:
             continue
         out = product(factors, jnp.concatenate(rows, axis=1) if len(rows) > 1 else rows[0])
@@ -179,47 +191,77 @@
             u[(first + t) * nz : (first + t + 1) * nz, :] = out[:, t * LANES : (t + 1) * LANES]
 
 
+def five_points(v, x, k):
+    return (v.at(x - 1, k) + v.at(x + 1, k)) + sideways(v.at(x, k))
+
+
+def packed_points(v, x, k):
+    mid = v.at(x, k)
+    return sideways(mid) + sideways(mid, GROUP)
+
+
 class Visit:
-    def __init__(self, level, nz, fields, rows, sums_of):
-        self.level, self.nz, self.fields, self.rows, self.sums_of = level, nz, fields, rows, sums_of
-
-    def __call__(self, j, k, g):
-        x = self.rows(j)
-        if x is None:
+    def __init__(self, level, fields, mine, sums_of):
+        self.level, self.fields, self.mine, self.sums_of = level, fields, mine, sums_of
+
+    def __call__(self, x, k, g):
+        if x not in self.mine:
             return None
-        b, *gs, v = (ref[(x + skip) * self.nz + k : (x + skip) * self.nz + k + 8, :] for ref, skip in self.fields)
+        b, *gs, v = (field.at(x, k) for field in self.fields)
         return stage_terms(self.level, b, (*gs, g), v)
 
-    def finish(self, j, terms):
+    def finish(self, x, terms):
         if terms:
-            self.sums_of(j).add(terms)
-
-
-def main_kernel(nz, nx, b_t, u0, below, above, h_wide, f0, f1, f2, u0e, u1e, u2e, g1e, g2e, g3, sums_out):
-    u0e[STEPS * nz : (STEPS + nx) * nz, :] = u0[...]
-    factors = (f0, f1, f2)
-    for ref, first in ((below, 0), (above, STEPS + nx)):
-        apply_inverse(factors, ref, u0e.at[pl.ds(first * nz, STEPS * nz), :], nz, STEPS, STEPS)
-    sums = Sums()
-
-    def around(v):
-        def of(j, k):
-            at = lambda r: v[r * nz + k : r * nz + k + 8, :]
-            return (at(j) + at(j + 2)) + sideways(at(j + 1))
-
-        return of
-
-    inside = lambda extra: (lambda j: j - extra if 0 <= j - extra < nx else None)
-    b_f, f1_f, f2_f = (b_t, 0), (g1e, 2), (g2e, 1)
-    one = Visit(0, nz, (b_f, (u0e, 3)), inside(2), lambda j: sums)
-    advance(factors, around(u0e), g1e, u1e, h_wide, nz, nx + 4, WIDTH, one)
-    two = Visit(1, nz, (b_f, f1_f, (u1e, 2)), inside(1), lambda j: sums)
-    advance(factors, around(u1e), g2e, u2e, h_wide, nz, nx + 2, WIDTH, two)
-    three = Visit(2, nz, (b_f, f1_f, f2_f, (u2e, 1)), inside(0), lambda j: sums)
-    advance(factors, around(u2e), g3, None, h_wide, nz, nx, WIDTH, three)
+            self.sums_of(x).add(terms)
+
+
+def inner_rows(nx, level):
+    return list(range(level, nx - level))
+
+
+def outer_rows(nx, level):
+    low = list(range(level - STEPS, level))
+    return low + [nx - 1 - x for x in reversed(low)]
+
+
+def store_sums(sums, out, start=None):
     lane = lane_ids(8)
     for i, name in enumerate(NAMES):
-        sums_out[8 * i : 8 * i + 8, :] = jnp.where((lane >= STEPS) & (lane < LANES - STEPS), sums.total[name], 0.0)
+        at = slice(8 * i, 8 * i + 8)
+        s = jnp.where((lane >= STEPS) & (lane < LANES - STEPS), sums.total[name], 0.0)
+        out[at, :] = s if start is None else start[at, :] + s
+
+
+def inner_kernel(nz, nx, b_t, u0, h_wide, f0, f1, f2, g1i, u1i, g2i, u2i, g3i, sums_out):
+    factors, every, sums = (f0, f1, f2), range(nx), Sums()
+    b, v0 = Field(nz, (b_t, every)), Field(nz, (u0, every))
+    rows = [inner_rows(nx, level) for level in range(STEPS + 1)]
+    v1, v2 = Field(nz, (u1i, rows[1])), Field(nz, (u2i, rows[2]))
+    e1, e2 = Field(nz, (g1i, rows[1])), Field(nz, (g2i, rows[2]))
+    count = lambda level, *fields: Visit(level, fields, every, lambda x: sums)
+    advance(factors, rows[1], v0, five_points, g1i, u1i, h_wide, WIDTH, count(0, b, v0))
+    advance(factors, rows[2], v1, five_points, g2i, u2i, h_wide, WIDTH, count(1, b, e1, v1))
+    advance(factors, rows[3], v2, five_points, g3i, None, h_wide, WIDTH, count(2, b, e1, e2, v2))
+    store_sums(sums, sums_out)
+
+
+def outer_kernel(nz, nx, b_t, u0, below, above, h_wide, f0, f1, f2, g1i, u1i, g2i, u2i, start, *outs):
+    u0x, g1x, u1x, g2x, u2x, g3x, sums_out = outs
+    factors, every, sums = (f0, f1, f2), range(nx), Sums()
+    half = STEPS * nz
+    out = product(factors, jnp.concatenate([ref[i * nz : (i + 1) * nz, :] for ref in (below, above) for i in range(STEPS)], axis=1))
+    for i in range(2 * STEPS):
+        u0x[i * nz : (i + 1) * nz, :] = out[:, i * LANES : (i + 1) * LANES]
+    inner = [inner_rows(nx, level) for level in range(STEPS + 1)]
+    outer = [outer_rows(nx, level) for level in range(STEPS + 1)]
+    both = lambda level, i, x: Field(nz, (i, inner[level]), (x, outer[level]))
+    b, v0, v1, v2 = Field(nz, (b_t, every)), both(0, u0, u0x), both(1, u1i, u1x), both(2, u2i, u2x)
+    e1, e2 = both(1, g1i, g1x), both(2, g2i, g2x)
+    count = lambda level, *fields: Visit(level, fields, every, lambda x: sums)
+    advance(factors, outer[1], v0, five_points, g1x, u1x, h_wide, WIDE, count(0, b, v0))
+    advance(factors, outer[2], v1, five_points, g2x, u2x, h_wide, WIDE, count(1, b, e1, v1))
+    advance(factors, outer[3], v2, five_points, g3x, None, h_wide, WIDE, count(2, b, e1, e2, v2))
+    store_sums(sums, sums_out, start)
 
 
 def strip_kernel(nz, nx, members, inner, outer, left, right, h_wide, sums_in, f0, f1, f2, bs, u0s, u1s, u2s, g1s, g2s, g3s, send):
@@ -231,22 +273,13 @@
         at = slice(t * nz, (t + 1) * nz)
         bs[t * nz : (t + 1) * nz, :] = jnp.where((pos < STEPS) & used, left[at, :], inner[at, :])
         bs[(t + 2) * nz : (t + 3) * nz, :] = jnp.where((pos >= STEPS) & (pos < 2 * STEPS) & used, right[at, :], outer[at, :])
-    near, far = Sums(), Sums()
-    sums_of = lambda j: near if j < 2 else far
-
-    def around(v):
-        def of(j, k):
-            mid = v[j * nz + k : j * nz + k + 8, :]
-            return sideways(mid) + sideways(mid, GROUP)
-
-        return of
-
-    every = lambda j: j
+    near, far, tiles = Sums(), Sums(), list(range(4))
+    field = lambda ref: Field(nz, (ref, tiles))
+    count = lambda level, *refs: Visit(level, [field(ref) for ref in refs], tiles, lambda j: near if j < 2 else far)
     apply_inverse(factors, bs, u0s, nz, 4, 4)
-    advance(factors, around(u0s), g1s, u1s, h_wide, nz, 4, 4, Visit(0, nz, ((bs, 0), (u0s, 0)), every, sums_of))
-    advance(factors, around(u1s), g2s, u2s, h_wide, nz, 4, 4, Visit(1, nz, ((bs, 0), (g1s, 0), (u1s, 0)), every, sums_of))
-    last = Visit(2, nz, ((bs, 0), (g1s, 0), (g2s, 0), (u2s, 0)), every, sums_of)
-    advance(factors, around(u2s), g3s, None, h_wide, nz, 4, 4, last)
+    advance(factors, tiles, field(u0s), packed_points, g1s, u1s, h_wide, 4, count(0, bs, u0s))
+    advance(factors, tiles, field(u1s), packed_points, g2s, u2s, h_wide, 4, count(1, bs, g1s, u1s))
+    advance(factors, tiles, field(u2s), packed_points, g3s, None, h_wide, 4, count(2, bs, g1s, g2s, u2s))
     lane = lane_ids(8)
     pos = place(lane)
     rows = (lane >= GROUP * STEPS) & (lane < GROUP * (STEPS + nx // 2))
@@ -282,40 +315,45 @@
     return m0 / g00 - l1 * c1 - l2 * c2, c1, c2
 
 
-def combine_kernel(nz, nx, kz, *refs):
-    got, fields, strips, outs, coef = refs[0], refs[1:8], refs[8:15], refs[15:17], refs[17]
-    step = pl.program_id(0)
-
-    @pl.when(step == 0)
-    def _():
-        total = jnp.sum(fold(got[...]), axis=0, keepdims=True)
-        line = lax.broadcasted_iota(jnp.int32, (1, LANES), 1)
-        pick = lambda i: jnp.sum(jnp.where(line == i, total, 0.0), axis=1, keepdims=True)
-        for i, c in enumerate(solve_small([pick(i) for i in range(9)])):
-            coef[i * 8 : i * 8 + 8, :] = jnp.broadcast_to(c, (8, LANES))
-
-    c0, c1, c2 = (jnp.concatenate([coef[i * 8 : i * 8 + 8, :]] * (kz // 8), axis=0) for i in range(3))
-    lane = lane_ids(kz)
+def combine_kernel(nz, nx, *refs):
+    got, b_t, u0, inside_refs, outside_refs = refs[0], refs[1], refs[2], refs[3:8], refs[8:14]
+    strips, outs, staged, sems = refs[14:21], refs[21:23], refs[23:25], refs[25]
+    g1i, u1i, g2i, u2i, g3i = inside_refs
+    u0x, g1x, u1x, g2x, u2x, g3x = outside_refs
+    every = range(nx)
+    both = lambda level, i, x: Field(nz, (i, inner_rows(nx, level)), (x, outer_rows(nx, level)))
+    fields = [Field(nz, (b_t, every)), Field(nz, (u0, every)), both(1, u1i, u1x), both(2, u2i, u2x)]
+    fields += [both(1, g1i, g1x), both(2, g2i, g2x), both(3, g3i, g3x)]
+    edges_of = [Field(nz, (ref, range(4))) for ref in strips]
+    total = jnp.sum(fold(got[...]), axis=0, keepdims=True)
+    line = lax.broadcasted_iota(jnp.int32, (1, LANES), 1)
+    pick = lambda i: jnp.sum(jnp.where(line == i, total, 0.0), axis=1, keepdims=True)
+    c0, c1, c2 = (jnp.broadcast_to(c, (8, LANES)) for c in solve_small([pick(i) for i in range(9)]))
+    lane = lane_ids(8)
     inside = (lane >= STEPS) & (lane < LANES - STEPS)
-    pos = place(lane)
+    near_place = place(lane) >= STEPS
 
     def combined(b, v0, v1, v2, f1, f2, f3):
         return c0 * v0 + c1 * v1 + c2 * v2, b - (c0 * (b - f1) + c1 * (f1 - f2) + c2 * (f2 - f3))
 
-    def at(ref, r):
-        return ref[pl.ds(pl.multiple_of(r * nz + step * kz, 8), kz), :]
-
-    edges = []
-    for t in range(2):
-        near, far = combined(*(at(ref, t) for ref in strips)), combined(*(at(ref, t + 2) for ref in strips))
-        edges.append([jnp.where(pos >= STEPS, p, q) for p, q in zip(near, far)])
-    for t, x, group in strip_places(nx):
-        if not t * (nx // 2) <= x < (t + 1) * (nx // 2):
-            continue
-        values = combined(*(at(ref, x + skip) for ref, skip in zip(fields, (0, 3, 2, 1, 2, 1, 0))))
-        for out, value, edge in zip(outs, values, edges[t]):
-            turned = pltpu.roll(edge, (-(GROUP * group + STEPS)) % LANES, 1)
-            out[pl.ds(x, kz, stride=nx), :] = jnp.where(inside, value, turned)
+    copies = []
+    for block in range(nz // BLOCK):
+        for k in range(block * BLOCK, (block + 1) * BLOCK, 8):
+            for t in range(2):
+                near, far = (combined(*(f.at(j, k) for f in edges_of)) for j in (t, t + 2))
+                edges = [jnp.where(near_place, p, q) for p, q in zip(near, far)]
+                for u, x, group in strip_places(nx):
+                    if u != t or not t * (nx // 2) <= x < (t + 1) * (nx // 2):
+                        continue
+                    for ref, value, edge in zip(staged, combined(*(f.at(x, k) for f in fields)), edges):
+                        turned = pltpu.roll(edge, (-(GROUP * group + STEPS)) % LANES, 1)
+                        ref[pl.ds(k * nx + x, 8, stride=nx), :] = jnp.where(inside, value, turned)
+        rows = pl.ds(block * BLOCK * nx, BLOCK * nx)
+        for i in range(2):
+            copies.append(pltpu.make_async_copy(staged[i].at[rows, :], outs[i].at[rows, :], sems.at[i, block]))
+            copies[-1].start()
+    for copy in copies:
+        copy.wait()
 
 
 def neighbours(array, axes, up):
@@ -330,13 +368,13 @@
     members = lax.axis_size(gx) * lax.axis_size(gy)
     part = lambda f, *a: (lambda *refs: f(*a, *refs))
     nat = source_heat.reshape(nz * nx, ny)
-    low, high, inv = pl.pallas_call(
+    low, high = pl.pallas_call(
         part(load_kernel, nz, nx),
-        in_specs=[spec()] * 2,
-        out_specs=[spec()] * 3,
-        out_shape=[vmem(STEPS * nz)] * 2 + [vmem(nz, nz)],
+        in_specs=[spec()],
+        out_specs=[spec()] * 2,
+        out_shape=[vmem(STEPS * nz)] * 2,
         compiler_params=params(4),
-    )(nat, column_inverse)
+    )(nat)
     below = neighbours(high, gx, True)
     above = neighbours(low, gx, False)
     b_t, u0, h_wide, inner_own, outer_own, *factors = pl.pallas_call(
@@ -347,7 +385,15 @@
         + [pltpu.VMEM((nz, count * nz), BF16) for count in (3, 2, 1)],
         compiler_params=params(8),
         cost_estimate=cost(12 * nz * nz * nx * ny, 1 << 20),
-    )(nat, horiz_coef.reshape(1, nz), inv)
+    )(nat, horiz_coef.reshape(1, nz), column_inverse)
+    *inside, start = pl.pallas_call(
+        part(inner_kernel, nz, nx),
+        in_specs=[spec()] * 6,
+        out_specs=[spec()] * 6,
+        out_shape=[vmem(r * nz) for r in (nx - 2, nx - 2, nx - 4, nx - 4, nx - 6)] + [vmem(72)],
+        compiler_params=params(8),
+        cost_estimate=cost(24 * nz * nz * nx * ny, 1 << 20),
+    )(b_t, u0, h_wide, *factors)
     inner, outer = pl.pallas_call(
         part(pack_kernel, nz, nx),
         in_specs=[spec()] * 4,
@@ -357,14 +403,14 @@
     )(inner_own, outer_own, below, above)
     from_left = neighbours(inner, gy, True)
     from_right = neighbours(inner, gy, False)
-    u0e, u1e, u2e, g1e, g2e, g3, sums = pl.pallas_call(
-        part(main_kernel, nz, nx),
-        in_specs=[spec()] * 8,
+    *outside, sums = pl.pallas_call(
+        part(outer_kernel, nz, nx),
+        in_specs=[spec()] * 13,
         out_specs=[spec()] * 7,
-        out_shape=[vmem(r * nz) for r in (nx + 6, nx + 4, nx + 2, nx + 4, nx + 2, nx)] + [vmem(72)],
-        compiler_params=params(12),
-        cost_estimate=cost(36 * nz * nz * nx * ny, 1 << 20),
-    )(b_t, u0, below, above, h_wide, *factors)
+        out_shape=[vmem(2 * STEPS * nz)] * 6 + [vmem(72)],
+        compiler_params=params(8),
+        cost_estimate=cost(36 * nz * nz * 6 * ny, 1 << 20),
+    )(b_t, u0, below, above, h_wide, *factors, *inside[:4], start)
     *strips, send = pl.pallas_call(
         part(strip_kernel, nz, nx, members),
         in_specs=[spec()] * 9,
@@ -373,16 +419,14 @@
         compiler_params=params(8),
     )(inner, outer, from_left, from_right, h_wide, sums, *factors)
     got = lax.all_to_all(send.reshape(members, 1, LANES), (gx, gy), split_axis=0, concat_axis=0, tiled=True)
-    kz = 80
     pressure, true_residual = pl.pallas_call(
-        part(combine_kernel, nz, nx, kz),
-        grid=(nz // kz,),
-        in_specs=[spec()] * 15,
-        out_specs=[pl.BlockSpec((kz * nx, ny), lambda i: (i, 0))] * 2,
+        part(combine_kernel, nz, nx),
+        in_specs=[spec()] * 21,
+        out_specs=[pl.BlockSpec(memory_space=pltpu.HBM)] * 2,
         out_shape=[jax.ShapeDtypeStruct((nz * nx, ny), F32)] * 2,
-        scratch_shapes=[pltpu.VMEM((24, LANES), F32)],
+        scratch_shapes=[pltpu.VMEM((nz * nx, ny), F32)] * 2 + [pltpu.SemaphoreType.DMA((2, nz // BLOCK))],
         compiler_params=params(8),
-    )(got.reshape(members, LANES), b_t, u0e, u1e, u2e, g1e, g2e, g3, *strips)
+    )(got.reshape(members, LANES), b_t, u0, *inside, *outside, *strips)
     return pressure.reshape(nz, nx, ny), true_residual.reshape(nz, nx, ny)
 
 

time: 54 us -> 52.4 us (0.970)
  waiting for transfers between devices: 1.05 us -> 0.09 us
    ppermute x4, waiting for transfers between devices: 1.05 us -> 0.09 us  [neighbours(): lax.ppermute(array, axes, pairs if up else [(b, a) for a, b in pairs])]
    pallas_call x3 -> x4, Pallas kernels: 8.17 us -> 7.63 us  [the longest x1 2.94 us: on_device(): pl.pallas_call(part(inner_kernel, nz, nx), in_specs=[spec()] * 6, out_spe...]
where the time goes in v4:
time: 52.4 us; the launch traced here: 52.3 us
  blocking collectives  25.7 us (49%)
  Pallas kernels  12.7 us (24%)
  starting transfers between devices  10.8 us (21%)
  local copies, waits for them, and re-layouts  2.24 us (4%)
  between operations  0.7 us (1%)
    all_to_all x1, blocking collectives, on_device(): lax.all_to_all(send.reshape(members, 1, LANES), (gx, gy), split_axis=0, c...  25.7 us
    ppermute x4, starting transfers between devices, neighbours(): lax.ppermute(array, axes, pairs if up else [(b, a) for a, b in pairs])  10.8 us
    pallas_call x1, Pallas kernels, on_device(): pl.pallas_call(part(inner_kernel, nz, nx), in_specs=[spec()] * 6, out_spe...  2.94 us
    pallas_call x1, Pallas kernels, on_device(): pl.pallas_call(part(own_kernel, nz, nx), in_specs=[spec()] * 3, out_specs...  2.48 us
    pallas_call x1, Pallas kernels, on_device(): pl.pallas_call(part(strip_kernel, nz, nx, members), in_specs=[spec()] * 9...  2.42 us
    pallas_call x1, Pallas kernels, on_device(): pl.pallas_call(part(combine_kernel, nz, nx), in_specs=[spec()] * 21, out_...  2.41 us
    unnamed x8, local copies, waits for them, and re-layouts  2.24 us
    pallas_call x1, Pallas kernels, on_device(): pl.pallas_call(part(outer_kernel, nz, nx), in_specs=[spec()] * 13, out_sp...  2.09 us
  transfers between devices with their start and end apart: 4, of which 1 were waited for; matrix products, arithmetic and copies ran while one was open for 0% of the time, Pallas kernels for 14%

profile of v4, /device:TPU:1, one launch (start us, length us, event | category | flops | bytes accessed | tf_op | source)
XLA Modules:
  0.0 52.3 jit_solution(5165333628347227933)
XLA Ops:
  0.6 0.0 copy-start.3
  0.6 0.0 copy-start
  0.6 1.3 %copy-done = f32[160,16,128]{2,1,0:T(8,128)S(1)} copy-done((f32[160,16,128]{2,1,0:T(8,128)S(1)}, f32[160,16,128]{2,1,0:T(8,128)}, u32[]{:S(2)}) %copy-start) | copy-done | bytes 1310744
  2.0 0.0 copy-start.1
  2.0 0.2 shard_map.51
  2.2 2.1 %collective-permute-start = (f32[480,128]{1,0:T(8,128)S(1)}, f32[480,128]{1,0:T(8,128)S(1)}, u32[]{:S(2)}, u32[]{:S(2)}) collective-permute-start(f32[480,128]{1,0:T(8,128)S(1)} %get-tuple-element.39), channel_id=1, source_target_pairs={{0,16},{16,32},{32,48},{48,64},{64,80},{80,96},{96,112},{112,128},... | collective-permute-start | bytes 737288 | tf_op jit(solution)/shard_map/ppermute | solution.py:362
  4.3 3.8 %collective-permute-start.1 = (f32[480,128]{1,0:T(8,128)S(1)}, f32[480,128]{1,0:T(8,128)S(1)}, u32[]{:S(2)}, u32[]{:S(2)}) collective-permute-start(f32[480,128]{1,0:T(8,128)S(1)} %get-tuple-element.40), channel_id=1, source_target_pairs={{16,0},{32,16},{48,32},{64,48},{80,64},{96,80},{112,96},{128,112},... | collective-permute-start | bytes 737288 | tf_op jit(solution)/shard_map/ppermute | solution.py:362
  8.1 0.0 copy-done.3
  8.1 0.0 copy-done.1
  8.1 0.0 copy-start.2
  8.1 0.9 %copy-done.2 = f32[160,160]{1,0:T(8,128)S(1)} copy-done((f32[160,160]{1,0:T(8,128)S(1)}, f32[160,160]{1,0:T(8,128)}, u32[]{:S(2)}) %copy-start.2) | copy-done | bytes 102424
  9.0 2.5 %shard_map.50 = (f32[2560,128]{1,0:T(8,128)S(1)}, f32[2560,128]{1,0:T(8,128)S(1)}, f32[160,128]{1,0:T(8,128)S(1)}, f32[320,128]{1,0:T(8,128)S(1)}, f32[320,128]{...) custom-call(f32[2560,128]{1,0:T(8,128)S(1)} %bitcast.9, ...), custom_call_target="tpu_custom_call" | custom-call | flops 629145600 | bytes 1048576 | tf_op jit(solution)/shard_map/pallas_call | solution.py:380
  11.5 0.1 collective-permute-done.refs_2_
  11.6 0.0 collective-permute-done.1.refs_3_
  11.6 0.2 shard_map.52
  11.8 3.4 %collective-permute-start.3 = (f32[320,128]{1,0:T(8,128)S(1)}, f32[320,128]{1,0:T(8,128)S(1)}, u32[]{:S(2)}, u32[]{:S(2)}) collective-permute-start(f32[320,128]{1,0:T(8,128)S(1)} %get-tuple-element.41.refs_0_), channel_id=1, source_target_pairs={{1,0},{2,1},{3,2},{4,3},{5,4},{6,5},{7,6},{8,7},{9,8},{10,9},{11,1... | collective-permute-start | bytes 491528 | tf_op jit(solution)/shard_map/ppermute | solution.py:362
  15.2 1.5 %collective-permute-start.2 = (f32[320,128]{1,0:T(8,128)S(1)}, f32[320,128]{1,0:T(8,128)S(1)}, u32[]{:S(2)}, u32[]{:S(2)}) collective-permute-start(f32[320,128]{1,0:T(8,128)S(1)} %get-tuple-element.41.refs_0_), channel_id=1, source_target_pairs={{0,1},{1,2},{2,3},{3,4},{4,5},{5,6},{6,7},{7,8},{8,9},{9,10},{10,1... | collective-permute-start | bytes 491528 | tf_op jit(solution)/shard_map/ppermute | solution.py:362
  16.7 2.9 %shard_map.53 = (f32[2240,128]{1,0:T(8,128)S(1)}, f32[2240,128]{1,0:T(8,128)S(1)}, f32[1920,128]{1,0:T(8,128)S(1)}, f32[1920,128]{1,0:T(8,128)S(1)}, f32[1600,128]{1,0:T(8,128)S(1)}, /*index=5*/f32[72,128]{1,0:T(8,128)S(1)}) custom-call(f32[2560,128]{1,0:T(8,128)S(1)} %get-tuple-element.44.refs_0_.refs_1_, ...), custom_call_target="tpu_custom_call" | custom-call | flops 1258291200 | bytes 1048576 | tf_op jit(solution)/shard_map/pallas_call | solution.py:389
  19.6 2.1 %shard_map.54 = (f32[960,128]{1,0:T(8,128)S(1)}, f32[960,128]{1,0:T(8,128)S(1)}, f32[960,128]{1,0:T(8,128)S(1)}, f32[960,128]{1,0:T(8,128)S(1)}, f32[960,128]{1,...) custom-call(f32[2560,128]{1,0:T(8,128)S(1)} %get-tuple-element.44.refs_0_.refs_1_, ...), custom_call_target="tpu_custom_call" | custom-call | flops 707788800 | bytes 1048576 | tf_op jit(solution)/shard_map/pallas_call | solution.py:406
  21.7 0.0 collective-permute-done.3.refs_3_
  21.7 0.0 collective-permute-done.2.refs_2_
  21.7 2.4 %shard_map.55 = (f32[640,128]{1,0:T(8,128)S(1)}, f32[640,128]{1,0:T(8,128)S(1)}, f32[640,128]{1,0:T(8,128)S(1)}, f32[640,128]{1,0:T(8,128)S(1)}, f32[640,128]{1,...) custom-call(f32[320,128]{1,0:T(8,128)S(1)} %get-tuple-element.41.refs_0_, ...), custom_call_target="tpu_custom_call" | custom-call | tf_op jit(solution)/shard_map/pallas_call | solution.py:414
  24.1 25.7 %all_to_all.5 = f32[256,1,128]{2,1,0:T(1,128)S(1)} all-to-all(f32[256,1,128]{2,1,0:T(1,128)S(1)} %bitcast.11), channel_id=1, replica_groups=mesh['gx'=16,'gy'=16] {'gx','gy'}, dimensions={0} | all-to-all | bytes 262144 | tf_op jit(solution)/shard_map/all_to_all | solution.py:421
  49.9 2.4 %shard_map.56 = (f32[2560,128]{1,0:T(8,128)}, f32[2560,128]{1,0:T(8,128)}) custom-call(f32[256,128]{1,0:T(8,128)S(1)} %bitcast.10, f32[2560,128]{1,0:T(8,128)S(1)} %get-tuple-element.44.refs_0_.refs_1_, f32[2560,128]{1,0:T(8,128)S(1)} %get-tuple-element.45.refs_1_.refs_2_, f32[2240,128]{1,0:T(8,128)S(1)} %get-tuple-element.49.refs_8_.refs_3_, ...), custom_call_target="tpu_custom_call" | custom-call | tf_op jit(solution)/shard_map/pallas_call | solution.py:422
Async XLA Ops:
  0.6 7.4 %copy-start.3 = (f32[160]{0:T(256)S(1)}, f32[160]{0:T(256)}, u32[]{:S(2)}) copy-start(f32[160]{0:T(256)} %param.5) | copy-start | bytes 1924
  0.6 1.3 %copy-start = (f32[160,16,128]{2,1,0:T(8,128)S(1)}, f32[160,16,128]{2,1,0:T(8,128)}, u32[]{:S(2)}) copy-start(f32[160,16,128]{2,1,0:T(8,128)} %param.4) | copy-start | bytes 3932164
  2.0 6.1 %copy-start.1 = (f32[160,16,128]{2,1,0:T(8,128)S(1)}, f32[160,16,128]{2,1,0:T(8,128)}, u32[]{:S(2)}) copy-start(f32[160,16,128]{2,1,0:T(8,128)} %param.4) | copy-start | bytes 3932164
  2.2 9.4 %collective-permute-start = (f32[480,128]{1,0:T(8,128)S(1)}, f32[480,128]{1,0:T(8,128)S(1)}, u32[]{:S(2)}, u32[]{:S(2)}) collective-permute-start(f32[480,128]{1,0:T(8,128)S(1)} %get-tuple-element.39), channel_id=1, source_target_pairs={{0,16},{16,32},{32,48},{48,64},{64,80},{80,96},{96,112},{112,128},... | collective-permute-start | bytes 737288 | tf_op jit(solution)/shard_map/ppermute | solution.py:362
  4.3 7.3 %collective-permute-start.1 = (f32[480,128]{1,0:T(8,128)S(1)}, f32[480,128]{1,0:T(8,128)S(1)}, u32[]{:S(2)}, u32[]{:S(2)}) collective-permute-start(f32[480,128]{1,0:T(8,128)S(1)} %get-tuple-element.40), channel_id=1, source_target_pairs={{16,0},{32,16},{48,32},{64,48},{80,64},{96,80},{112,96},{128,112},... | collective-permute-start | bytes 737288 | tf_op jit(solution)/shard_map/ppermute | solution.py:362
  8.1 0.9 %copy-start.2 = (f32[160,160]{1,0:T(8,128)S(1)}, f32[160,160]{1,0:T(8,128)}, u32[]{:S(2)}) copy-start(f32[160,160]{1,0:T(8,128)} %refs_2_.1) | copy-start | bytes 307204
  11.8 9.9 %collective-permute-start.3 = (f32[320,128]{1,0:T(8,128)S(1)}, f32[320,128]{1,0:T(8,128)S(1)}, u32[]{:S(2)}, u32[]{:S(2)}) collective-permute-start(f32[320,128]{1,0:T(8,128)S(1)} %get-tuple-element.41.refs_0_), channel_id=1, source_target_pairs={{1,0},{2,1},{3,2},{4,3},{5,4},{6,5},{7,6},{8,7},{9,8},{10,9},{11,1... | collective-permute-start | bytes 491528 | tf_op jit(solution)/shard_map/ppermute | solution.py:362
  15.2 6.5 %collective-permute-start.2 = (f32[320,128]{1,0:T(8,128)S(1)}, f32[320,128]{1,0:T(8,128)S(1)}, u32[]{:S(2)}, u32[]{:S(2)}) collective-permute-start(f32[320,128]{1,0:T(8,128)S(1)} %get-tuple-element.41.refs_0_), channel_id=1, source_target_pairs={{0,1},{1,2},{2,3},{3,4},{4,5},{5,6},{6,7},{7,8},{8,9},{9,10},{10,1... | collective-permute-start | bytes 491528 | tf_op jit(solution)/shard_map/ppermute | solution.py:362

commit v5 on v4

--- a/solution.py
+++ b/solution.py
@@ -108,7 +108,8 @@
     lax.fori_loop(0, nz // tile, body, 0, unroll=4 if fresh else True)
 
 
-def own_kernel(nz, nx, nat, h_row, inv, b_t, u0, h_wide, inner, outer, *factors):
+def own_kernel(nz, nx, nat, h_row, inv, b_t, u0, h_wide, inner, outer, *outs):
+    factors, inside = outs[:3], outs[3:]
     for ref, piece, count in zip(factors, pieces(inv[...]), (3, 2, 1)):
         wide = piece.astype(F32)
         ref[...] = jnp.concatenate([wide] * count, axis=1).astype(BF16) if count > 1 else piece
@@ -120,6 +121,7 @@
     have = lambda x, k: b_t[pl.ds(pl.multiple_of(x * nz + k, 8), 8), :]
     pack_edges((range(nx), have), 0, nx, nz, inner, outer, 8, True)
     apply_inverse(factors, b_t, u0, nz, nx, nx)
+    inner_part(nz, nx, b_t, u0, h_wide, factors, *inside)
 
 
 def pack_kernel(nz, nx, inner_own, outer_own, below, above, inner, outer):
@@ -232,8 +234,8 @@
         out[at, :] = s if start is None else start[at, :] + s
 
 
-def inner_kernel(nz, nx, b_t, u0, h_wide, f0, f1, f2, g1i, u1i, g2i, u2i, g3i, sums_out):
-    factors, every, sums = (f0, f1, f2), range(nx), Sums()
+def inner_part(nz, nx, b_t, u0, h_wide, factors, g1i, u1i, g2i, u2i, g3i, sums_out):
+    every, sums = range(nx), Sums()
     b, v0 = Field(nz, (b_t, every)), Field(nz, (u0, every))
     rows = [inner_rows(nx, level) for level in range(STEPS + 1)]
     v1, v2 = Field(nz, (u1i, rows[1])), Field(nz, (u2i, rows[2]))
@@ -377,23 +379,18 @@
     )(nat)
     below = neighbours(high, gx, True)
     above = neighbours(low, gx, False)
-    b_t, u0, h_wide, inner_own, outer_own, *factors = pl.pallas_call(
+    b_t, u0, h_wide, inner_own, outer_own, *rest = pl.pallas_call(
         part(own_kernel, nz, nx),
         in_specs=[spec()] * 3,
-        out_specs=[spec()] * 8,
+        out_specs=[spec()] * 14,
         out_shape=[vmem(nz * nx), vmem(nz * nx), vmem(nz), vmem(2 * nz), vmem(2 * nz)]
-        + [pltpu.VMEM((nz, count * nz), BF16) for count in (3, 2, 1)],
+        + [pltpu.VMEM((nz, count * nz), BF16) for count in (3, 2, 1)]
+        + [vmem(r * nz) for r in (nx - 2, nx - 2, nx - 4, nx - 4, nx - 6)]
+        + [vmem(72)],
         compiler_params=params(8),
-        cost_estimate=cost(12 * nz * nz * nx * ny, 1 << 20),
+        cost_estimate=cost(36 * nz * nz * nx * ny, 1 << 20),
     )(nat, horiz_coef.reshape(1, nz), column_inverse)
-    *inside, start = pl.pallas_call(
-        part(inner_kernel, nz, nx),
-        in_specs=[spec()] * 6,
-        out_specs=[spec()] * 6,
-        out_shape=[vmem(r * nz) for r in (nx - 2, nx - 2, nx - 4, nx - 4, nx - 6)] + [vmem(72)],
-        compiler_params=params(8),
-        cost_estimate=cost(24 * nz * nz * nx * ny, 1 << 20),
-    )(b_t, u0, h_wide, *factors)
+    factors, inside, start = rest[:3], rest[3:8], rest[8]
     inner, outer = pl.pallas_call(
         part(pack_kernel, nz, nx),
         in_specs=[spec()] * 4,

time: 52.4 us -> 52.4 us (level)
  starting transfers between devices: 10.8 us -> 8.64 us
  waiting for transfers between devices: 0.09 us -> 2.07 us
    pallas_call x1 -> x0, Pallas kernels: 2.94 us -> none  [on_device(): pl.pallas_call(part(inner_kernel, nz, nx), in_specs=[spec()] * 6, out_spe...]
    pallas_call x1, Pallas kernels: 2.48 us -> 5.23 us  [on_device(): pl.pallas_call(part(own_kernel, nz, nx), in_specs=[spec()] * 3, out_specs...]
    ppermute x4, starting transfers between devices: 10.8 us -> 8.64 us  [neighbours(): lax.ppermute(array, axes, pairs if up else [(b, a) for a, b in pairs])]
    ppermute x4, waiting for transfers between devices: 0.09 us -> 2.07 us  [neighbours(): lax.ppermute(array, axes, pairs if up else [(b, a) for a, b in pairs])]
  transfers between devices with their start and end apart: 4 -> 4, of which waited for: 1 -> 2; matrix products, arithmetic and copies ran while one was open for 0% -> 0% of each run, Pallas kernels for 14% -> 14%
where the time goes in v5:
time: 52.4 us; the launch traced here: 52.3 us
  blocking collectives  26.1 us (50%)
  Pallas kernels  12.5 us (24%)
  starting transfers between devices  8.64 us (16%)
  local copies, waits for them, and re-layouts  2.24 us (4%)
  waiting for transfers between devices  2.07 us (4%)
  between operations  0.69 us (1%)
    all_to_all x1, blocking collectives, on_device(): lax.all_to_all(send.reshape(members, 1, LANES), (gx, gy), split_axis=0, c...  26.1 us
    ppermute x4, starting transfers between devices, neighbours(): lax.ppermute(array, axes, pairs if up else [(b, a) for a, b in pairs])  8.64 us
    pallas_call x1, Pallas kernels, on_device(): pl.pallas_call(part(own_kernel, nz, nx), in_specs=[spec()] * 3, out_specs...  5.23 us
    pallas_call x1, Pallas kernels, on_device(): pl.pallas_call(part(strip_kernel, nz, nx, members), in_specs=[spec()] * 9...  2.41 us
    pallas_call x1, Pallas kernels, on_device(): pl.pallas_call(part(combine_kernel, nz, nx), in_specs=[spec()] * 21, out_...  2.41 us
    unnamed x8, local copies, waits for them, and re-layouts  2.24 us
    pallas_call x1, Pallas kernels, on_device(): pl.pallas_call(part(outer_kernel, nz, nx), in_specs=[spec()] * 13, out_sp...  2.08 us
    ppermute x4, waiting for transfers between devices, neighbours(): lax.ppermute(array, axes, pairs if up else [(b, a) for a, b in pairs])  2.07 us
  transfers between devices with their start and end apart: 4, of which 2 were waited for; matrix products, arithmetic and copies ran while one was open for 0% of the time, Pallas kernels for 14%

profile of v5, /device:TPU:1, one launch (start us, length us, event | category | flops | bytes accessed | tf_op | source)
XLA Modules:
  0.0 52.3 jit_solution(13629342770982118073)
XLA Ops:
  0.6 0.0 copy-start.3
  0.6 0.0 copy-start
  0.6 1.3 %copy-done = f32[160,16,128]{2,1,0:T(8,128)S(1)} copy-done((f32[160,16,128]{2,1,0:T(8,128)S(1)}, f32[160,16,128]{2,1,0:T(8,128)}, u32[]{:S(2)}) %copy-start) | copy-done | bytes 1310744
  2.0 0.0 copy-start.1
  2.0 0.2 shard_map.51
  2.2 2.1 %collective-permute-start = (f32[480,128]{1,0:T(8,128)S(1)}, f32[480,128]{1,0:T(8,128)S(1)}, u32[]{:S(2)}, u32[]{:S(2)}) collective-permute-start(f32[480,128]{1,0:T(8,128)S(1)} %get-tuple-element.39), channel_id=1, source_target_pairs={{0,16},{16,32},{32,48},{48,64},{64,80},{80,96},{96,112},{112,128},... | collective-permute-start | bytes 737288 | tf_op jit(solution)/shard_map/ppermute | solution.py:364
  4.3 3.8 %collective-permute-start.1 = (f32[480,128]{1,0:T(8,128)S(1)}, f32[480,128]{1,0:T(8,128)S(1)}, u32[]{:S(2)}, u32[]{:S(2)}) collective-permute-start(f32[480,128]{1,0:T(8,128)S(1)} %get-tuple-element.40), channel_id=1, source_target_pairs={{16,0},{32,16},{48,32},{64,48},{80,64},{96,80},{112,96},{128,112},... | collective-permute-start | bytes 737288 | tf_op jit(solution)/shard_map/ppermute | solution.py:364
  8.1 0.0 copy-done.3
  8.1 0.0 copy-done.1
  8.1 0.0 copy-start.2
  8.1 0.9 %copy-done.2 = f32[160,160]{1,0:T(8,128)S(1)} copy-done((f32[160,160]{1,0:T(8,128)S(1)}, f32[160,160]{1,0:T(8,128)}, u32[]{:S(2)}) %copy-start.2) | copy-done | bytes 102424
  9.0 5.2 %shard_map.50 = (f32[2560,128]{1,0:T(8,128)S(1)}, f32[2560,128]{1,0:T(8,128)S(1)}, f32[160,128]{1,0:T(8,128)S(1)}, f32[320,128]{1,0:T(8,128)S(1)}, f32[320,128]{...) custom-call(f32[2560,128]{1,0:T(8,128)S(1)} %bitcast.9, ...), custom_call_target="tpu_custom_call" | custom-call | flops 1887436800 | bytes 1048576 | tf_op jit(solution)/shard_map/pallas_call | solution.py:382
  14.2 0.0 collective-permute-done.refs_2_
  14.2 0.0 collective-permute-done.1.refs_3_
  14.2 0.2 shard_map.52
  14.4 2.7 %collective-permute-start.3 = (f32[320,128]{1,0:T(8,128)S(1)}, f32[320,128]{1,0:T(8,128)S(1)}, u32[]{:S(2)}, u32[]{:S(2)}) collective-permute-start(f32[320,128]{1,0:T(8,128)S(1)} %get-tuple-element.41.refs_0_), channel_id=1, source_target_pairs={{1,0},{2,1},{3,2},{4,3},{5,4},{6,5},{7,6},{8,7},{9,8},{10,9},{11,1... | collective-permute-start | bytes 491528 | tf_op jit(solution)/shard_map/ppermute | solution.py:364
  17.2 0.0 collective-permute-start.2
  17.2 2.1 %shard_map.53 = (f32[960,128]{1,0:T(8,128)S(1)}, f32[960,128]{1,0:T(8,128)S(1)}, f32[960,128]{1,0:T(8,128)S(1)}, f32[960,128]{1,0:T(8,128)S(1)}, f32[960,128]{1,...) custom-call(f32[2560,128]{1,0:T(8,128)S(1)} %get-tuple-element.44.refs_0_.refs_1_, ...), custom_call_target="tpu_custom_call" | custom-call | flops 707788800 | bytes 1048576 | tf_op jit(solution)/shard_map/pallas_call | solution.py:403
  19.3 0.7 %collective-permute-done.3.refs_3_ = f32[320,128]{1,0:T(8,128)S(1)} collective-permute-done((f32[320,128]{1,0:T(8,128)S(1)}, f32[320,128]{1,0:T(8,128)S(1)}, u32[]{:S(2)}, u32[]{:S(2)}) %collective-permute-start.3) | collective-permute-done | bytes 163872 | tf_op jit(solution)/shard_map/ppermute | solution.py:364
  20.0 1.3 %collective-permute-done.2.refs_2_ = f32[320,128]{1,0:T(8,128)S(1)} collective-permute-done((f32[320,128]{1,0:T(8,128)S(1)}, f32[320,128]{1,0:T(8,128)S(1)}, u32[]{:S(2)}, u32[]{:S(2)}) %collective-permute-start.2) | collective-permute-done | bytes 163872 | tf_op jit(solution)/shard_map/ppermute | solution.py:364
  21.3 2.4 %shard_map.54 = (f32[640,128]{1,0:T(8,128)S(1)}, f32[640,128]{1,0:T(8,128)S(1)}, f32[640,128]{1,0:T(8,128)S(1)}, f32[640,128]{1,0:T(8,128)S(1)}, f32[640,128]{1,...) custom-call(f32[320,128]{1,0:T(8,128)S(1)} %get-tuple-element.41.refs_0_, ...), custom_call_target="tpu_custom_call" | custom-call | tf_op jit(solution)/shard_map/pallas_call | solution.py:411
  23.7 26.1 %all_to_all.5 = f32[256,1,128]{2,1,0:T(1,128)S(1)} all-to-all(f32[256,1,128]{2,1,0:T(1,128)S(1)} %bitcast.11), channel_id=1, replica_groups=mesh['gx'=16,'gy'=16] {'gx','gy'}, dimensions={0} | all-to-all | bytes 262144 | tf_op jit(solution)/shard_map/all_to_all | solution.py:418
  49.8 2.4 %shard_map.55 = (f32[2560,128]{1,0:T(8,128)}, f32[2560,128]{1,0:T(8,128)}) custom-call(f32[256,128]{1,0:T(8,128)S(1)} %bitcast.10, f32[2560,128]{1,0:T(8,128)S(1)} %get-tuple-element.44.refs_0_.refs_1_, f32[2560,128]{1,0:T(8,128)S(1)} %get-tuple-element.45.refs_1_.refs_2_, f32[2240,128]{1,0:T(8,128)S(1)} %get-tuple-element.49.refs_8_.refs_3_, ...), custom_call_target="tpu_custom_call" | custom-call | tf_op jit(solution)/shard_map/pallas_call | solution.py:419
Async XLA Ops:
  0.6 7.4 %copy-start.3 = (f32[160]{0:T(256)S(1)}, f32[160]{0:T(256)}, u32[]{:S(2)}) copy-start(f32[160]{0:T(256)} %param.5) | copy-start | bytes 1924
  0.6 1.3 %copy-start = (f32[160,16,128]{2,1,0:T(8,128)S(1)}, f32[160,16,128]{2,1,0:T(8,128)}, u32[]{:S(2)}) copy-start(f32[160,16,128]{2,1,0:T(8,128)} %param.4) | copy-start | bytes 3932164
  2.0 6.1 %copy-start.1 = (f32[160,16,128]{2,1,0:T(8,128)S(1)}, f32[160,16,128]{2,1,0:T(8,128)}, u32[]{:S(2)}) copy-start(f32[160,16,128]{2,1,0:T(8,128)} %param.4) | copy-start | bytes 3932164
  2.2 12.1 %collective-permute-start = (f32[480,128]{1,0:T(8,128)S(1)}, f32[480,128]{1,0:T(8,128)S(1)}, u32[]{:S(2)}, u32[]{:S(2)}) collective-permute-start(f32[480,128]{1,0:T(8,128)S(1)} %get-tuple-element.39), channel_id=1, source_target_pairs={{0,16},{16,32},{32,48},{48,64},{64,80},{80,96},{96,112},{112,128},... | collective-permute-start | bytes 737288 | tf_op jit(solution)/shard_map/ppermute | solution.py:364
  4.3 10.0 %collective-permute-start.1 = (f32[480,128]{1,0:T(8,128)S(1)}, f32[480,128]{1,0:T(8,128)S(1)}, u32[]{:S(2)}, u32[]{:S(2)}) collective-permute-start(f32[480,128]{1,0:T(8,128)S(1)} %get-tuple-element.40), channel_id=1, source_target_pairs={{16,0},{32,16},{48,32},{64,48},{80,64},{96,80},{112,96},{128,112},... | collective-permute-start | bytes 737288 | tf_op jit(solution)/shard_map/ppermute | solution.py:364
  8.1 0.9 %copy-start.2 = (f32[160,160]{1,0:T(8,128)S(1)}, f32[160,160]{1,0:T(8,128)}, u32[]{:S(2)}) copy-start(f32[160,160]{1,0:T(8,128)} %refs_2_.1) | copy-start | bytes 307204
  14.4 5.5 %collective-permute-start.3 = (f32[320,128]{1,0:T(8,128)S(1)}, f32[320,128]{1,0:T(8,128)S(1)}, u32[]{:S(2)}, u32[]{:S(2)}) collective-permute-start(f32[320,128]{1,0:T(8,128)S(1)} %get-tuple-element.41.refs_0_), channel_id=1, source_target_pairs={{1,0},{2,1},{3,2},{4,3},{5,4},{6,5},{7,6},{8,7},{9,8},{10,9},{11,1... | collective-permute-start | bytes 491528 | tf_op jit(solution)/shard_map/ppermute | solution.py:364
  17.2 4.1 %collective-permute-start.2 = (f32[320,128]{1,0:T(8,128)S(1)}, f32[320,128]{1,0:T(8,128)S(1)}, u32[]{:S(2)}, u32[]{:S(2)}) collective-permute-start(f32[320,128]{1,0:T(8,128)S(1)} %get-tuple-element.41.refs_0_), channel_id=1, source_target_pairs={{0,1},{1,2},{2,3},{3,4},{4,5},{5,6},{6,7},{7,8},{8,9},{9,10},{10,1... | collective-permute-start | bytes 491528 | tf_op jit(solution)/shard_map/ppermute | solution.py:364

commit v6 on v5

--- a/solution.py
+++ b/solution.py
@@ -3,7 +3,6 @@
 from jax import lax
 from jax.experimental import pallas as pl
 from jax.experimental.pallas import tpu as pltpu
-from jax.sharding import Mesh
 from jax.sharding import PartitionSpec as P
 
 F32 = jnp.float32
@@ -59,10 +58,12 @@
             dst[(first + t) * nz : (first + t + 1) * nz, :] = out[:, t * LANES : (t + 1) * LANES]
 
 
-def load_kernel(nz, nx, nat, low, high):
-    for i in range(STEPS):
+def load_kernel(nz, nx, nat, low, high, far_low, far_high):
+    for i in range(2):
         low[i * nz : (i + 1) * nz, :] = nat[pl.ds(i, nz, stride=nx), :]
-        high[i * nz : (i + 1) * nz, :] = nat[pl.ds(nx - STEPS + i, nz, stride=nx), :]
+        high[i * nz : (i + 1) * nz, :] = nat[pl.ds(nx - 2 + i, nz, stride=nx), :]
+    far_low[...] = nat[pl.ds(2, nz, stride=nx), :]
+    far_high[...] = nat[pl.ds(nx - STEPS, nz, stride=nx), :]
 
 
 def place(lane):
@@ -87,7 +88,7 @@
     return inner, outer
 
 
-def pack_edges(rows, first_x, nx, nz, inner, outer, tile, fresh):
+def pack_edges(rows, nx, nz, inner, outer, tile, fresh):
     lane = lane_ids(tile)
     wanted, have = rows
 
@@ -119,21 +120,21 @@
     for x in range(nx):
         b_t[x * nz : (x + 1) * nz, :] = nat[pl.ds(x, nz, stride=nx), :]
     have = lambda x, k: b_t[pl.ds(pl.multiple_of(x * nz + k, 8), 8), :]
-    pack_edges((range(nx), have), 0, nx, nz, inner, outer, 8, True)
+    pack_edges((range(nx), have), nx, nz, inner, outer, 8, True)
     apply_inverse(factors, b_t, u0, nz, nx, nx)
     inner_part(nz, nx, b_t, u0, h_wide, factors, *inside)
 
 
-def pack_kernel(nz, nx, inner_own, outer_own, below, above, inner, outer):
+def pack_kernel(nz, nx, inner_own, outer_own, below, above, inner, outer, to_right, to_left):
     inner[...] = inner_own[...]
     outer[...] = outer_own[...]
-
-    def have(x, k):
-        ref, r = (below, x + STEPS) if x < 0 else (above, x - nx)
-        return ref[pl.ds(pl.multiple_of(r * nz + k, 8), 8), :]
-
-    wanted = [*range(-STEPS, 0), *range(nx, nx + STEPS)]
-    pack_edges((wanted, have), -STEPS, nx, nz, inner, outer, 8, False)
+    halo = Field(nz, (below, (-2, -1)), (above, (nx, nx + 1)))
+    rows = (list(halo.where), lambda x, k: halo.ref_at(x, k))
+    pack_edges(rows, nx, nz, inner, outer, 8, False)
+    pos = place(lane_ids(nz))
+    first, second = inner[:nz, :], pltpu.roll(inner[nz:, :], STEPS, 1)
+    to_right[...] = jnp.where(pos < STEPS, first, second)
+    to_left[...] = jnp.where(pos < 2 * STEPS, first, second)
 
 
 def sideways(mid, step=1):
@@ -170,6 +171,10 @@
     def at(self, x, k, size=8):
         ref, i = self.where[x]
         return ref[i * self.nz + k : i * self.nz + k + size, :]
+
+    def ref_at(self, x, k, size=8):
+        ref, i = self.where[x]
+        return ref[pl.ds(pl.multiple_of(i * self.nz + k, 8), size), :]
 
 
 def advance(factors, xs, u_last, around, g, u, h_ref, width, visit, tile=8):
@@ -247,13 +252,17 @@
     store_sums(sums, sums_out)
 
 
-def outer_kernel(nz, nx, b_t, u0, below, above, h_wide, f0, f1, f2, g1i, u1i, g2i, u2i, start, *outs):
-    u0x, g1x, u1x, g2x, u2x, g3x, sums_out = outs
+def outer_kernel(nz, nx, b_t, u0, below, above, far_below, far_above, edges_in, edges_out, h_wide, f0, f1, f2, *refs):
+    g1i, u1i, g2i, u2i, start, u0x, g1x, u1x, g2x, u2x, g3x, sums_out, edges_in_all, edges_out_all = refs
     factors, every, sums = (f0, f1, f2), range(nx), Sums()
-    half = STEPS * nz
-    out = product(factors, jnp.concatenate([ref[i * nz : (i + 1) * nz, :] for ref in (below, above) for i in range(STEPS)], axis=1))
+    halo = Field(nz, (far_below, (-3,)), (below, (-2, -1)), (above, (nx, nx + 1)), (far_above, (nx + 2,)))
+    out = product(factors, jnp.concatenate([halo.at(x, 0, nz) for x in outer_rows(nx, 0)], axis=1))
     for i in range(2 * STEPS):
         u0x[i * nz : (i + 1) * nz, :] = out[:, i * LANES : (i + 1) * LANES]
+    edges_in_all[...] = edges_in[...]
+    edges_out_all[...] = edges_out[...]
+    rows = ((-STEPS, nx + STEPS - 1), lambda x, k: halo.ref_at(x, k))
+    pack_edges(rows, nx, nz, edges_in_all, edges_out_all, 8, False)
     inner = [inner_rows(nx, level) for level in range(STEPS + 1)]
     outer = [outer_rows(nx, level) for level in range(STEPS + 1)]
     both = lambda level, i, x: Field(nz, (i, inner[level]), (x, outer[level]))
@@ -273,8 +282,9 @@
     used = lane < GROUP * (nx // 2 + 2 * STEPS)
     for t in range(2):
         at = slice(t * nz, (t + 1) * nz)
-        bs[t * nz : (t + 1) * nz, :] = jnp.where((pos < STEPS) & used, left[at, :], inner[at, :])
-        bs[(t + 2) * nz : (t + 3) * nz, :] = jnp.where((pos >= STEPS) & (pos < 2 * STEPS) & used, right[at, :], outer[at, :])
+        beyond = [pltpu.roll(ref[...], LANES - STEPS, 1) if t else ref[...] for ref in (left, right)]
+        bs[t * nz : (t + 1) * nz, :] = jnp.where((pos < STEPS) & used, beyond[0], inner[at, :])
+        bs[(t + 2) * nz : (t + 3) * nz, :] = jnp.where((pos >= STEPS) & (pos < 2 * STEPS) & used, beyond[1], outer[at, :])
     near, far, tiles = Sums(), Sums(), list(range(4))
     field = lambda ref: Field(nz, (ref, tiles))
     count = lambda level, *refs: Visit(level, [field(ref) for ref in refs], tiles, lambda j: near if j < 2 else far)
@@ -321,7 +331,7 @@
     got, b_t, u0, inside_refs, outside_refs = refs[0], refs[1], refs[2], refs[3:8], refs[8:14]
     strips, outs, staged, sems = refs[14:21], refs[21:23], refs[23:25], refs[25]
     g1i, u1i, g2i, u2i, g3i = inside_refs
-    u0x, g1x, u1x, g2x, u2x, g3x = outside_refs
+    _, g1x, u1x, g2x, u2x, g3x = outside_refs
     every = range(nx)
     both = lambda level, i, x: Field(nz, (i, inner_rows(nx, level)), (x, outer_rows(nx, level)))
     fields = [Field(nz, (b_t, every)), Field(nz, (u0, every)), both(1, u1i, u1x), both(2, u2i, u2x)]
@@ -370,15 +380,17 @@
     members = lax.axis_size(gx) * lax.axis_size(gy)
     part = lambda f, *a: (lambda *refs: f(*a, *refs))
     nat = source_heat.reshape(nz * nx, ny)
-    low, high = pl.pallas_call(
+    low, high, far_low, far_high = pl.pallas_call(
         part(load_kernel, nz, nx),
         in_specs=[spec()],
-        out_specs=[spec()] * 2,
-        out_shape=[vmem(STEPS * nz)] * 2,
+        out_specs=[spec()] * 4,
+        out_shape=[vmem(2 * nz)] * 2 + [vmem(nz)] * 2,
         compiler_params=params(4),
     )(nat)
     below = neighbours(high, gx, True)
     above = neighbours(low, gx, False)
+    far_below = neighbours(far_high, gx, True)
+    far_above = neighbours(far_low, gx, False)
     b_t, u0, h_wide, inner_own, outer_own, *rest = pl.pallas_call(
         part(own_kernel, nz, nx),
         in_specs=[spec()] * 3,
@@ -391,23 +403,23 @@
         cost_estimate=cost(36 * nz * nz * nx * ny, 1 << 20),
     )(nat, horiz_coef.reshape(1, nz), column_inverse)
     factors, inside, start = rest[:3], rest[3:8], rest[8]
-    inner, outer = pl.pallas_call(
+    inner, outer, to_right, to_left = pl.pallas_call(
         part(pack_kernel, nz, nx),
         in_specs=[spec()] * 4,
-        out_specs=[spec()] * 2,
-        out_shape=[vmem(2 * nz)] * 2,
+        out_specs=[spec()] * 4,
+        out_shape=[vmem(2 * nz)] * 2 + [vmem(nz)] * 2,
         compiler_params=params(4),
     )(inner_own, outer_own, below, above)
-    from_left = neighbours(inner, gy, True)
-    from_right = neighbours(inner, gy, False)
-    *outside, sums = pl.pallas_call(
+    from_left = neighbours(to_right, gy, True)
+    from_right = neighbours(to_left, gy, False)
+    *outside, sums, inner, outer = pl.pallas_call(
         part(outer_kernel, nz, nx),
-        in_specs=[spec()] * 13,
-        out_specs=[spec()] * 7,
-        out_shape=[vmem(2 * STEPS * nz)] * 6 + [vmem(72)],
+        in_specs=[spec()] * 17,
+        out_specs=[spec()] * 9,
+        out_shape=[vmem(2 * STEPS * nz)] * 6 + [vmem(72)] + [vmem(2 * nz)] * 2,
         compiler_params=params(8),
         cost_estimate=cost(36 * nz * nz * 6 * ny, 1 << 20),
-    )(b_t, u0, below, above, h_wide, *factors, *inside[:4], start)
+    )(b_t, u0, below, above, far_below, far_above, inner, outer, h_wide, *factors, *inside[:4], start)
     *strips, send = pl.pallas_call(
         part(strip_kernel, nz, nx, members),
         in_specs=[spec()] * 9,

time: 52.4 us -> 55 us (1.050)
  starting transfers between devices: 8.64 us -> 14 us
  blocking collectives: 26.1 us -> 23.3 us
    ppermute x4 -> x6, starting transfers between devices: 8.64 us -> 14 us  [neighbours(): lax.ppermute(array, axes, pairs if up else [(b, a) for a, b in pairs])]
    all_to_all x1, blocking collectives: 26.1 us -> 23.3 us  [on_device(): lax.all_to_all(send.reshape(members, 1, LANES), (gx, gy), split_axis=0, c...]
    ppermute x4 -> x6, waiting for transfers between devices: 2.07 us -> 1.85 us  [neighbours(): lax.ppermute(array, axes, pairs if up else [(b, a) for a, b in pairs])]
  transfers between devices with their start and end apart: 4 -> 6, of which waited for: 2 -> 1; matrix products, arithmetic and copies ran while one was open for 0% -> 0% of each run, Pallas kernels for 14% -> 14%
where the time goes in v6:
time: 55 us; the launch traced here: 54.9 us
  blocking collectives  23.3 us (42%)
  starting transfers between devices  14 us (25%)
  Pallas kernels  12.6 us (23%)
  local copies, waits for them, and re-layouts  2.24 us (4%)
  waiting for transfers between devices  1.85 us (3%)
  between operations  0.86 us (2%)
    all_to_all x1, blocking collectives, on_device(): lax.all_to_all(send.reshape(members, 1, LANES), (gx, gy), split_axis=0, c...  23.3 us
    ppermute x6, starting transfers between devices, neighbours(): lax.ppermute(array, axes, pairs if up else [(b, a) for a, b in pairs])  14 us
    pallas_call x1, Pallas kernels, on_device(): pl.pallas_call(part(own_kernel, nz, nx), in_specs=[spec()] * 3, out_specs...  5.23 us
    pallas_call x1, Pallas kernels, on_device(): pl.pallas_call(part(strip_kernel, nz, nx, members), in_specs=[spec()] * 9...  2.48 us
    pallas_call x1, Pallas kernels, on_device(): pl.pallas_call(part(combine_kernel, nz, nx), in_specs=[spec()] * 21, out_...  2.41 us
    unnamed x8, local copies, waits for them, and re-layouts  2.24 us
    pallas_call x1, Pallas kernels, on_device(): pl.pallas_call(part(outer_kernel, nz, nx), in_specs=[spec()] * 17, out_sp...  2.1 us
    ppermute x6, waiting for transfers between devices, neighbours(): lax.ppermute(array, axes, pairs if up else [(b, a) for a, b in pairs])  1.85 us
  transfers between devices with their start and end apart: 6, of which 1 were waited for; matrix products, arithmetic and copies ran while one was open for 0% of the time, Pallas kernels for 14%

profile of v6, /device:TPU:1, one launch (start us, length us, event | category | flops | bytes accessed | tf_op | source)
XLA Modules:
  0.0 54.9 jit_solution(13484047359898436650)
XLA Ops:
  0.6 0.0 copy-start.3
  0.6 0.0 copy-start
  0.6 1.3 %copy-done = f32[160,16,128]{2,1,0:T(8,128)S(1)} copy-done((f32[160,16,128]{2,1,0:T(8,128)S(1)}, f32[160,16,128]{2,1,0:T(8,128)}, u32[]{:S(2)}) %copy-start) | copy-done | bytes 1310744
  2.0 0.0 copy-start.1
  2.0 0.2 shard_map.51
  2.2 2.1 %collective-permute-start.2 = (f32[160,128]{1,0:T(8,128)S(1)}, f32[160,128]{1,0:T(8,128)S(1)}, u32[]{:S(2)}, u32[]{:S(2)}) collective-permute-start(f32[160,128]{1,0:T(8,128)S(1)} %get-tuple-element.47), channel_id=1, source_target_pairs={{0,16},{16,32},{32,48},{48,64},{64,80},{80,96},{96,112},{112,128},... | collective-permute-start | bytes 245768 | tf_op jit(solution)/shard_map/ppermute | solution.py:374
  4.3 3.8 %collective-permute-start.3 = (f32[160,128]{1,0:T(8,128)S(1)}, f32[160,128]{1,0:T(8,128)S(1)}, u32[]{:S(2)}, u32[]{:S(2)}) collective-permute-start(f32[160,128]{1,0:T(8,128)S(1)} %get-tuple-element.48), channel_id=1, source_target_pairs={{16,0},{32,16},{48,32},{64,48},{80,64},{96,80},{112,96},{128,112},... | collective-permute-start | bytes 245768 | tf_op jit(solution)/shard_map/ppermute | solution.py:374
  8.1 0.0 collective-permute-start
  8.1 4.8 %collective-permute-start.1 = (f32[320,128]{1,0:T(8,128)S(1)}, f32[320,128]{1,0:T(8,128)S(1)}, u32[]{:S(2)}, u32[]{:S(2)}) collective-permute-start(f32[320,128]{1,0:T(8,128)S(1)} %get-tuple-element.46), channel_id=1, source_target_pairs={{16,0},{32,16},{48,32},{64,48},{80,64},{96,80},{112,96},{128,112},... | collective-permute-start | bytes 491528 | tf_op jit(solution)/shard_map/ppermute | solution.py:374
  12.9 0.0 copy-done.3
  12.9 0.0 copy-done.1
  12.9 0.0 copy-start.2
  12.9 0.9 %copy-done.2 = f32[160,160]{1,0:T(8,128)S(1)} copy-done((f32[160,160]{1,0:T(8,128)S(1)}, f32[160,160]{1,0:T(8,128)}, u32[]{:S(2)}) %copy-start.2) | copy-done | bytes 102424
  13.8 5.2 %shard_map.50 = (f32[2560,128]{1,0:T(8,128)S(1)}, f32[2560,128]{1,0:T(8,128)S(1)}, f32[160,128]{1,0:T(8,128)S(1)}, f32[320,128]{1,0:T(8,128)S(1)}, f32[320,128]{...) custom-call(f32[2560,128]{1,0:T(8,128)S(1)} %bitcast.9, ...), custom_call_target="tpu_custom_call" | custom-call | flops 1887436800 | bytes 1048576 | tf_op jit(solution)/shard_map/pallas_call | solution.py:394
  19.0 0.0 collective-permute-done.refs_2_
  19.0 0.0 collective-permute-done.1.refs_3_
  19.0 0.2 shard_map.52
  19.2 3.1 %collective-permute-start.4 = (f32[160,128]{1,0:T(8,128)S(1)}, f32[160,128]{1,0:T(8,128)S(1)}, u32[]{:S(2)}, u32[]{:S(2)}) collective-permute-start(f32[160,128]{1,0:T(8,128)S(1)} %get-tuple-element.64), channel_id=1, source_target_pairs={{0,1},{1,2},{2,3},{3,4},{4,5},{5,6},{6,7},{7,8},{8,9},{9,10},{10,1... | collective-permute-start | bytes 245768 | tf_op jit(solution)/shard_map/ppermute | solution.py:374
  22.3 0.2 collective-permute-start.5
  22.5 0.0 collective-permute-done.2.refs_4_
  22.5 0.0 collective-permute-done.3.refs_5_
  22.5 2.1 %shard_map.53 = (f32[960,128]{1,0:T(8,128)S(1)}, f32[960,128]{1,0:T(8,128)S(1)}, f32[960,128]{1,0:T(8,128)S(1)}, f32[960,128]{1,0:T(8,128)S(1)}, f32[960,128]{1,...) custom-call(f32[2560,128]{1,0:T(8,128)S(1)} %get-tuple-element.43.re, ...), custom_call_target="tpu_custom_call" | custom-call | flops 707788800 | bytes 1048576 | tf_op jit(solution)/shard_map/pallas_call | solution.py:415
  24.6 0.0 collective-permute-done.4.refs_2_
  24.7 1.8 %collective-permute-done.5.refs_3_ = f32[160,128]{1,0:T(8,128)S(1)} collective-permute-done((f32[160,128]{1,0:T(8,128)S(1)}, f32[160,128]{1,0:T(8,128)S(1)}, u32[]{:S(2)}, u32[]{:S(2)}) %collective-permute-start.5) | collective-permute-done | bytes 81952 | tf_op jit(solution)/shard_map/ppermute | solution.py:374
  26.5 2.5 %shard_map.54 = (f32[640,128]{1,0:T(8,128)S(1)}, f32[640,128]{1,0:T(8,128)S(1)}, f32[640,128]{1,0:T(8,128)S(1)}, f32[640,128]{1,0:T(8,128)S(1)}, f32[640,128]{1,...) custom-call(f32[320,128]{1,0:T(8,128)S(1)} %get-tuple-element.62.refs_0_, ...), custom_call_target="tpu_custom_call" | custom-call | tf_op jit(solution)/shard_map/pallas_call | solution.py:423
  29.0 23.3 %all_to_all.5 = f32[256,1,128]{2,1,0:T(1,128)S(1)} all-to-all(f32[256,1,128]{2,1,0:T(1,128)S(1)} %bitcast.11), channel_id=1, replica_groups=mesh['gx'=16,'gy'=16] {'gx','gy'}, dimensions={0} | all-to-all | bytes 262144 | tf_op jit(solution)/shard_map/all_to_all | solution.py:430
  52.3 2.4 %shard_map.55 = (f32[2560,128]{1,0:T(8,128)}, f32[2560,128]{1,0:T(8,128)}) custom-call(f32[256,128]{1,0:T(8,128)S(1)} %bitcast.10, f32[2560,128]{1,0:T(8,128)S(1)} %get-tuple-element.43.refs_0_.refs_1_, f32[2560,128]{1,0:T(8,128)S(1)} %get-tuple-element.44.refs_1_.refs_2_, f32[2240,128]{1,0:T(8,128)S(1)} %get-tuple-element.57.refs_12_.refs_3_, ...), custom_call_target="tpu_custom_call" | custom-call | tf_op jit(solution)/shard_map/pallas_call | solution.py:431
Async XLA Ops:
  0.6 12.2 %copy-start.3 = (f32[160]{0:T(256)S(1)}, f32[160]{0:T(256)}, u32[]{:S(2)}) copy-start(f32[160]{0:T(256)} %param.5) | copy-start | bytes 1924
  0.6 1.3 %copy-start = (f32[160,16,128]{2,1,0:T(8,128)S(1)}, f32[160,16,128]{2,1,0:T(8,128)}, u32[]{:S(2)}) copy-start(f32[160,16,128]{2,1,0:T(8,128)} %param.4) | copy-start | bytes 3932164
  2.0 10.9 %copy-start.1 = (f32[160,16,128]{2,1,0:T(8,128)S(1)}, f32[160,16,128]{2,1,0:T(8,128)}, u32[]{:S(2)}) copy-start(f32[160,16,128]{2,1,0:T(8,128)} %param.4) | copy-start | bytes 3932164
  2.2 20.4 %collective-permute-start.2 = (f32[160,128]{1,0:T(8,128)S(1)}, f32[160,128]{1,0:T(8,128)S(1)}, u32[]{:S(2)}, u32[]{:S(2)}) collective-permute-start(f32[160,128]{1,0:T(8,128)S(1)} %get-tuple-element.47), channel_id=1, source_target_pairs={{0,16},{16,32},{32,48},{48,64},{64,80},{80,96},{96,112},{112,128},... | collective-permute-start | bytes 245768 | tf_op jit(solution)/shard_map/ppermute | solution.py:374
  4.3 18.3 %collective-permute-start.3 = (f32[160,128]{1,0:T(8,128)S(1)}, f32[160,128]{1,0:T(8,128)S(1)}, u32[]{:S(2)}, u32[]{:S(2)}) collective-permute-start(f32[160,128]{1,0:T(8,128)S(1)} %get-tuple-element.48), channel_id=1, source_target_pairs={{16,0},{32,16},{48,32},{64,48},{80,64},{96,80},{112,96},{128,112},... | collective-permute-start | bytes 245768 | tf_op jit(solution)/shard_map/ppermute | solution.py:374
  8.1 10.9 %collective-permute-start = (f32[320,128]{1,0:T(8,128)S(1)}, f32[320,128]{1,0:T(8,128)S(1)}, u32[]{:S(2)}, u32[]{:S(2)}) collective-permute-start(f32[320,128]{1,0:T(8,128)S(1)} %get-tuple-element.45), channel_id=1, source_target_pairs={{0,16},{16,32},{32,48},{48,64},{64,80},{80,96},{96,112},{112,128},... | collective-permute-start | bytes 491528 | tf_op jit(solution)/shard_map/ppermute | solution.py:374
  8.1 10.9 %collective-permute-start.1 = (f32[320,128]{1,0:T(8,128)S(1)}, f32[320,128]{1,0:T(8,128)S(1)}, u32[]{:S(2)}, u32[]{:S(2)}) collective-permute-start(f32[320,128]{1,0:T(8,128)S(1)} %get-tuple-element.46), channel_id=1, source_target_pairs={{16,0},{32,16},{48,32},{64,48},{80,64},{96,80},{112,96},{128,112},... | collective-permute-start | bytes 491528 | tf_op jit(solution)/shard_map/ppermute | solution.py:374
  12.9 0.9 %copy-start.2 = (f32[160,160]{1,0:T(8,128)S(1)}, f32[160,160]{1,0:T(8,128)}, u32[]{:S(2)}) copy-start(f32[160,160]{1,0:T(8,128)} %refs_2_.1) | copy-start | bytes 307204
  19.2 5.4 %collective-permute-start.4 = (f32[160,128]{1,0:T(8,128)S(1)}, f32[160,128]{1,0:T(8,128)S(1)}, u32[]{:S(2)}, u32[]{:S(2)}) collective-permute-start(f32[160,128]{1,0:T(8,128)S(1)} %get-tuple-element.64), channel_id=1, source_target_pairs={{0,1},{1,2},{2,3},{3,4},{4,5},{5,6},{6,7},{7,8},{8,9},{9,10},{10,1... | collective-permute-start | bytes 245768 | tf_op jit(solution)/shard_map/ppermute | solution.py:374
  22.3 4.2 %collective-permute-start.5 = (f32[160,128]{1,0:T(8,128)S(1)}, f32[160,128]{1,0:T(8,128)S(1)}, u32[]{:S(2)}, u32[]{:S(2)}) collective-permute-start(f32[160,128]{1,0:T(8,128)S(1)} %get-tuple-element.65), channel_id=1, source_target_pairs={{1,0},{2,1},{3,2},{4,3},{5,4},{6,5},{7,6},{8,7},{9,8},{10,9},{11,1... | collective-permute-start | bytes 245768 | tf_op jit(solution)/shard_map/ppermute | solution.py:374

commit v7 on v5

--- a/solution.py
+++ b/solution.py
@@ -124,7 +124,7 @@
     inner_part(nz, nx, b_t, u0, h_wide, factors, *inside)
 
 
-def pack_kernel(nz, nx, inner_own, outer_own, below, above, inner, outer):
+def pack_kernel(nz, nx, inner_own, outer_own, below, above, inner, outer, to_right, to_left):
     inner[...] = inner_own[...]
     outer[...] = outer_own[...]
 
@@ -134,6 +134,10 @@
 
     wanted = [*range(-STEPS, 0), *range(nx, nx + STEPS)]
     pack_edges((wanted, have), -STEPS, nx, nz, inner, outer, 8, False)
+    pos = place(lane_ids(nz))
+    first, second = inner[:nz, :], pltpu.roll(inner[nz:, :], STEPS, 1)
+    to_right[...] = jnp.where(pos < STEPS, first, second)
+    to_left[...] = jnp.where(pos < 2 * STEPS, first, second)
 
 
 def sideways(mid, step=1):
@@ -273,8 +277,9 @@
     used = lane < GROUP * (nx // 2 + 2 * STEPS)
     for t in range(2):
         at = slice(t * nz, (t + 1) * nz)
-        bs[t * nz : (t + 1) * nz, :] = jnp.where((pos < STEPS) & used, left[at, :], inner[at, :])
-        bs[(t + 2) * nz : (t + 3) * nz, :] = jnp.where((pos >= STEPS) & (pos < 2 * STEPS) & used, right[at, :], outer[at, :])
+        beyond = [pltpu.roll(ref[...], LANES - STEPS, 1) if t else ref[...] for ref in (left, right)]
+        bs[t * nz : (t + 1) * nz, :] = jnp.where((pos < STEPS) & used, beyond[0], inner[at, :])
+        bs[(t + 2) * nz : (t + 3) * nz, :] = jnp.where((pos >= STEPS) & (pos < 2 * STEPS) & used, beyond[1], outer[at, :])
     near, far, tiles = Sums(), Sums(), list(range(4))
     field = lambda ref: Field(nz, (ref, tiles))
     count = lambda level, *refs: Visit(level, [field(ref) for ref in refs], tiles, lambda j: near if j < 2 else far)
@@ -391,15 +396,15 @@
         cost_estimate=cost(36 * nz * nz * nx * ny, 1 << 20),
     )(nat, horiz_coef.reshape(1, nz), column_inverse)
     factors, inside, start = rest[:3], rest[3:8], rest[8]
-    inner, outer = pl.pallas_call(
+    inner, outer, to_right, to_left = pl.pallas_call(
         part(pack_kernel, nz, nx),
         in_specs=[spec()] * 4,
-        out_specs=[spec()] * 2,
-        out_shape=[vmem(2 * nz)] * 2,
+        out_specs=[spec()] * 4,
+        out_shape=[vmem(2 * nz)] * 2 + [vmem(nz)] * 2,
         compiler_params=params(4),
     )(inner_own, outer_own, below, above)
-    from_left = neighbours(inner, gy, True)
-    from_right = neighbours(inner, gy, False)
+    from_left = neighbours(to_right, gy, True)
+    from_right = neighbours(to_left, gy, False)
     *outside, sums = pl.pallas_call(
         part(outer_kernel, nz, nx),
         in_specs=[spec()] * 13,

time: 52.4 us -> 51.9 us (level)
  transfers between devices with their start and end apart: 4 -> 4, of which waited for: 2 -> 1; matrix products, arithmetic and copies ran while one was open for 0% -> 0% of each run, Pallas kernels for 14% -> 14%
where the time goes in v7:
time: 51.9 us; the launch traced here: 51.7 us
  blocking collectives  26 us (50%)
  Pallas kernels  12.6 us (24%)
  starting transfers between devices  8.66 us (17%)
  local copies, waits for them, and re-layouts  2.24 us (4%)
  waiting for transfers between devices  1.57 us (3%)
  between operations  0.7 us (1%)
    all_to_all x1, blocking collectives, on_device(): lax.all_to_all(send.reshape(members, 1, LANES), (gx, gy), split_axis=0, c...  26 us
    ppermute x4, starting transfers between devices, neighbours(): lax.ppermute(array, axes, pairs if up else [(b, a) for a, b in pairs])  8.66 us
    pallas_call x1, Pallas kernels, on_device(): pl.pallas_call(part(own_kernel, nz, nx), in_specs=[spec()] * 3, out_specs...  5.23 us
    pallas_call x1, Pallas kernels, on_device(): pl.pallas_call(part(strip_kernel, nz, nx, members), in_specs=[spec()] * 9...  2.47 us
    pallas_call x1, Pallas kernels, on_device(): pl.pallas_call(part(combine_kernel, nz, nx), in_specs=[spec()] * 21, out_...  2.41 us
    unnamed x8, local copies, waits for them, and re-layouts  2.24 us
    pallas_call x1, Pallas kernels, on_device(): pl.pallas_call(part(outer_kernel, nz, nx), in_specs=[spec()] * 13, out_sp...  2.08 us
    ppermute x4, waiting for transfers between devices, neighbours(): lax.ppermute(array, axes, pairs if up else [(b, a) for a, b in pairs])  1.57 us
  transfers between devices with their start and end apart: 4, of which 1 were waited for; matrix products, arithmetic and copies ran while one was open for 0% of the time, Pallas kernels for 14%

profile of v7, /device:TPU:1, one launch (start us, length us, event | category | flops | bytes accessed | tf_op | source)
XLA Modules:
  0.0 51.7 jit_solution(16518710326900449688)
XLA Ops:
  0.6 0.0 copy-start.3
  0.6 0.0 copy-start
  0.6 1.3 %copy-done = f32[160,16,128]{2,1,0:T(8,128)S(1)} copy-done((f32[160,16,128]{2,1,0:T(8,128)S(1)}, f32[160,16,128]{2,1,0:T(8,128)}, u32[]{:S(2)}) %copy-start) | copy-done | bytes 1310744
  2.0 0.0 copy-start.1
  2.0 0.2 shard_map.51
  2.2 2.1 %collective-permute-start = (f32[480,128]{1,0:T(8,128)S(1)}, f32[480,128]{1,0:T(8,128)S(1)}, u32[]{:S(2)}, u32[]{:S(2)}) collective-permute-start(f32[480,128]{1,0:T(8,128)S(1)} %get-tuple-element.41), channel_id=1, source_target_pairs={{0,16},{16,32},{32,48},{48,64},{64,80},{80,96},{96,112},{112,128},... | collective-permute-start | bytes 737288 | tf_op jit(solution)/shard_map/ppermute | solution.py:369
  4.3 3.8 %collective-permute-start.1 = (f32[480,128]{1,0:T(8,128)S(1)}, f32[480,128]{1,0:T(8,128)S(1)}, u32[]{:S(2)}, u32[]{:S(2)}) collective-permute-start(f32[480,128]{1,0:T(8,128)S(1)} %get-tuple-element.42), channel_id=1, source_target_pairs={{16,0},{32,16},{48,32},{64,48},{80,64},{96,80},{112,96},{128,112},... | collective-permute-start | bytes 737288 | tf_op jit(solution)/shard_map/ppermute | solution.py:369
  8.1 0.0 copy-done.3
  8.1 0.0 copy-done.1
  8.1 0.0 copy-start.2
  8.1 0.9 %copy-done.2 = f32[160,160]{1,0:T(8,128)S(1)} copy-done((f32[160,160]{1,0:T(8,128)S(1)}, f32[160,160]{1,0:T(8,128)}, u32[]{:S(2)}) %copy-start.2) | copy-done | bytes 102424
  9.0 5.2 %shard_map.50 = (f32[2560,128]{1,0:T(8,128)S(1)}, f32[2560,128]{1,0:T(8,128)S(1)}, f32[160,128]{1,0:T(8,128)S(1)}, f32[320,128]{1,0:T(8,128)S(1)}, f32[320,128]{...) custom-call(f32[2560,128]{1,0:T(8,128)S(1)} %bitcast.9, ...), custom_call_target="tpu_custom_call" | custom-call | flops 1887436800 | bytes 1048576 | tf_op jit(solution)/shard_map/pallas_call | solution.py:387
  14.2 0.0 collective-permute-done.refs_2_
  14.2 0.0 collective-permute-done.1.refs_3_
  14.2 0.2 shard_map.52
  14.5 2.5 %collective-permute-start.2 = (f32[160,128]{1,0:T(8,128)S(1)}, f32[160,128]{1,0:T(8,128)S(1)}, u32[]{:S(2)}, u32[]{:S(2)}) collective-permute-start(f32[160,128]{1,0:T(8,128)S(1)} %get-tuple-element.45), channel_id=1, source_target_pairs={{0,1},{1,2},{2,3},{3,4},{4,5},{5,6},{6,7},{7,8},{8,9},{9,10},{10,1... | collective-permute-start | bytes 245768 | tf_op jit(solution)/shard_map/ppermute | solution.py:369
  17.0 0.2 collective-permute-start.3
  17.2 2.1 %shard_map.53 = (f32[960,128]{1,0:T(8,128)S(1)}, f32[960,128]{1,0:T(8,128)S(1)}, f32[960,128]{1,0:T(8,128)S(1)}, f32[960,128]{1,0:T(8,128)S(1)}, f32[960,128]{1,...) custom-call(f32[2560,128]{1,0:T(8,128)S(1)} %get-tuple-element.48.refs_0_.refs_1_, ...), custom_call_target="tpu_custom_call" | custom-call | flops 707788800 | bytes 1048576 | tf_op jit(solution)/shard_map/pallas_call | solution.py:408
  19.3 0.0 collective-permute-done.2.refs_2_
  19.3 1.6 %collective-permute-done.3.refs_3_ = f32[160,128]{1,0:T(8,128)S(1)} collective-permute-done((f32[160,128]{1,0:T(8,128)S(1)}, f32[160,128]{1,0:T(8,128)S(1)}, u32[]{:S(2)}, u32[]{:S(2)}) %collective-permute-start.3) | collective-permute-done | bytes 81952 | tf_op jit(solution)/shard_map/ppermute | solution.py:369
  20.9 2.5 %shard_map.54 = (f32[640,128]{1,0:T(8,128)S(1)}, f32[640,128]{1,0:T(8,128)S(1)}, f32[640,128]{1,0:T(8,128)S(1)}, f32[640,128]{1,0:T(8,128)S(1)}, f32[640,128]{1,...) custom-call(f32[320,128]{1,0:T(8,128)S(1)} %get-tuple-element.43.refs_0_, ...), custom_call_target="tpu_custom_call" | custom-call | tf_op jit(solution)/shard_map/pallas_call | solution.py:416
  23.4 26.0 %all_to_all.5 = f32[256,1,128]{2,1,0:T(1,128)S(1)} all-to-all(f32[256,1,128]{2,1,0:T(1,128)S(1)} %bitcast.11), channel_id=1, replica_groups=mesh['gx'=16,'gy'=16] {'gx','gy'}, dimensions={0} | all-to-all | bytes 262144 | tf_op jit(solution)/shard_map/all_to_all | solution.py:423
  49.3 2.4 %shard_map.55 = (f32[2560,128]{1,0:T(8,128)}, f32[2560,128]{1,0:T(8,128)}) custom-call(f32[256,128]{1,0:T(8,128)S(1)} %bitcast.10, f32[2560,128]{1,0:T(8,128)S(1)} %get-tuple-element.48.refs_0_.refs_1_, f32[2560,128]{1,0:T(8,128)S(1)} %get-tuple-element.49.refs_1_.refs_2_, f32[2240,128]{1,0:T(8,128)S(1)} %get-tuple-element.53.refs_8_.refs_3_, ...), custom_call_target="tpu_custom_call" | custom-call | tf_op jit(solution)/shard_map/pallas_call | solution.py:424
Async XLA Ops:
  0.6 7.4 %copy-start.3 = (f32[160]{0:T(256)S(1)}, f32[160]{0:T(256)}, u32[]{:S(2)}) copy-start(f32[160]{0:T(256)} %param.5) | copy-start | bytes 1924
  0.6 1.3 %copy-start = (f32[160,16,128]{2,1,0:T(8,128)S(1)}, f32[160,16,128]{2,1,0:T(8,128)}, u32[]{:S(2)}) copy-start(f32[160,16,128]{2,1,0:T(8,128)} %param.4) | copy-start | bytes 3932164
  2.0 6.1 %copy-start.1 = (f32[160,16,128]{2,1,0:T(8,128)S(1)}, f32[160,16,128]{2,1,0:T(8,128)}, u32[]{:S(2)}) copy-start(f32[160,16,128]{2,1,0:T(8,128)} %param.4) | copy-start | bytes 3932164
  2.2 12.1 %collective-permute-start = (f32[480,128]{1,0:T(8,128)S(1)}, f32[480,128]{1,0:T(8,128)S(1)}, u32[]{:S(2)}, u32[]{:S(2)}) collective-permute-start(f32[480,128]{1,0:T(8,128)S(1)} %get-tuple-element.41), channel_id=1, source_target_pairs={{0,16},{16,32},{32,48},{48,64},{64,80},{80,96},{96,112},{112,128},... | collective-permute-start | bytes 737288 | tf_op jit(solution)/shard_map/ppermute | solution.py:369
  4.3 10.0 %collective-permute-start.1 = (f32[480,128]{1,0:T(8,128)S(1)}, f32[480,128]{1,0:T(8,128)S(1)}, u32[]{:S(2)}, u32[]{:S(2)}) collective-permute-start(f32[480,128]{1,0:T(8,128)S(1)} %get-tuple-element.42), channel_id=1, source_target_pairs={{16,0},{32,16},{48,32},{64,48},{80,64},{96,80},{112,96},{128,112},... | collective-permute-start | bytes 737288 | tf_op jit(solution)/shard_map/ppermute | solution.py:369
  8.1 0.9 %copy-start.2 = (f32[160,160]{1,0:T(8,128)S(1)}, f32[160,160]{1,0:T(8,128)}, u32[]{:S(2)}) copy-start(f32[160,160]{1,0:T(8,128)} %refs_2_.1) | copy-start | bytes 307204
  14.5 4.8 %collective-permute-start.2 = (f32[160,128]{1,0:T(8,128)S(1)}, f32[160,128]{1,0:T(8,128)S(1)}, u32[]{:S(2)}, u32[]{:S(2)}) collective-permute-start(f32[160,128]{1,0:T(8,128)S(1)} %get-tuple-element.45), channel_id=1, source_target_pairs={{0,1},{1,2},{2,3},{3,4},{4,5},{5,6},{6,7},{7,8},{8,9},{9,10},{10,1... | collective-permute-start | bytes 245768 | tf_op jit(solution)/shard_map/ppermute | solution.py:369
  17.0 3.9 %collective-permute-start.3 = (f32[160,128]{1,0:T(8,128)S(1)}, f32[160,128]{1,0:T(8,128)S(1)}, u32[]{:S(2)}, u32[]{:S(2)}) collective-permute-start(f32[160,128]{1,0:T(8,128)S(1)} %get-tuple-element.46), channel_id=1, source_target_pairs={{1,0},{2,1},{3,2},{4,3},{5,4},{6,5},{7,6},{8,7},{9,8},{10,9},{11,1... | collective-permute-start | bytes 245768 | tf_op jit(solution)/shard_map/ppermute | solution.py:369
